TPU v7x, 256 devices: a whole 4x4x8 slice. The times are simulated.
256 devices in a mesh: seq: 128 (over z, x_hi, y, core), mp: 2 (over x_lo).
Axes of the slice: x: 4 (x_hi: 2, x_lo: 2; x = x_hi * 2 + x_lo), y: 4, z: 8, core: 2. Of those that a mesh axis runs over, the one named last changes fastest.
Arguments:
- stream: bfloat16 [16384, 8192], P('seq', 'mp'), may hold values from -17 to 17
- norm_gain: float32 [8192], P('mp'), may hold values from 0.5 to 1.5
- short_outer: bfloat16 [16384, 8192], P('seq', 'mp'), may hold values from -4 to 4
- short_inner: bfloat16 [16384, 8192], P('seq', 'mp'), may hold values from -4 to 4
- short_filter: bfloat16 [128, 8192], P(None, 'mp'), may hold values from -0.5 to 0.5
- long_outer: bfloat16 [16384, 8192], P('seq', 'mp'), may hold values from -4 to 4
- long_inner: bfloat16 [16384, 8192], P('seq', 'mp'), may hold values from -4 to 4
- long_decay: float32 [8192], P('mp'), may hold values from 1e-06 to 0.03
- query_heads: bfloat16 [16384, 8192], P('seq', 'mp'), may hold values from -6 to 6
- key_heads: bfloat16 [16384, 8192], P('seq', 'mp'), may hold values from -6 to 6
Outputs:
- long_mixed: bfloat16 [16384, 8192], P('seq', 'mp')
- attended: bfloat16 [16384, 8192], P('seq', 'mp')
All inputs are finite; a program needn't handle non-finite values.
Results may differ from a plain program's by a relative error of at most 0.013.
Values may be sent and summed in bfloat16 or wider, within the bound.
No kernel may reach another device: no remote copies, remote signals or barrier semaphores. Data moves between devices by JAX's collectives and lax.ppermute only.
A program may use at most 64 MiB of HBM per device.

v0:
```python
import jax
import jax.numpy as jnp
from jax import lax
from jax.sharding import Mesh
from jax.sharding import PartitionSpec as P

D = 8192
HEAD_DIM = 128
SEQ = ("seq_0", "seq_1", "seq_2", "seq_3")


def sent_to_all(array, axis):
    copies = jnp.broadcast_to(array, (lax.axis_size(axis), *array.shape))
    return lax.all_to_all(copies, axis, split_axis=0, concat_axis=0, tiled=True)


def taken_together(array, axis):
    everything = sent_to_all(array, axis)
    return jnp.sum(everything, axis=0)


def shifted(block, axis, distance):
    devices = range(lax.axis_size(axis))
    route = [(i - distance, i) for i in devices if i - distance in devices]
    return lax.ppermute(block, axis, route)


def nothing_yet(array, identity):
    return jax.tree.map(
        lambda part, zero: jnp.zeros_like(part) + jnp.asarray(zero, part.dtype), array, identity
    )


def entering(array, axes, combine, identity):
    before = start = nothing_yet(array, identity)
    so_far = array
    for axis in reversed(axes):
        size, place = (lax.axis_size(axis), lax.axis_index(axis))
        pieces = jax.tree.map(lambda part: lax.all_gather(part, axis), so_far)
        inside, so_far = (start, start)
        for k in range(size):
            passed = k < place
            so_far = combine(so_far, jax.tree.map(lambda part: part[k], pieces))
            inside = jax.tree.map(lambda new, old: jnp.where(passed, new, old), so_far, inside)
        before = combine(inside, before)
    return before


def pair_combine(first_pair, second_pair):
    return (first_pair[0] * second_pair[0], second_pair[0] * first_pair[1] + second_pair[1])


def on_device(
    stream,
    norm_gain,
    short_outer,
    short_inner,
    short_filter,
    long_outer,
    long_inner,
    long_decay,
    query_heads,
    key_heads,
):
    rows_here = stream.shape[0]
    width_here = stream.shape[1]
    x_float = stream.astype(jnp.float32)
    totals = taken_together(jnp.sum(x_float * x_float, axis=1), "mp")
    normed = x_float * norm_gain / jnp.sqrt(totals[:, None] / D + 0.5)
    short_in = (short_inner.astype(jnp.float32) * normed).astype(jnp.bfloat16)
    filter_len = short_filter.shape[0]
    tail_rows = shifted(short_in[rows_here - (filter_len - 1) :], SEQ, 1)
    extended = jnp.concatenate([tail_rows, short_in], axis=0).astype(jnp.float32)
    kernel = short_filter.astype(jnp.float32)[::-1][:, None, :]
    short_conv = lax.conv_general_dilated(
        extended[None],
        kernel,
        (1,),
        [(0, 0)],
        dimension_numbers=("NWC", "WIO", "NWC"),
        feature_group_count=width_here,
        precision=lax.Precision.HIGHEST,
    )[0]
    long_in = (
        long_inner.astype(jnp.float32) * short_outer.astype(jnp.float32) * short_conv
    ).astype(jnp.bfloat16)
    rates = jnp.exp(-long_decay)
    scales = jnp.sqrt(-jnp.expm1(-2.0 * long_decay))
    factors = jnp.broadcast_to(rates, long_in.shape)
    powers, states = lax.associative_scan(
        pair_combine, (factors, long_in.astype(jnp.float32)), axis=0
    )
    identity = (jnp.ones((width_here,), jnp.float32), jnp.zeros((width_here,), jnp.float32))
    carried = entering((powers[-1], states[-1]), SEQ, pair_combine, identity)
    long_conv = (states + powers * carried[1]) * scales
    long_mixed = (long_outer.astype(jnp.float32) * long_conv).astype(jnp.bfloat16)
    stacked = jnp.stack([key_heads, long_mixed])
    before = shifted(stacked, SEQ, 1)
    heads_here = width_here // HEAD_DIM
    keys = jnp.concatenate([before[0], key_heads], axis=0).reshape(
        2 * rows_here, heads_here, HEAD_DIM
    )
    values = jnp.concatenate([before[1], long_mixed], axis=0).reshape(
        2 * rows_here, heads_here, HEAD_DIM
    )
    query = query_heads.reshape(rows_here, heads_here, HEAD_DIM)
    scores = jnp.einsum(
        "thd,shd->hts", query, keys, preferred_element_type=jnp.float32
    ) * HEAD_DIM ** (-0.5)
    row_pos = jnp.arange(rows_here, dtype=jnp.int32)[:, None]
    col_pos = jnp.arange(2 * rows_here, dtype=jnp.int32)[None, :]
    valid = (col_pos <= row_pos + rows_here) & ((col_pos >= rows_here) | (lax.axis_index(SEQ) > 0))
    scores = jnp.where(valid[None], scores, -1e30)
    weights = jax.nn.softmax(scores, axis=-1).astype(jnp.bfloat16)
    result = jnp.einsum("hts,shd->thd", weights, values, preferred_element_type=jnp.float32)
    attended = result.reshape(rows_here, width_here).astype(jnp.bfloat16)
    return (long_mixed, attended)


def solution(mesh):
    finer = Mesh(
        mesh.devices.reshape(8, 2, 4, 2, mesh.shape["mp"]),
        ("seq_0", "seq_1", "seq_2", "seq_3", "mp"),
    )
    placed = (
        P(SEQ, "mp"),
        P("mp"),
        P(SEQ, "mp"),
        P(SEQ, "mp"),
        P(None, "mp"),
        P(SEQ, "mp"),
        P(SEQ, "mp"),
        P("mp"),
        P(SEQ, "mp"),
        P(SEQ, "mp"),
    )
    return jax.shard_map(
        on_device,
        mesh=finer,
        in_specs=placed,
        out_specs=(P(SEQ, "mp"), P(SEQ, "mp")),
        check_vma=False,
    )
```

profile of v0, /device:TPU:128, one launch (start us, length us, event | category | flops | bytes accessed | tf_op | source)
XLA Modules:
  0.0 308.0 jit_solution(8889508349496317646)
XLA Ops:
  0.6 1.6 fusion.7
  2.3 6.3 %all_to_all.6 = f32[2,1,128]{2,1,0:T(1,128)S(1)} all-to-all(f32[2,1,128]{2,1,0:T(1,128)S(1)} %broadcast_in_dim.22), channel_id=1, replica_groups=mesh['seq_0'=8,'seq_1'=2,'seq_2'=4,'seq_3'=2,'mp'=2] {'mp'}, dimensions={0} | all-to-all | bytes 2048 | tf_op jit(solution)/shard_map/all_to_all | solution.py:14
  8.6 2.1 fusion.6
  10.7 1.2 slice.417
  11.9 2.0 collective-permute-start
  14.0 10.6 %rev.3 = f32[128,4096]{1,0:T(8,128)} reverse(bf16[128,4096]{1,0:T(8,128)(2,1)S(1)} %copy-done.11), dimensions={0} | reverse | bytes 3145728 | tf_op jit(solution)/shard_map/rev | solution.py:74
  25.4 1.3 pad.104
  26.7 7.5 %collective-permute-done = bf16[127,4096]{1,0:T(8,128)(2,1)} collective-permute-done((bf16[127,4096]{1,0:T(8,128)(2,1)}, bf16[127,4096]{1,0:T(8,128)(2,1)}, u32[]{:S(2)}, u32[]{:S(2)}) %collective-permute-start) | collective-permute-done | bytes 1040416 | tf_op jit(solution)/shard_map/ppermute | solution.py:25
  34.2 1.5 maximum_bitcast_fusion
  35.8 23.9 %fusion.1 = f32[1,128,4096]{2,0,1:T(1,128)S(1)} fusion(bf16[1,255,4096]{2,1,0:T(8,128)(2,1)S(1)} %maximum_bitcast_fusion, f32[128,1,4096]{2,0,1:T(8,128)S(1)} %bitcast.306), kind=kOutput, calls=%fused_computation.4 | convolution fusion | flops 805306368 | bytes 6283264 | tf_op jit(solution)/shard_map/conv_general_dilated | solution.py:75
  59.7 1.9 fusion.24
  61.6 3.0 slice.296
  64.5 2.8 slice.297
  67.4 2.6 multiply_add_fusion
  70.0 3.3 %slice.301 = f32[32,4096]{1,0:T(8,128)} slice(f32[64,4096]{1,0:T(8,128)} %multiply_add_fusion), slice={[0:63:2], [0:4096:1]} | slice | bytes 1048576 | tf_op jit(solution)/shard_map/slice | solution.py:90
  73.2 3.3 %slice.302 = f32[32,4096]{1,0:T(8,128)} slice(f32[64,4096]{1,0:T(8,128)} %multiply_add_fusion), slice={[1:64:2], [0:4096:1]} | slice | bytes 1048576 | tf_op jit(solution)/shard_map/slice | solution.py:90
  76.5 2.1 multiply_add_fusion.1
  78.6 1.7 slice.306
  80.3 1.7 slice.307
  82.0 1.1 multiply_add_fusion.2
  86.9 1.5 multiply_add_fusion.4
  88.4 1.4 slice.321
  89.8 1.4 slice.322
  92.6 1.7 slice.333
  94.3 3.3 %slice.335 = f32[31,4096]{1,0:T(8,128)} slice(f32[64,4096]{1,0:T(8,128)} %multiply_add_fusion), slice={[2:64:2], [0:4096:1]} | slice | bytes 1015808 | tf_op jit(solution)/shard_map/slice | solution.py:90
  97.6 3.0 slice.337
  101.6 1.0 fusion.86
  107.9 1.1 pad.96
  108.9 1.5 fusion.29
  114.1 1.0 fusion.28
  115.3 2.1 pad.98
  117.4 1.1 add.274
  118.5 8.6 %pad.100 = f32[128,4096]{1,0:T(8,128)} pad(f32[64,4096]{1,0:T(8,128)} %add.274, f32[]{:T(128)} %constant.25.clone.1), padding=1_0_1x0_0_0 | pad | bytes 3145732 | tf_op jit(solution)/shard_map/pad | solution.py:90
  127.1 4.6 %pad.112 = f32[64,4096]{1,0:T(8,128)} pad(f32[32,4096]{1,0:T(8,128)} %add.281, f32[]{:T(128)} %constant.25.clone.1), padding=1_0_1x0_0_0 | pad | bytes 1572868 | tf_op jit(solution)/shard_map/pad | solution.py:90
  131.7 1.9 pad_maximum_fusion.4
  133.6 4.7 %pad.111 = f32[64,4096]{1,0:T(8,128)} pad(f32[32,4096]{1,0:T(8,128)} %pad_maximum_fusion.4, f32[]{:T(128)} %constant.25.clone.1), padding=0_1_1x0_0_0 | pad | bytes 1572868 | tf_op jit(solution)/shard_map/pad | solution.py:90
  138.3 2.8 add.282
  141.1 1.4 fusion.27
  142.5 1.1 pad_maximum_fusion.1
  143.5 4.2 %pad.99 = f32[128,4096]{1,0:T(8,128)S(1)} pad(f32[64,4096]{1,0:T(8,128)} %pad_maximum_fusion.1, f32[]{:T(128)} %constant.25.clone.1), padding=0_1_1x0_0_0 | pad | bytes 3145732 | tf_op jit(solution)/shard_map/pad | solution.py:90
  147.7 1.1 add_bitcast_fusion
  148.8 1.8 all-gather.4
  150.6 8.7 %pad.114 = f32[128,4096]{1,0:T(8,128)} pad(f32[64,4096]{1,0:T(8,128)} %add.282, f32[]{:T(128)} %constant.25.clone.1), padding=1_0_1x0_0_0 | pad | bytes 3145732 | tf_op jit(solution)/shard_map/pad | solution.py:90
  159.3 2.3 pad_maximum_fusion.2
  161.6 8.7 %pad.113 = f32[128,4096]{1,0:T(8,128)} pad(f32[64,4096]{1,0:T(8,128)} %pad_maximum_fusion.2, f32[]{:T(128)} %constant.25.clone.1), padding=0_1_1x0_0_0 | pad | bytes 3145732 | tf_op jit(solution)/shard_map/pad | solution.py:90
  170.3 1.1 add_bitcast_fusion.1
  171.4 1.8 all-gather
  173.3 11.9 %all-gather.1 = f32[4,1,4096]{2,1,0:T(1,128)S(1)} all-gather(f32[1,1,4096]{2,1,0:T(1,128)S(1)} %get-tuple-element.21), channel_id=1, replica_groups=mesh['seq_0'=8,'seq_1'=2,'seq_2'=4,'seq_3'=2,'mp'=2] {'seq_2'}, dimensions={0}, use_global_device_ids=true | all-gather | bytes 81920 | tf_op jit(solution)/shard_map/all_gather | solution.py:39
  185.1 11.9 %all-gather.5 = f32[4,1,4096]{2,1,0:T(1,128)S(1)} all-gather(f32[1,1,4096]{2,1,0:T(1,128)S(1)} %bitcast.322), channel_id=1, replica_groups=mesh['seq_0'=8,'seq_1'=2,'seq_2'=4,'seq_3'=2,'mp'=2] {'seq_2'}, dimensions={0}, use_global_device_ids=true | all-gather | bytes 81920 | tf_op jit(solution)/shard_map/all_gather | solution.py:39
  197.0 5.9 %all-gather.2 = f32[2,1,4096]{2,1,0:T(1,128)S(1)} all-gather(f32[1,1,4096]{2,1,0:T(1,128)S(1)} %get-tuple-element.16), channel_id=1, replica_groups=mesh['seq_0'=8,'seq_1'=2,'seq_2'=4,'seq_3'=2,'mp'=2] {'seq_1'}, dimensions={0}, use_global_device_ids=true | all-gather | bytes 49152 | tf_op jit(solution)/shard_map/all_gather | solution.py:39
  203.0 5.9 %all-gather.6 = f32[2,1,4096]{2,1,0:T(1,128)S(1)} all-gather(f32[1,1,4096]{2,1,0:T(1,128)S(1)} %bitcast.324), channel_id=1, replica_groups=mesh['seq_0'=8,'seq_1'=2,'seq_2'=4,'seq_3'=2,'mp'=2] {'seq_1'}, dimensions={0}, use_global_device_ids=true | all-gather | bytes 49152 | tf_op jit(solution)/shard_map/all_gather | solution.py:39
  208.9 24.6 %all-gather.3 = f32[8,1,4096]{2,1,0:T(1,128)S(1)} all-gather(f32[1,1,4096]{2,1,0:T(1,128)S(1)} %get-tuple-element.19), channel_id=1, replica_groups=mesh['seq_0'=8,'seq_1'=2,'seq_2'=4,'seq_3'=2,'mp'=2] {'seq_0'}, dimensions={0}, use_global_device_ids=true | all-gather | bytes 147456 | tf_op jit(solution)/shard_map/all_gather | solution.py:39
  233.5 24.7 %all-gather.7 = f32[8,1,4096]{2,1,0:T(1,128)S(1)} all-gather(f32[1,1,4096]{2,1,0:T(1,128)S(1)} %bitcast.323), channel_id=1, replica_groups=mesh['seq_0'=8,'seq_1'=2,'seq_2'=4,'seq_3'=2,'mp'=2] {'seq_0'}, dimensions={0}, use_global_device_ids=true | all-gather | bytes 147456 | tf_op jit(solution)/shard_map/all_gather | solution.py:39
  258.5 4.4 %multiply_convert_fusion = bf16[128,4096]{1,0:T(8,128)(2,1)S(1)} fusion(f32[128,4096]{1,0:T(8,128)} %pad.113, f32[128,4096]{1,0:T(8,128)} %pad.114, f32[128,4096]{1,0:T(8,128)} %copy-done.5, f32[128,4096]{1,0:T(8,128)} %pad.100, bf16[128,4096]{1,0:T(8,128)(2,1)S(1)} %copy-done.12, f32[4096]{0:T(1024)S(1)} %copy-done.30, f32[4096]{0:T(1024)S(1)} %bitcast.325), kind=kLoop, calls=%fused_computation.28 | loop fusion | flops 4194304 | bytes 10518528 | tf_op jit(solution)/shard_map/convert_element_type | solution.py:96
  263.0 1.7 pad_maximum_fusion
  264.7 1.9 collective-permute-start.1
  266.6 1.3 copy.54
  267.9 1.6 copy.56
  269.7 1.3 copy.62
  271.0 27.0 %collective-permute-done.1 = bf16[2,128,4096]{2,1,0:T(8,128)(2,1)} collective-permute-done((bf16[2,128,4096]{2,1,0:T(8,128)(2,1)}, bf16[2,128,4096]{2,1,0:T(8,128)(2,1)}, u32[]{:S(2)}, u32[]{:S(2)}) %collective-permute-start.1) | collective-permute-done | bytes 2097184 | tf_op jit(solution)/shard_map/ppermute | solution.py:25
  298.0 2.7 fusion.85
  301.4 2.3 copy.61
  304.4 1.1 fusion.87
  306.6 1.3 copy.59
  (133 shorter events, 18.8 us)
Async XLA Ops:
  0.6 303.1 %copy-start = (bf16[128,4096]{1,0:T(8,128)(2,1)S(1)}, bf16[128,4096]{1,0:T(8,128)(2,1)}, u32[]{:S(2)}) copy-start(bf16[128,4096]{1,0:T(8,128)(2,1)} %param.18) | copy-start | bytes 3145732
  8.6 5.4 %copy-start.11 = (bf16[128,4096]{1,0:T(8,128)(2,1)S(1)}, bf16[128,4096]{1,0:T(8,128)(2,1)}, u32[]{:S(2)}) copy-start(bf16[128,4096]{1,0:T(8,128)(2,1)} %param.14) | copy-start | bytes 3145732
  11.9 12.7 %copy-start.31 = (f32[4096]{0:T(1024)S(1)}, f32[4096]{0:T(1024)}, u32[]{:S(2)}) copy-start(f32[4096]{0:T(1024)} %param.17) | copy-start | bytes 49156
  11.9 22.3 %collective-permute-start = (bf16[127,4096]{1,0:T(8,128)(2,1)}, bf16[127,4096]{1,0:T(8,128)(2,1)}, u32[]{:S(2)}, u32[]{:S(2)}) collective-permute-start(bf16[127,4096]{1,0:T(8,128)(2,1)} %slice.417), channel_id=1, source_target_pairs={{0,2},{2,4},{4,6},{6,8},{8,10},{10,12},{12,14},{14,16},{16,18},{18... | collective-permute-start | bytes 3121160 | tf_op jit(solution)/shard_map/ppermute | solution.py:25
  25.3 10.5 %copy-start.27 = (f32[4096]{0:T(1024)}, f32[4096]{0:T(1024)S(1)}, u32[]{:S(2)}) copy-start(f32[4096]{0:T(1024)S(1)} %get-tuple-element.32) | copy-start | bytes 49156
  25.3 10.5 %copy-start.29 = (f32[4096]{0:T(1024)}, f32[4096]{0:T(1024)S(1)}, u32[]{:S(2)}) copy-start(f32[4096]{0:T(1024)S(1)} %get-tuple-element.31) | copy-start | bytes 49156
  25.3 42.1 %copy-start.20 = (f32[4096]{0:T(1024)}, f32[4096]{0:T(1024)S(1)}, u32[]{:S(2)}) copy-start(f32[4096]{0:T(1024)S(1)} %get-tuple-element.34) | copy-start | bytes 49156
  25.3 51.2 %copy-start.22 = (f32[4096]{0:T(1024)}, f32[4096]{0:T(1024)S(1)}, u32[]{:S(2)}) copy-start(f32[4096]{0:T(1024)S(1)} %get-tuple-element.33) | copy-start | bytes 49156
  25.3 56.7 %copy-start.24 = (f32[4096]{0:T(1024)}, f32[4096]{0:T(1024)S(1)}, u32[]{:S(2)}) copy-start(f32[4096]{0:T(1024)S(1)} %get-tuple-element.27) | copy-start | bytes 49156
  25.3 59.2 %copy-start.25 = (f32[4096]{0:T(1024)}, f32[4096]{0:T(1024)S(1)}, u32[]{:S(2)}) copy-start(f32[4096]{0:T(1024)S(1)} %get-tuple-element.28) | copy-start | bytes 49156
  26.7 9.1 %copy-start.9 = (f32[128,4096]{1,0:T(8,128)S(1)}, f32[128,4096]{1,0:T(8,128)}, u32[]{:S(2)}) copy-start(f32[128,4096]{1,0:T(8,128)} %rev.3) | copy-start | bytes 6291460
  35.8 23.9 %copy-start.16 = (bf16[128,4096]{1,0:T(8,128)(2,1)S(1)}, bf16[128,4096]{1,0:T(8,128)(2,1)}, u32[]{:S(2)}) copy-start(bf16[128,4096]{1,0:T(8,128)(2,1)} %param.12) | copy-start | bytes 3145732
  35.8 23.9 %copy-start.17 = (bf16[128,4096]{1,0:T(8,128)(2,1)S(1)}, bf16[128,4096]{1,0:T(8,128)(2,1)}, u32[]{:S(2)}) copy-start(bf16[128,4096]{1,0:T(8,128)(2,1)} %param.16) | copy-start | bytes 3145732
  61.5 39.0 %copy-start.1 = (f32[128,4096]{1,0:T(8,128)}, f32[128,4096]{1,0:T(8,128)S(1)}, u32[]{:S(2)}) copy-start(f32[128,4096]{1,0:T(8,128)S(1)} %fusion.24) | copy-start | bytes 6291460
  83.1 17.5 %copy-start.10 = (f32[16,4096]{1,0:T(8,128)}, f32[16,4096]{1,0:T(8,128)S(1)}, u32[]{:S(2)}) copy-start(f32[16,4096]{1,0:T(8,128)S(1)} %multiply_add_fusion.2) | copy-start | bytes 786436
  85.5 15.1 %copy-start.18 = (f32[8,4096]{1,0:T(8,128)}, f32[8,4096]{1,0:T(8,128)S(1)}, u32[]{:S(2)}) copy-start(f32[8,4096]{1,0:T(8,128)S(1)} %multiply_add_fusion.3) | copy-start | bytes 393220
  91.9 9.6 %copy-start.28 = (f32[4096]{0:T(1024)S(1)}, f32[4096]{0:T(1024)}, u32[]{:S(2)}) copy-start(f32[4096]{0:T(1024)} %copy-done.27) | copy-start | bytes 49156
  100.6 5.7 %slice-start.4 = ((f32[8,4096]{1,0:T(8,128)}), f32[1,4096]{1,0:T(1,128)S(1)}, s32[]{:S(2)}) async-start(f32[8,4096]{1,0:T(8,128)} %copy-done.18), calls=%async_computation.5 | async-start | bytes 32768 | tf_op jit(solution)/shard_map/slice | solution.py:90
  100.6 5.9 %copy-start.19 = (f32[7,4096]{1,0:T(8,128)S(1)}, f32[7,4096]{1,0:T(8,128)}, u32[]{:S(2)}) copy-start(f32[7,4096]{1,0:T(8,128)} %slice.331) | copy-start | bytes 344068
  100.6 5.9 %copy-start.26 = (f32[4096]{0:T(1024)S(1)}, f32[4096]{0:T(1024)}, u32[]{:S(2)}) copy-start(f32[4096]{0:T(1024)} %copy-done.25) | copy-start | bytes 49156
  106.3 0.7 slice-start.3
  106.6 2.3 copy-start.13
  107.9 3.4 %slice-start.2 = ((f32[32,4096]{1,0:T(8,128)}), f32[1,4096]{1,0:T(1,128)S(1)}, s32[]{:S(2)}) async-start(f32[32,4096]{1,0:T(8,128)} %multiply_add_fusion.1), calls=%async_computation.3 | async-start | bytes 32768 | tf_op jit(solution)/shard_map/slice | solution.py:90
  112.3 1.8 copy-start.23
  112.4 1.7 copy-start.8
  114.1 1.0 slice-start.1
  133.6 7.5 %copy-start.21 = (f32[4096]{0:T(1024)S(1)}, f32[4096]{0:T(1024)}, u32[]{:S(2)}) copy-start(f32[4096]{0:T(1024)} %copy-done.20) | copy-start | bytes 49156
  138.3 2.8 copy-start.2
  138.3 2.8 copy-start.3
  138.3 2.8 copy-start.6
  141.1 1.4 slice-start
  147.7 13.8 %copy-start.5 = (f32[128,4096]{1,0:T(8,128)}, f32[128,4096]{1,0:T(8,128)S(1)}, u32[]{:S(2)}) copy-start(f32[128,4096]{1,0:T(8,128)S(1)} %pad.99) | copy-start | bytes 6291460
  161.6 96.9 %copy-start.30 = (f32[4096]{0:T(1024)S(1)}, f32[4096]{0:T(1024)}, u32[]{:S(2)}) copy-start(f32[4096]{0:T(1024)} %get-tuple-element.26) | copy-start | bytes 49156
  170.3 88.2 %copy-start.12 = (bf16[128,4096]{1,0:T(8,128)(2,1)S(1)}, bf16[128,4096]{1,0:T(8,128)(2,1)}, u32[]{:S(2)}) copy-start(bf16[128,4096]{1,0:T(8,128)(2,1)} %param.15) | copy-start | bytes 3145732
  258.5 4.5 %copy-start.7 = (bf16[128,4096]{1,0:T(8,128)(2,1)S(1)}, bf16[128,4096]{1,0:T(8,128)(2,1)}, u32[]{:S(2)}) copy-start(bf16[128,4096]{1,0:T(8,128)(2,1)} %param.19) | copy-start | bytes 3145732
  263.0 6.7 %copy-start.4 = (bf16[128,4096]{1,0:T(8,128)(2,1)}, bf16[128,4096]{1,0:T(8,128)(2,1)S(1)}, u32[]{:S(2)}) copy-start(bf16[128,4096]{1,0:T(8,128)(2,1)S(1)} %multiply_convert_fusion) | copy-start | bytes 3145732
  264.7 33.4 %collective-permute-start.1 = (bf16[2,128,4096]{2,1,0:T(8,128)(2,1)}, bf16[2,128,4096]{2,1,0:T(8,128)(2,1)}, u32[]{:S(2)}, u32[]{:S(2)}) collective-permute-start(bf16[2,128,4096]{2,1,0:T(8,128)(2,1)} %pad_maximum_fusion), channel_id=1, source_target_pairs={{0,2},{2,4},{4,6},{6,8},{8,10},{10,12},{12,14},{14,16},{16,18},{18... | collective-permute-start | bytes 6291464 | tf_op jit(solution)/shard_map/ppermute | solution.py:25
  304.4 1.2 copy-start.14
  304.4 1.5 copy-start.15
where the time goes:
time: 311 us; the launch traced here: 308 us
  local copies, waits for them, and re-layouts  99.3 us (32%)
  blocking collectives  94.8 us (30%)
  other arithmetic  48.7 us (16%)
  waiting for transfers between devices  34.6 us (11%)
  matrix products  25.3 us (8%)
  starting transfers between devices  3.95 us (1%)
    all_gather x8, blocking collectives, entering(): pieces = jax.tree.map(lambda part: lax.all_gather(part, axis), so_far)  88.5 us
    pad x24, local copies, waits for them, and re-layouts, on_device(): lax.associative_scan(pair_combine, (factors, long_in.astype(jnp.float32))...  44.7 us
    ppermute x2, waiting for transfers between devices, shifted(): return lax.ppermute(block, axis, route)  34.6 us
    slice x27, local copies, waits for them, and re-layouts, on_device(): lax.associative_scan(pair_combine, (factors, long_in.astype(jnp.float32))...  31 us
    conv_general_dilated x1, matrix products, on_device(): lax.conv_general_dilated(extended[None], kernel, (1,), [(0, 0)], dimensio...  23.9 us
    add x14, other arithmetic, pair_combine(): second_pair[0] * first_pair[1] + second_pair[1]  14.4 us
    rev x1, local copies, waits for them, and re-layouts, on_device(): kernel = short_filter.astype(jnp.float32)[::-1][:, None, :]  10.6 us
    concatenate x11, other arithmetic, on_device(): lax.associative_scan(pair_combine, (factors, long_in.astype(jnp.float32))...  8.66 us
  transfers between devices with their start and end apart: 2, of which 2 were waited for; matrix products, arithmetic and copies ran while one was open for 6% of the time, Pallas kernels for 0%

commit v1 on v0

v1 whole, which is shorter than its diff:
```python
import jax
import jax.numpy as jnp
import numpy as np
from jax import lax
from jax.experimental import pallas as pl
from jax.experimental.pallas import tpu as pltpu
from jax.sharding import Mesh
from jax.sharding import PartitionSpec as P

D = 8192
HEAD_DIM = 128
BLOCK = 128
SEQ = ("seq_0", "seq_1", "seq_2", "seq_3")
NEAR = ("seq_2", "seq_3")
FAR = ("seq_0", "seq_1")
F32 = jnp.float32
BF16 = jnp.bfloat16
SUB = 256


def dft_matrices():
    n = 2 * BLOCK
    k = np.arange(BLOCK, dtype=np.float64)[:, None]
    t = np.arange(n, dtype=np.float64)[None, :]
    angle = np.pi * (2 * k + 1) * t / n
    forward = np.concatenate([np.cos(angle), -np.sin(angle)], axis=0)
    back = np.concatenate([np.cos(angle), -np.sin(angle)], axis=0).T[BLOCK:] * (2.0 / n)
    return forward.astype(np.float32), back.astype(np.float32)


FORWARD, BACK = dft_matrices()


def split(value):
    high = value.astype(BF16)
    return high, (value - high.astype(F32)).astype(BF16)


def dot(a, b):
    return jnp.dot(a, b, preferred_element_type=F32)


def shifted(block, axis, distance):
    size = lax.axis_size(axis)
    return lax.ppermute(block, axis, [(i, i + distance) for i in range(size - distance)])


def copies(array, axis):
    sent = jnp.broadcast_to(array, (lax.axis_size(axis), *array.shape))
    return lax.all_to_all(sent, axis, split_axis=0, concat_axis=0, tiled=True)


def gate_body(stream, inner, gain, v, squares, acc):
    step = pl.program_id(0)
    x = stream[...].astype(F32)
    v[...] = (inner[...].astype(F32) * x * gain[...]).astype(BF16)
    sq = x * x
    part = sq[:, :128]
    for j in range(1, x.shape[1] // 128):
        part = part + sq[:, j * 128 : (j + 1) * 128]

    @pl.when(step == 0)
    def _():
        acc[...] = part

    @pl.when(step > 0)
    def _():
        acc[...] = acc[...] + part

    @pl.when(step == pl.num_programs(0) - 1)
    def _():
        squares[...] = jnp.sum(acc[...].T, axis=0, keepdims=True)


def gated(stream, inner, gain, tile=1024):
    rows, width = stream.shape
    wide = pl.BlockSpec((rows, tile), lambda i: (0, i))
    return pl.pallas_call(
        gate_body,
        grid=(width // tile,),
        in_specs=[wide, wide, pl.BlockSpec((1, tile), lambda i: (0, i))],
        out_specs=[wide, pl.BlockSpec((1, rows), lambda i: (0, 0))],
        out_shape=[
            jax.ShapeDtypeStruct((rows, width), BF16),
            jax.ShapeDtypeStruct((1, rows), F32),
        ],
        scratch_shapes=[pltpu.VMEM((rows, 128), F32)],
        name="gated",
    )(stream, inner, gain)


def conv_body(
    before, here, taps, factor, forward, back, lower, inner, outer, decay, local, state, fr_hi, fr_lo
):
    step = pl.program_id(0)

    @pl.when(step == 0)
    def _():
        hi, lo = split(forward[...] * factor[...])
        fr_hi[...] = hi
        fr_lo[...] = lo

    f_hi, f_lo = split(forward[:, :BLOCK])
    b_hi, b_lo = split(back[...])
    for j in range(here.shape[1] // SUB):
        at = slice(j * SUB, (j + 1) * SUB)
        s = jnp.concatenate([before[:, at], here[:, at]], axis=0)
        x = dot(fr_hi[...], s) + dot(fr_lo[...], s)
        f = taps[:, at]
        h = dot(f_hi, f) + dot(f_lo, f)
        x_re, x_im = x[:BLOCK], x[BLOCK:]
        h_re, h_im = h[:BLOCK], h[BLOCK:]
        y = jnp.concatenate([x_re * h_re - x_im * h_im, x_re * h_im + x_im * h_re], axis=0)
        y_hi, y_lo = split(y)
        conv = dot(b_hi, y_hi) + dot(b_hi, y_lo) + dot(b_lo, y_hi)
        long_in = (inner[:, at].astype(F32) * outer[:, at].astype(F32) * conv).astype(BF16)
        d = decay[:, at]
        time = lax.broadcasted_iota(jnp.int32, (BLOCK, SUB), 0).astype(F32)
        z_hi, z_lo = split(long_in.astype(F32) * jnp.exp(d * time))
        total = dot(lower[...], z_hi) + dot(lower[...], z_lo)
        result = total * jnp.exp(-d * time)
        local[:, at] = result
        state[:, at] = result[BLOCK - 1 :]


def conv_scan(before, here, taps, factor, inner, outer, decay, tile=1024):
    rows, width = here.shape
    wide = pl.BlockSpec((rows, tile), lambda i: (0, i))
    row = pl.BlockSpec((1, tile), lambda i: (0, i))
    whole = lambda shape: pl.BlockSpec(shape, lambda i: (0, 0))
    lower = jnp.asarray(np.tril(np.ones((rows, rows), np.float32)), BF16)
    return pl.pallas_call(
        conv_body,
        grid=(width // tile,),
        in_specs=[
            wide,
            wide,
            wide,
            whole((1, 2 * rows)),
            whole((2 * rows, 2 * rows)),
            whole((rows, 2 * rows)),
            whole((rows, rows)),
            wide,
            wide,
            row,
        ],
        out_specs=[wide, row],
        out_shape=[
            jax.ShapeDtypeStruct((rows, width), F32),
            jax.ShapeDtypeStruct((1, width), F32),
        ],
        scratch_shapes=[pltpu.VMEM((2 * rows, 2 * rows), BF16)] * 2,
        name="conv_scan",
    )(before, here, taps, factor, jnp.asarray(FORWARD), jnp.asarray(BACK), lower, inner, outer, decay)


def mix_body(local, outer, decay, scale, carry, mixed):
    d = decay[...]
    time = lax.broadcasted_iota(jnp.int32, local.shape, 0).astype(F32)
    state = local[...] + jnp.exp(-d * (time + 1.0)) * carry[...]
    mixed[...] = (outer[...].astype(F32) * (state * scale[...])).astype(BF16)


def mix(local, outer, decay, scale, carry, tile=1024):
    rows, width = local.shape
    wide = pl.BlockSpec((rows, tile), lambda i: (0, i))
    row = pl.BlockSpec((1, tile), lambda i: (0, i))
    return pl.pallas_call(
        mix_body,
        grid=(width // tile,),
        in_specs=[wide, wide, row, row, row],
        out_specs=wide,
        out_shape=jax.ShapeDtypeStruct((rows, width), BF16),
        name="mix",
    )(local, outer, decay, scale, carry)


def weigh_body(first, query, key_before, key_here, weights):
    rows = query.shape[0]
    row_pos = lax.broadcasted_iota(jnp.int32, (rows, 2 * rows), 0)
    col_pos = lax.broadcasted_iota(jnp.int32, (rows, 2 * rows), 1)
    lowest = jnp.where(first[0] > 0, rows, 0)
    valid = (col_pos <= row_pos + rows) & (col_pos >= lowest)
    for j in range(query.shape[1] // HEAD_DIM):
        at = slice(j * HEAD_DIM, (j + 1) * HEAD_DIM)
        keys = jnp.concatenate([key_before[:, at], key_here[:, at]], axis=0)
        scores = lax.dot_general(
            query[:, at], keys, (((1,), (1,)), ((), ())), preferred_element_type=F32
        ) * HEAD_DIM ** (-0.5)
        scores = jnp.where(valid, scores, -1e30)
        top = jnp.max(scores, axis=1, keepdims=True)
        e = jnp.exp(scores - top)
        weights[j] = (e * (1.0 / jnp.sum(e, axis=1, keepdims=True))).astype(BF16)


def weigh(first, query, key_before, key_here, tile=1024):
    rows, width = query.shape
    heads = tile // HEAD_DIM
    wide = pl.BlockSpec((rows, tile), lambda i: (0, i))
    return pl.pallas_call(
        weigh_body,
        grid=(width // tile,),
        in_specs=[pl.BlockSpec(memory_space=pltpu.SMEM), wide, wide, wide],
        out_specs=pl.BlockSpec((heads, rows, 2 * rows), lambda i: (i, 0, 0)),
        out_shape=jax.ShapeDtypeStruct((width // HEAD_DIM, rows, 2 * rows), BF16),
        cost_estimate=pl.CostEstimate(flops=4 * 10**9, transcendentals=10**6, bytes_accessed=5 * 10**6),
        name="weigh",
    )(first, query, key_before, key_here)


def attend_body(weights, before, here, out):
    for j in range(weights.shape[0]):
        at = slice(j * HEAD_DIM, (j + 1) * HEAD_DIM)
        values = jnp.concatenate([before[:, at], here[:, at]], axis=0)
        out[:, at] = dot(weights[j], values).astype(BF16)


def attend(weights, before, here, tile=1024):
    rows, width = here.shape
    heads = tile // HEAD_DIM
    wide = pl.BlockSpec((rows, tile), lambda i: (0, i))
    return pl.pallas_call(
        attend_body,
        grid=(width // tile,),
        in_specs=[pl.BlockSpec((heads, rows, 2 * rows), lambda i: (i, 0, 0)), wide, wide],
        out_specs=wide,
        out_shape=jax.ShapeDtypeStruct((rows, width), BF16),
        name="attend",
    )(weights, before, here)


def weighted(pieces, place, rate):
    size = pieces.shape[0]
    pieces = pieces.astype(F32)
    k = lax.broadcasted_iota(jnp.int32, (size, 1, 1), 0)
    gap = place - 1 - k
    inside = jnp.where(gap >= 0, jnp.exp(-rate * jnp.maximum(gap, 0).astype(F32)), 0.0)
    return jnp.sum(inside * pieces, axis=0)


def on_device(
    stream,
    norm_gain,
    short_outer,
    short_inner,
    short_filter,
    long_outer,
    long_inner,
    long_decay,
    query_heads,
    key_heads,
):
    rows, width = stream.shape
    decay = long_decay[None]
    scale = jnp.sqrt(-jnp.expm1(-2.0 * decay))
    v, squares = gated(stream, short_inner, norm_gain[None])
    squares_before = shifted(squares, SEQ, 1)
    v, squares_before = lax.optimization_barrier((v, squares_before))
    v_before = shifted(v, SEQ, 1)
    both = jnp.concatenate([squares_before, squares], axis=1)
    totals = jnp.sum(copies(both, "mp"), axis=0)
    factor = 1.0 / jnp.sqrt(totals / D + 0.5)
    keys, factor = lax.optimization_barrier((key_heads, factor))
    key_before = shifted(keys, SEQ, 1)
    local, state = conv_scan(
        v_before, v, short_filter, factor, long_inner, short_outer, decay
    )
    near, far = lax.axis_index(NEAR), lax.axis_index(FAR)
    near_size = lax.axis_size(NEAR)
    rate = long_decay.reshape(width // 128, 128) * rows
    pieces = copies(state.reshape(width // 128, 128).astype(BF16), NEAR)
    group = weighted(pieces, near_size, rate)
    others = copies(group.astype(BF16), FAR)
    entering = weighted(pieces, near, rate) + jnp.exp(-rate * near.astype(F32)) * weighted(
        others, far, rate * near_size
    )
    mixed = mix(local, long_outer, decay, scale, entering.reshape(1, width))
    mixed_before = shifted(mixed, SEQ, 1)
    first = (lax.axis_index(SEQ) == 0).astype(jnp.int32)[None]
    weights = weigh(first, query_heads, key_before, key_heads)
    attended = attend(weights, mixed_before, mixed)
    return (mixed, attended)


def solution(mesh):
    finer = Mesh(
        mesh.devices.reshape(8, 2, 4, 2, mesh.shape["mp"]),
        ("seq_0", "seq_1", "seq_2", "seq_3", "mp"),
    )
    placed = (
        P(SEQ, "mp"),
        P("mp"),
        P(SEQ, "mp"),
        P(SEQ, "mp"),
        P(None, "mp"),
        P(SEQ, "mp"),
        P(SEQ, "mp"),
        P("mp"),
        P(SEQ, "mp"),
        P(SEQ, "mp"),
    )
    return jax.shard_map(
        on_device,
        mesh=finer,
        in_specs=placed,
        out_specs=(P(SEQ, "mp"), P(SEQ, "mp")),
        check_vma=False,
    )
```

time: 311 us -> 112 us (0.36)
  the two profiles are of different devices: /device:TPU:128 before, /device:TPU:34 now
where the time goes in v1:
time: 112 us; the launch traced here: 111 us
  waiting for transfers between devices  47 us (42%)
  Pallas kernels  29.9 us (27%)
  starting transfers between devices  25.7 us (23%)
  local copies, waits for them, and re-layouts  4.83 us (4%)
  other arithmetic  2.94 us (3%)
    ppermute x4, waiting for transfers between devices, shifted(): lax.ppermute(block, axis, [(i, i + distance) for i in range(size - distan...  32.1 us
    all_to_all x3, starting transfers between devices, copies(): return lax.all_to_all(sent, axis, split_axis=0, concat_axis=0, tiled=True)  18.1 us
    all_to_all x3, waiting for transfers between devices, copies(): return lax.all_to_all(sent, axis, split_axis=0, concat_axis=0, tiled=True)  14.9 us
    pallas_call x1, Pallas kernels, conv_scan(): pl.pallas_call(conv_body, grid=(width // tile,), in_specs=[wide, wide, wi...  12.6 us
    ppermute x4, starting transfers between devices, shifted(): lax.ppermute(block, axis, [(i, i + distance) for i in range(size - distan...  7.64 us
    pallas_call x1, Pallas kernels, weigh(): pl.pallas_call(weigh_body, grid=(width // tile,), in_specs=[pl.BlockSpec(...  4.97 us
    pallas_call x1, Pallas kernels, attend(): pl.pallas_call(attend_body, grid=(width // tile,), in_specs=[pl.BlockSpec...  4.43 us
    pallas_call x1, Pallas kernels, mix(): pl.pallas_call(mix_body, grid=(width // tile,), in_specs=[wide, wide, row...  4.05 us
  transfers between devices with their start and end apart: 7, of which 7 were waited for; matrix products, arithmetic and copies ran while one was open for 2% of the time, Pallas kernels for 8%

profile of v1, /device:TPU:34, one launch (start us, length us, event | category | flops | bytes accessed | tf_op | source)
XLA Modules:
  0.0 111.2 jit_solution(1819781184291011118)
XLA Ops:
  0.6 0.0 copy-start.2
  0.6 3.9 %gated.1 = (bf16[128,4096]{1,0:T(8,128)(2,1)}, f32[1,128]{1,0:T(1,128)}) custom-call(bf16[128,4096]{1,0:T(8,128)(2,1)} %stream.1, bf16[128,4096]{1,0:T(8,128)(2,1)} %inner.2, f32[1,4096]{1,0:T(1,128)} %bitcast.23), custom_call_target="tpu_custom_call" | custom-call | tf_op jit(solution)/shard_map/gated/pallas_call | solution.py:78
  4.5 1.9 %collective-permute-start = (f32[1,128]{1,0:T(1,128)}, f32[1,128]{1,0:T(1,128)S(1)}, u32[]{:S(2)}, u32[]{:S(2)}) collective-permute-start(f32[1,128]{1,0:T(1,128)} %get-tuple-element.11), channel_id=1, source_target_pairs={{0,2},{2,4},{4,6},{6,8},{8,10},{10,12},{12,14},{14,16},{16,18},{18... | collective-permute-start | bytes 1544 | tf_op jit(solution)/shard_map/ppermute | solution.py:45
  6.4 7.6 %collective-permute-done = f32[1,128]{1,0:T(1,128)S(1)} collective-permute-done((f32[1,128]{1,0:T(1,128)}, f32[1,128]{1,0:T(1,128)S(1)}, u32[]{:S(2)}, u32[]{:S(2)}) %collective-permute-start) | collective-permute-done | bytes 544 | tf_op jit(solution)/shard_map/ppermute | solution.py:45
  14.0 1.9 %collective-permute-start.1 = (bf16[128,4096]{1,0:T(8,128)(2,1)}, bf16[128,4096]{1,0:T(8,128)(2,1)S(1)}, u32[]{:S(2)}, u32[]{:S(2)}) collective-permute-start(bf16[128,4096]{1,0:T(8,128)(2,1)} %get-tuple-element.12.here), channel_id=1, source_target_pairs={{0,2},{2,4},{4,6},{6,8},{8,10},{10,12},{12,14},{14,16},{16,18},{18... | collective-permute-start | bytes 3145736 | tf_op jit(solution)/shard_map/ppermute | solution.py:45
  16.0 0.0 copy-done.2
  16.0 0.7 pad_maximum_fusion
  16.6 0.6 broadcast_in_dim.54
  17.2 3.7 %all-to-all-start = ((f32[2,1,256]{2,1,0:T(1,128)}), f32[2,1,256]{2,1,0:T(1,128)S(1)}, u32[]{:S(2)}, u32[]{:S(2)}) async-start(f32[2,1,256]{2,1,0:T(1,128)} %broadcast_in_dim.54), calls=%async_computation | async-start | bytes 4096 | tf_op jit(solution)/shard_map/all_to_all | solution.py:50
  21.0 1.8 %all-to-all-done = f32[2,1,256]{2,1,0:T(1,128)S(1)} async-done(((f32[2,1,256]{2,1,0:T(1,128)}), f32[2,1,256]{2,1,0:T(1,128)S(1)}, u32[]{:S(2)}, u32[]{:S(2)}) %all-to-all-start) | async-done | bytes 2080 | tf_op jit(solution)/shard_map/all_to_all | solution.py:50
  22.8 0.6 add_rsqrt_fusion
  23.3 11.5 %collective-permute-done.1.before = bf16[128,4096]{1,0:T(8,128)(2,1)S(1)} collective-permute-done((bf16[128,4096]{1,0:T(8,128)(2,1)}, bf16[128,4096]{1,0:T(8,128)(2,1)S(1)}, u32[]{:S(2)}, u32[]{:S(2)}) %collective-permute-start.1) | collective-permute-done | bytes 1048608 | tf_op jit(solution)/shard_map/ppermute | solution.py:45
  34.9 0.0 copy-start.1
  34.9 1.0 copy-done.1
  35.8 0.0 copy-start.4
  35.8 0.0 copy-start.3
  35.8 12.6 %conv_scan.1 = (f32[128,4096]{1,0:T(8,128)}, f32[1,4096]{1,0:T(1,128)}) custom-call(bf16[128,4096]{1,0:T(8,128)(2,1)} %copy-done.1, bf16[128,4096]{1,0:T(8,128)(2,1)} %get-tuple-element.12.here, bf16[128,4096]{1,0:T(8,128)(2,1)} %taps.1, f32[1,256]{1,0:T(1,128)} %bitcast.24, f32[256,256]{1,0:T(8,128)} %constant.57.clone.forward, ...), custom_call_target="tpu_custom_call" | custom-call | tf_op jit(solution)/shard_map/conv_scan/pallas_call | solution.py:132
  48.4 0.8 convert_reduce_fusion
  49.2 0.6 broadcast_in_dim.58
  49.8 3.4 %all-to-all-start.1 = ((bf16[8,32,128]{2,1,0:T(8,128)(2,1)}), bf16[8,32,128]{2,1,0:T(8,128)(2,1)S(1)}, u32[]{:S(2)}, u32[]{:S(2)}) async-start(bf16[8,32,128]{2,1,0:T(8,128)(2,1)} %broadcast_in_dim.58), calls=%async_computation.1 | async-start | bytes 131072 | tf_op jit(solution)/shard_map/all_to_all | solution.py:50
  53.2 5.5 %all-to-all-done.1 = bf16[8,32,128]{2,1,0:T(8,128)(2,1)S(1)} async-done(((bf16[8,32,128]{2,1,0:T(8,128)(2,1)}), bf16[8,32,128]{2,1,0:T(8,128)(2,1)S(1)}, u32[]{:S(2)}, u32[]{:S(2)}) %all-to-all-start.1) | async-done | bytes 65568 | tf_op jit(solution)/shard_map/all_to_all | solution.py:50
  58.7 0.1 fusion
  58.9 0.7 broadcast_in_dim.62
  59.6 11.0 %all-to-all-start.2 = ((bf16[16,32,128]{2,1,0:T(8,128)(2,1)}), bf16[16,32,128]{2,1,0:T(8,128)(2,1)S(1)}, u32[]{:S(2)}, u32[]{:S(2)}) async-start(bf16[16,32,128]{2,1,0:T(8,128)(2,1)} %broadcast_in_dim.62), calls=%async_computation.2 | async-start | bytes 262144 | tf_op jit(solution)/shard_map/all_to_all | solution.py:50
  70.6 0.0 copy-done.4
  70.6 1.9 %collective-permute-start.2 = (bf16[128,4096]{1,0:T(8,128)(2,1)S(1)}, bf16[128,4096]{1,0:T(8,128)(2,1)S(1)}, u32[]{:S(2)}, u32[]{:S(2)}) collective-permute-start(bf16[128,4096]{1,0:T(8,128)(2,1)S(1)} %copy-done.4), channel_id=1, source_target_pairs={{0,2},{2,4},{4,6},{6,8},{8,10},{10,12},{12,14},{14,16},{16,18},{18... | collective-permute-start | bytes 3145736 | tf_op jit(solution)/shard_map/ppermute | solution.py:45
  72.5 7.6 %all-to-all-done.2 = bf16[16,32,128]{2,1,0:T(8,128)(2,1)S(1)} async-done(((bf16[16,32,128]{2,1,0:T(8,128)(2,1)}), bf16[16,32,128]{2,1,0:T(8,128)(2,1)S(1)}, u32[]{:S(2)}, u32[]{:S(2)}) %all-to-all-start.2) | async-done | bytes 131104 | tf_op jit(solution)/shard_map/all_to_all | solution.py:50
  80.1 0.1 multiply_reduce_fusion
  80.3 0.0 copy-done.3
  80.3 0.6 fusion.2
  80.9 4.1 %mix.1.here = bf16[128,4096]{1,0:T(8,128)(2,1)} custom-call(f32[128,4096]{1,0:T(8,128)} %get-tuple-element.15.local, bf16[128,4096]{1,0:T(8,128)(2,1)} %outer.3, f32[1,4096]{1,0:T(1,128)} %bitcast.19, f32[1,4096]{1,0:T(1,128)} %bitcast.21, f32[1,4096]{1,0:T(1,128)} %bitcast.20), custom_call_target="tpu_custom_call" | custom-call | tf_op jit(solution)/shard_map/mix/pallas_call | solution.py:168
  85.0 1.9 %collective-permute-start.3 = (bf16[128,4096]{1,0:T(8,128)(2,1)}, bf16[128,4096]{1,0:T(8,128)(2,1)S(1)}, u32[]{:S(2)}, u32[]{:S(2)}) collective-permute-start(bf16[128,4096]{1,0:T(8,128)(2,1)} %mix.1.here), channel_id=1, source_target_pairs={{0,2},{2,4},{4,6},{6,8},{8,10},{10,12},{12,14},{14,16},{16,18},{18... | collective-permute-start | bytes 3145736 | tf_op jit(solution)/shard_map/ppermute | solution.py:45
  86.9 4.5 %collective-permute-done.2.key_before = bf16[128,4096]{1,0:T(8,128)(2,1)S(1)} collective-permute-done((bf16[128,4096]{1,0:T(8,128)(2,1)S(1)}, bf16[128,4096]{1,0:T(8,128)(2,1)S(1)}, u32[]{:S(2)}, u32[]{:S(2)}) %collective-permute-start.2) | collective-permute-done | bytes 1048608 | tf_op jit(solution)/shard_map/ppermute | solution.py:45
  91.4 0.0 copy-start.5
  91.4 1.0 copy-done.5
  92.3 5.0 %weigh.1.weights = bf16[32,128,256]{2,1,0:T(8,128)(2,1)} custom-call(s32[1]{0:T(128)} %bitcast.10.first, bf16[128,4096]{1,0:T(8,128)(2,1)} %query.1, bf16[128,4096]{1,0:T(8,128)(2,1)} %copy-done.5, bf16[128,4096]{1,0:T(8,128)(2,1)} %key_here.1), custom_call_target="tpu_custom_call" | custom-call | flops 4000000000 | bytes 5000000 | tf_op jit(solution)/shard_map/weigh/pallas_call | solution.py:200
  97.3 8.5 %collective-permute-done.3.before = bf16[128,4096]{1,0:T(8,128)(2,1)S(1)} collective-permute-done((bf16[128,4096]{1,0:T(8,128)(2,1)}, bf16[128,4096]{1,0:T(8,128)(2,1)S(1)}, u32[]{:S(2)}, u32[]{:S(2)}) %collective-permute-start.3) | collective-permute-done | bytes 1048608 | tf_op jit(solution)/shard_map/ppermute | solution.py:45
  105.8 0.0 copy-start
  105.8 1.0 copy-done
  106.8 4.4 %attend.1 = bf16[128,4096]{1,0:T(8,128)(2,1)} custom-call(bf16[32,128,256]{2,1,0:T(8,128)(2,1)} %weigh.1.weights, bf16[128,4096]{1,0:T(8,128)(2,1)} %copy-done, bf16[128,4096]{1,0:T(8,128)(2,1)} %mix.1.here), custom_call_target="tpu_custom_call" | custom-call | tf_op jit(solution)/shard_map/attend/pallas_call | solution.py:222
  (6 shorter events, 0.1 us)
Async XLA Ops:
  0.6 15.3 %copy-start.2 = (f32[4096]{0:T(1024)S(1)}, f32[4096]{0:T(1024)}, u32[]{:S(2)}) copy-start(f32[4096]{0:T(1024)} %param.20) | copy-start | bytes 49156
  4.5 9.5 %collective-permute-start = (f32[1,128]{1,0:T(1,128)}, f32[1,128]{1,0:T(1,128)S(1)}, u32[]{:S(2)}, u32[]{:S(2)}) collective-permute-start(f32[1,128]{1,0:T(1,128)} %get-tuple-element.11), channel_id=1, source_target_pairs={{0,2},{2,4},{4,6},{6,8},{8,10},{10,12},{12,14},{14,16},{16,18},{18... | collective-permute-start | bytes 1544 | tf_op jit(solution)/shard_map/ppermute | solution.py:45
  14.0 20.8 %collective-permute-start.1 = (bf16[128,4096]{1,0:T(8,128)(2,1)}, bf16[128,4096]{1,0:T(8,128)(2,1)S(1)}, u32[]{:S(2)}, u32[]{:S(2)}) collective-permute-start(bf16[128,4096]{1,0:T(8,128)(2,1)} %get-tuple-element.12.here), channel_id=1, source_target_pairs={{0,2},{2,4},{4,6},{6,8},{8,10},{10,12},{12,14},{14,16},{16,18},{18... | collective-permute-start | bytes 3145736 | tf_op jit(solution)/shard_map/ppermute | solution.py:45
  17.2 5.5 %all-to-all-start = ((f32[2,1,256]{2,1,0:T(1,128)}), f32[2,1,256]{2,1,0:T(1,128)S(1)}, u32[]{:S(2)}, u32[]{:S(2)}) async-start(f32[2,1,256]{2,1,0:T(1,128)} %broadcast_in_dim.54), calls=%async_computation | async-start | bytes 4096 | tf_op jit(solution)/shard_map/all_to_all | solution.py:50
  34.9 1.0 copy-start.1
  35.8 34.7 %copy-start.4 = (bf16[128,4096]{1,0:T(8,128)(2,1)S(1)}, bf16[128,4096]{1,0:T(8,128)(2,1)}, u32[]{:S(2)}) copy-start(bf16[128,4096]{1,0:T(8,128)(2,1)} %key_here.1) | copy-start | bytes 3145732
  35.8 44.4 %copy-start.3 = (f32[4096]{0:T(1024)S(1)}, f32[4096]{0:T(1024)}, u32[]{:S(2)}) copy-start(f32[4096]{0:T(1024)} %param.20) | copy-start | bytes 49156
  49.8 8.9 %all-to-all-start.1 = ((bf16[8,32,128]{2,1,0:T(8,128)(2,1)}), bf16[8,32,128]{2,1,0:T(8,128)(2,1)S(1)}, u32[]{:S(2)}, u32[]{:S(2)}) async-start(bf16[8,32,128]{2,1,0:T(8,128)(2,1)} %broadcast_in_dim.58), calls=%async_computation.1 | async-start | bytes 131072 | tf_op jit(solution)/shard_map/all_to_all | solution.py:50
  59.6 20.6 %all-to-all-start.2 = ((bf16[16,32,128]{2,1,0:T(8,128)(2,1)}), bf16[16,32,128]{2,1,0:T(8,128)(2,1)S(1)}, u32[]{:S(2)}, u32[]{:S(2)}) async-start(bf16[16,32,128]{2,1,0:T(8,128)(2,1)} %broadcast_in_dim.62), calls=%async_computation.2 | async-start | bytes 262144 | tf_op jit(solution)/shard_map/all_to_all | solution.py:50
  70.6 20.8 %collective-permute-start.2 = (bf16[128,4096]{1,0:T(8,128)(2,1)S(1)}, bf16[128,4096]{1,0:T(8,128)(2,1)S(1)}, u32[]{:S(2)}, u32[]{:S(2)}) collective-permute-start(bf16[128,4096]{1,0:T(8,128)(2,1)S(1)} %copy-done.4), channel_id=1, source_target_pairs={{0,2},{2,4},{4,6},{6,8},{8,10},{10,12},{12,14},{14,16},{16,18},{18... | collective-permute-start | bytes 3145736 | tf_op jit(solution)/shard_map/ppermute | solution.py:45
  85.0 20.8 %collective-permute-start.3 = (bf16[128,4096]{1,0:T(8,128)(2,1)}, bf16[128,4096]{1,0:T(8,128)(2,1)S(1)}, u32[]{:S(2)}, u32[]{:S(2)}) collective-permute-start(bf16[128,4096]{1,0:T(8,128)(2,1)} %mix.1.here), channel_id=1, source_target_pairs={{0,2},{2,4},{4,6},{6,8},{8,10},{10,12},{12,14},{14,16},{16,18},{18... | collective-permute-start | bytes 3145736 | tf_op jit(solution)/shard_map/ppermute | solution.py:45
  91.4 1.0 copy-start.5
  105.8 1.0 copy-start

commit v2 on v1

v2 whole, which is shorter than its diff:
```python
import jax
import jax.numpy as jnp
import numpy as np
from jax import lax
from jax.experimental import pallas as pl
from jax.experimental.pallas import tpu as pltpu
from jax.sharding import Mesh
from jax.sharding import PartitionSpec as P

D = 8192
HEAD_DIM = 128
BLOCK = 128
SEQ = ("seq_0", "seq_1", "seq_2", "seq_3")
NEAR = ("seq_2", "seq_3")
FAR = ("seq_0", "seq_1")
F32 = jnp.float32
BF16 = jnp.bfloat16
SUB = 256
VMEM = 8 * 2**20


def dft_matrices():
    n = 2 * BLOCK
    k = np.arange(BLOCK, dtype=np.float64)[:, None]
    t = np.arange(n, dtype=np.float64)[None, :]
    angle = np.pi * (2 * k + 1) * t / n
    forward = np.concatenate([np.cos(angle), -np.sin(angle)], axis=0)
    back = np.concatenate([np.cos(angle), -np.sin(angle)], axis=0).T[BLOCK:] * (2.0 / n)
    return forward.astype(np.float32), back.astype(np.float32)


FORWARD, BACK = dft_matrices()


def split(value):
    high = value.astype(BF16)
    return high, (value - high.astype(F32)).astype(BF16)


def dot(a, b):
    return jnp.dot(a, b, preferred_element_type=F32)


def shifted(block, axis, distance):
    size = lax.axis_size(axis)
    return lax.ppermute(block, axis, [(i, i + distance) for i in range(size) if 0 <= i + distance < size])


def copies(array, axis):
    sent = jnp.broadcast_to(array, (lax.axis_size(axis), *array.shape))
    return lax.all_to_all(sent, axis, split_axis=0, concat_axis=0, tiled=True)


def call(body, outs, name, scratch=(), scalars=0, operands=0, flops=10**8):
    specs = [pl.BlockSpec(memory_space=pltpu.SMEM)] * scalars
    specs += [pl.BlockSpec(memory_space=pltpu.VMEM)] * operands
    return pl.pallas_call(
        body,
        in_specs=specs,
        out_specs=[pl.BlockSpec(memory_space=pltpu.VMEM)] * len(outs),
        out_shape=[jax.ShapeDtypeStruct(shape, kind) for shape, kind in outs],
        scratch_shapes=list(scratch),
        compiler_params=pltpu.CompilerParams(vmem_limit_bytes=VMEM),
        cost_estimate=pl.CostEstimate(flops=flops, transcendentals=0, bytes_accessed=10**6),
        name=name,
    )


def pieces_of(width, sub=SUB):
    return [slice(j * sub, (j + 1) * sub) for j in range(width // sub)]


def times(width):
    return lax.broadcasted_iota(jnp.int32, (BLOCK, width), 0).astype(F32)


def gate_body(stream, inner, gain, v, squares, acc):
    step = pl.program_id(0)
    x = stream[...].astype(F32)
    v[...] = (inner[...].astype(F32) * x * gain[...]).astype(BF16)
    sq = x * x
    part = sq[:, :128]
    for j in range(1, x.shape[1] // 128):
        part = part + sq[:, j * 128 : (j + 1) * 128]

    @pl.when(step == 0)
    def _():
        acc[...] = part

    @pl.when(step > 0)
    def _():
        acc[...] = acc[...] + part

    @pl.when(step == pl.num_programs(0) - 1)
    def _():
        squares[...] = jnp.sum(acc[...].T, axis=0, keepdims=True)


def gated(stream, inner, gain, tile=512):
    rows, width = stream.shape
    wide = pl.BlockSpec((rows, tile), lambda i: (0, i))
    return pl.pallas_call(
        gate_body,
        grid=(width // tile,),
        in_specs=[wide, wide, pl.BlockSpec((1, tile), lambda i: (0, i))],
        out_specs=[wide, pl.BlockSpec((1, rows), lambda i: (0, 0))],
        out_shape=[
            jax.ShapeDtypeStruct((rows, width), BF16),
            jax.ShapeDtypeStruct((1, rows), F32),
        ],
        scratch_shapes=[pltpu.VMEM((rows, 128), F32)],
        compiler_params=pltpu.CompilerParams(vmem_limit_bytes=VMEM),
        name="gated",
    )(stream, inner, gain)


def tables_body(forward, taps, inner, short_outer, long_outer, decay, scale, spectrum, gate, outer):
    f_hi, f_lo = split(forward[:, :BLOCK])
    for at in pieces_of(taps.shape[1]):
        d = decay[:, at]
        spectrum[:, at] = dot(f_hi, taps[:, at]) + dot(f_lo, taps[:, at])
        time = times(SUB)
        gate[:, at] = inner[:, at].astype(F32) * short_outer[:, at].astype(F32) * jnp.exp(d * time)
        outer[:, at] = long_outer[:, at].astype(F32) * scale[:, at] * jnp.exp(-d * time)


def conv_body(
    before, here, factor, forward, back, lower, spectrum, gate, decay, total, copied, rows32
):
    fr = (forward[...] * factor[...]).astype(BF16)
    b = back[...].astype(BF16)
    for j, at in enumerate(pieces_of(here.shape[1])):
        x = dot(fr, jnp.concatenate([before[:, at], here[:, at]], axis=0))
        h = spectrum[:, at]
        x_re, x_im = x[:BLOCK], x[BLOCK:]
        h_re, h_im = h[:BLOCK], h[BLOCK:]
        y_re = (x_re * h_re - x_im * h_im).astype(BF16)
        y_im = (x_re * h_im + x_im * h_re).astype(BF16)
        conv = dot(b, jnp.concatenate([y_re, y_im], axis=0))
        result = dot(lower[...], (gate[:, at] * conv).astype(BF16))
        total[:, at] = result
        last = result[BLOCK - 1 :] * jnp.exp(decay[:, at] * (1.0 - BLOCK))
        for k in range(SUB // 128):
            row = j * (SUB // 128) + k
            rows32[row : row + 1, :] = last[:, k * 128 : (k + 1) * 128]
    state = rows32[...].astype(BF16)
    for k in range(copied.shape[0]):
        copied[k] = state


def weighted(pieces, place, rate):
    out = jnp.zeros(rate.shape, F32)
    for k in range(pieces.shape[0]):
        gap = place - 1 - k
        weight = jnp.exp(-rate * jnp.maximum(gap, 0).astype(F32))
        out = out + jnp.where(gap >= 0, weight * pieces[k].astype(F32), 0.0)
    return out


def near_body(place, pieces, rate, inside, copied):
    size = pieces.shape[0]
    inside[...] = weighted(pieces, place[0], rate[...])
    group = weighted(pieces, jnp.int32(size), rate[...]).astype(BF16)
    for k in range(copied.shape[0]):
        copied[k] = group


def finish_body(place, others, inside, rate, near_size, total, outer, decay, weights, mixed, ahead):
    near, far = place[0], place[1]
    r = rate[...]
    carry = inside[...] + jnp.exp(-r * near.astype(F32)) * weighted(
        others, far, r * near_size[0].astype(F32)
    )
    for j in range(total.shape[1] // HEAD_DIM):
        at = slice(j * HEAD_DIM, (j + 1) * HEAD_DIM)
        entering = carry[j : j + 1] * jnp.exp(-decay[:, at])
        value = (outer[:, at] * (total[:, at] + entering)).astype(BF16)
        mixed[:, at] = value
        ahead[:, at] = dot(weights[j], value).astype(BF16)


def score(query, key):
    return lax.dot_general(
        query, key, (((1,), (1,)), ((), ())), preferred_element_type=F32
    ) * HEAD_DIM ** (-0.5)


def soft(scores):
    top = jnp.max(scores, axis=1, keepdims=True)
    e = jnp.exp(scores - top)
    return e, top, jnp.sum(e, axis=1, keepdims=True)


def own_body(query, key, weights, stats):
    row = lax.broadcasted_iota(jnp.int32, (BLOCK, BLOCK), 0)
    lane = lax.broadcasted_iota(jnp.int32, (BLOCK, BLOCK), 1)
    kept = jnp.zeros((BLOCK, BLOCK), F32)
    heads = weights.shape[0]
    for j in range(heads):
        at = slice(j * HEAD_DIM, (j + 1) * HEAD_DIM)
        e, top, size = soft(jnp.where(lane <= row, score(query[:, at], key[:, at]), -1e30))
        weights[j] = e.astype(BF16)
        kept = jnp.where(lane == j, top, jnp.where(lane == heads + j, size, kept))
    stats[...] = kept


def ahead_body(query, key, weights, stats):
    lane = lax.broadcasted_iota(jnp.int32, (BLOCK, BLOCK), 1)
    kept = jnp.zeros((BLOCK, BLOCK), F32)
    heads = weights.shape[0]
    for j in range(heads):
        at = slice(j * HEAD_DIM, (j + 1) * HEAD_DIM)
        e, top, size = soft(score(query[:, at], key[:, at]))
        weights[j] = (e * (1.0 / size)).astype(BF16)
        kept = jnp.where(lane == j, top, jnp.where(lane == heads + j, size, kept))
    stats[...] = kept


def here_body(weights, mixed, here, before, partial, share):
    heads = weights.shape[0]
    lane = lax.broadcasted_iota(jnp.int32, (BLOCK, BLOCK), 1)
    kept = jnp.zeros((BLOCK, BLOCK), F32)
    for j in range(heads):
        at = slice(j * HEAD_DIM, (j + 1) * HEAD_DIM)
        top, size = here[:, j : j + 1], here[:, heads + j : heads + j + 1]
        top_b, size_b = before[:, j : j + 1], before[:, heads + j : heads + j + 1]
        top_b = jnp.where(size_b > 0.0, top_b, -1e30)
        highest = jnp.maximum(top, top_b)
        scale = jnp.exp(top - highest)
        scale_b = size_b * jnp.exp(top_b - highest)
        whole = 1.0 / (size * scale + scale_b)
        partial[:, at] = dot(weights[j], mixed[:, at]) * (scale * whole)
        kept = jnp.where(lane == j, scale_b * whole, kept)
    share[...] = kept


def join_body(partial, share, before, attended):
    for j in range(partial.shape[1] // HEAD_DIM):
        at = slice(j * HEAD_DIM, (j + 1) * HEAD_DIM)
        attended[:, at] = (
            partial[:, at] + share[:, j : j + 1] * before[:, at].astype(F32)
        ).astype(BF16)


def on_device(
    stream,
    norm_gain,
    short_outer,
    short_inner,
    short_filter,
    long_outer,
    long_inner,
    long_decay,
    query_heads,
    key_heads,
):
    rows, width = stream.shape
    heads, lanes = width // HEAD_DIM, width // 128
    decay = long_decay[None]
    scale = jnp.sqrt(-jnp.expm1(-2.0 * decay))
    rate = long_decay.reshape(lanes, 128) * rows
    near, far = lax.axis_index(NEAR), lax.axis_index(FAR)
    near_size, far_size = lax.axis_size(NEAR), lax.axis_size(FAR)
    forward, back = jnp.asarray(FORWARD), jnp.asarray(BACK)
    lower = jnp.asarray(np.tril(np.ones((rows, rows), np.float32)), BF16)
    square = ((rows, rows), F32)
    wide, wide_float = ((rows, width), BF16), ((rows, width), F32)

    query_next = shifted(query_heads, SEQ, -1)
    v, squares = gated(stream, short_inner, norm_gain[None])
    v_before = shifted(v, SEQ, 1)
    totals = jnp.sum(copies(squares, "mp"), axis=0)
    totals_before = shifted(totals, SEQ, 1)
    factor = 1.0 / jnp.sqrt(jnp.concatenate([totals_before, totals], axis=1) / D + 0.5)
    spectrum, gate, outer = call(
        tables_body,
        [((2 * rows, width), F32), wide_float, wide_float],
        "tables",
        operands=7,
    )(forward, short_filter, long_inner, short_outer, long_outer, decay, scale)
    total, state = call(
        conv_body,
        [wide_float, ((near_size, lanes, 128), BF16)],
        "conv",
        scratch=[pltpu.VMEM((lanes, 128), F32)],
        operands=9,
    )(v_before, v, factor, forward, back, lower, spectrum, gate, decay)
    pieces = lax.all_to_all(state, NEAR, 0, 0, tiled=True)
    inside, group = call(
        near_body,
        [((lanes, 128), F32), ((far_size, lanes, 128), BF16)],
        "near",
        scalars=1,
        operands=2,
    )(near[None], pieces, rate)
    others = lax.all_to_all(group, FAR, 0, 0, tiled=True)
    weights_here, stats_here = call(
        own_body, [((heads, rows, rows), BF16), square], "own", operands=2
    )(query_heads, key_heads)
    weights_next, stats_next = call(
        ahead_body, [((heads, rows, rows), BF16), square], "ahead", operands=2
    )(query_next, key_heads)
    stats_before = shifted(stats_next, SEQ, 1)
    weights_next, stats_before = lax.optimization_barrier((weights_next, stats_before))

    def finish(place, others, inside, rate, total, outer, decay, weights, mixed, ahead):
        finish_body(
            place, others, inside, rate, [jnp.int32(near_size)], total, outer, decay, weights, mixed, ahead
        )

    mixed, sent = call(finish, [wide, wide], "finish", scalars=1, operands=7)(
        jnp.stack([near, far]), others, inside, rate, total, outer, decay, weights_next
    )
    arrived = shifted(sent, SEQ, 1)
    partial, share = call(here_body, [wide_float, square], "here", operands=4)(
        weights_here, mixed, stats_here, stats_before
    )
    (attended,) = call(join_body, [wide], "join", operands=3)(partial, share, arrived)
    return (mixed, attended)


def solution(mesh):
    finer = Mesh(
        mesh.devices.reshape(8, 2, 4, 2, mesh.shape["mp"]),
        ("seq_0", "seq_1", "seq_2", "seq_3", "mp"),
    )
    placed = (
        P(SEQ, "mp"),
        P("mp"),
        P(SEQ, "mp"),
        P(SEQ, "mp"),
        P(None, "mp"),
        P(SEQ, "mp"),
        P(SEQ, "mp"),
        P("mp"),
        P(SEQ, "mp"),
        P(SEQ, "mp"),
    )
    return jax.shard_map(
        on_device,
        mesh=finer,
        in_specs=placed,
        out_specs=(P(SEQ, "mp"), P(SEQ, "mp")),
        check_vma=False,
    )
```

time: 112 us -> 111 us (level)
  the two profiles are of different devices: /device:TPU:34 before, /device:TPU:128 now
where the time goes in v2:
time: 111 us; the launch traced here: 110 us
  starting transfers between devices  35.9 us (32%)
  Pallas kernels  31.6 us (28%)
  waiting for transfers between devices  28.8 us (26%)
  local copies, waits for them, and re-layouts  12.7 us (11%)
    ppermute x5, waiting for transfers between devices, shifted(): lax.ppermute(block, axis, [(i, i + distance) for i in range(size) if 0 <=...  19.5 us
    ppermute x5, starting transfers between devices, shifted(): lax.ppermute(block, axis, [(i, i + distance) for i in range(size) if 0 <=...  17.3 us
    unnamed x36, local copies, waits for them, and re-layouts  12.1 us
    pallas_call x1, Pallas kernels, on_device(): call(here_body, [wide_float, square], 'here', operands=4)  10.4 us
    all_to_all x1, starting transfers between devices, on_device(): pieces = lax.all_to_all(state, NEAR, 0, 0, tiled=True)  7.75 us
    all_to_all x1, starting transfers between devices, on_device(): others = lax.all_to_all(group, FAR, 0, 0, tiled=True)  7.65 us
    all_to_all x1, waiting for transfers between devices, on_device(): pieces = lax.all_to_all(state, NEAR, 0, 0, tiled=True)  5.62 us
    pallas_call x1, Pallas kernels, on_device(): call(conv_body, [wide_float, ((near_size, lanes, 128), BF16)], 'conv', sc...  5.62 us
  transfers between devices with their start and end apart: 8, of which 5 were waited for; matrix products, arithmetic and copies ran while one was open for 1% of the time, Pallas kernels for 22%

profile of v2, /device:TPU:128, one launch (start us, length us, event | category | flops | bytes accessed | tf_op | source)
XLA Modules:
  0.0 110.0 jit_solution(15881282361497072094)
XLA Ops:
  0.6 0.0 copy-start.7
  0.6 0.0 copy-start.3
  0.7 0.0 copy-start.8
  0.7 1.3 %copy-done.8 = bf16[128,4096]{1,0:T(8,128)(2,1)S(1)} copy-done((bf16[128,4096]{1,0:T(8,128)(2,1)S(1)}, bf16[128,4096]{1,0:T(8,128)(2,1)}, u32[]{:S(2)}) %copy-start.8) | copy-done | bytes 1048600
  2.0 0.0 copy-start.9
  2.0 1.2 %copy-done.9 = bf16[128,4096]{1,0:T(8,128)(2,1)S(1)} copy-done((bf16[128,4096]{1,0:T(8,128)(2,1)S(1)}, bf16[128,4096]{1,0:T(8,128)(2,1)}, u32[]{:S(2)}) %copy-start.9) | copy-done | bytes 1048600
  3.2 0.0 copy-start.17
  3.2 0.7 copy-done.17
  3.9 0.0 copy-start.14
  3.9 3.2 %gated.1 = (bf16[128,4096]{1,0:T(8,128)(2,1)}, f32[1,128]{1,0:T(1,128)S(1)}) custom-call(bf16[128,4096]{1,0:T(8,128)(2,1)S(1)} %copy-done.8, bf16[128,4096]{1,0:T(8,128)(2,1)S(1)} %copy-done.9, f32[1,4096]{1,0:T(1,128)S(1)} %bitcast.14), custom_call_target="tpu_custom_call" | custom-call | tf_op jit(solution)/shard_map/gated/pallas_call | solution.py:102
  7.1 1.9 %collective-permute-start = (bf16[128,4096]{1,0:T(8,128)(2,1)}, bf16[128,4096]{1,0:T(8,128)(2,1)}, u32[]{:S(2)}, u32[]{:S(2)}) collective-permute-start(bf16[128,4096]{1,0:T(8,128)(2,1)} %get-tuple-element.21.here), channel_id=1, source_target_pairs={{0,2},{2,4},{4,6},{6,8},{8,10},{10,12},{12,14},{14,16},{16,18},{18... | collective-permute-start | bytes 3145736 | tf_op jit(solution)/shard_map/ppermute | solution.py:46
  9.0 9.4 %collective-permute-start.2 = (bf16[128,4096]{1,0:T(8,128)(2,1)}, bf16[128,4096]{1,0:T(8,128)(2,1)}, u32[]{:S(2)}, u32[]{:S(2)}) collective-permute-start(bf16[128,4096]{1,0:T(8,128)(2,1)} %query.1), channel_id=1, source_target_pairs={{2,0},{4,2},{6,4},{8,6},{10,8},{12,10},{14,12},{16,14},{18,16},{20... | collective-permute-start | bytes 3145736 | tf_op jit(solution)/shard_map/ppermute | solution.py:46
  18.4 0.6 broadcast_in_dim.11
  19.0 3.2 %all-to-all-start = ((f32[2,1,128]{2,1,0:T(1,128)}), f32[2,1,128]{2,1,0:T(1,128)S(1)}, u32[]{:S(2)}, u32[]{:S(2)}) async-start(f32[2,1,128]{2,1,0:T(1,128)} %broadcast_in_dim.11), calls=%async_computation | async-start | bytes 2048 | tf_op jit(solution)/shard_map/all_to_all | solution.py:51
  22.2 0.0 copy-done.14
  22.2 3.7 %all-to-all-done = f32[2,1,128]{2,1,0:T(1,128)S(1)} async-done(((f32[2,1,128]{2,1,0:T(1,128)}), f32[2,1,128]{2,1,0:T(1,128)S(1)}, u32[]{:S(2)}, u32[]{:S(2)}) %all-to-all-start) | async-done | bytes 1056 | tf_op jit(solution)/shard_map/all_to_all | solution.py:51
  25.9 1.9 %collective-permute-start.1 = (f32[1,128]{1,0:T(1,128)S(1)}, f32[1,128]{1,0:T(1,128)S(1)}, u32[]{:S(2)}, u32[]{:S(2)}) collective-permute-start(f32[1,128]{1,0:T(1,128)S(1)} %bitcast.17), channel_id=1, source_target_pairs={{0,2},{2,4},{4,6},{6,8},{8,10},{10,12},{12,14},{14,16},{16,18},{18... | collective-permute-start | bytes 1544 | tf_op jit(solution)/shard_map/ppermute | solution.py:46
  27.9 0.0 copy-done.7
  27.9 0.0 copy-done.3
  27.9 0.0 copy-start.4
  27.9 1.2 %copy-done.4 = bf16[128,4096]{1,0:T(8,128)(2,1)S(1)} copy-done((bf16[128,4096]{1,0:T(8,128)(2,1)S(1)}, bf16[128,4096]{1,0:T(8,128)(2,1)}, u32[]{:S(2)}) %copy-start.4) | copy-done | bytes 1048600
  29.1 0.0 copy-start.5
  29.1 1.2 %copy-done.5 = bf16[128,4096]{1,0:T(8,128)(2,1)S(1)} copy-done((bf16[128,4096]{1,0:T(8,128)(2,1)S(1)}, bf16[128,4096]{1,0:T(8,128)(2,1)}, u32[]{:S(2)}) %copy-start.5) | copy-done | bytes 1048600
  30.3 0.0 copy-start.6
  30.3 1.2 %copy-done.6 = bf16[128,4096]{1,0:T(8,128)(2,1)S(1)} copy-done((bf16[128,4096]{1,0:T(8,128)(2,1)S(1)}, bf16[128,4096]{1,0:T(8,128)(2,1)}, u32[]{:S(2)}) %copy-start.6) | copy-done | bytes 1048600
  31.6 0.0 copy-start.15
  31.6 0.0 copy-start.16
  31.6 1.5 %tables.1 = (f32[256,4096]{1,0:T(8,128)S(1)}, f32[128,4096]{1,0:T(8,128)S(1)}, f32[128,4096]{1,0:T(8,128)S(1)}) custom-call(f32[256,256]{1,0:T(8,128)S(1)} %copy-done.7, bf16[128,4096]{1,0:T(8,128)(2,1)S(1)} %copy-done.3, bf16[128,4096]{1,0:T(8,128)(2,1)S(1)} %copy-done.4, bf16[128,4096]{1,0:T(8,128)(2,1)S(1)} %copy-done.5, bf16[128,4096]{1,0:T(8,128)(2,1)S(1)} %copy-done.6, ...), custom_call_target="tpu_custom_call" | custom-call | flops 100000000 | bytes 1000000 | tf_op jit(solution)/shard_map/tables/pallas_call | solution.py:275
  33.0 3.5 %collective-permute-done.1 = f32[1,128]{1,0:T(1,128)S(1)} collective-permute-done((f32[1,128]{1,0:T(1,128)S(1)}, f32[1,128]{1,0:T(1,128)S(1)}, u32[]{:S(2)}, u32[]{:S(2)}) %collective-permute-start.1) | collective-permute-done | bytes 544 | tf_op jit(solution)/shard_map/ppermute | solution.py:46
  36.6 0.0 collective-permute-done.before
  36.6 0.0 copy-done.15
  36.6 0.0 copy-done.16
  36.6 0.0 copy-start
  36.6 5.6 %conv.1 = (f32[128,4096]{1,0:T(8,128)S(1)}, bf16[8,32,128]{2,1,0:T(8,128)(2,1)}) custom-call(bf16[128,4096]{1,0:T(8,128)(2,1)} %collective-permute-done.before, bf16[128,4096]{1,0:T(8,128)(2,1)} %get-tuple-element.21.here, f32[1,256]{1,0:T(1,128)S(1)} %fusion.1.factor, f32[256,256]{1,0:T(8,128)S(1)} %copy-done.7, f32[128,256]{1,0:T(8,128)S(1)} %copy-done.15, ...), custom_call_target="tpu_custom_call" | custom-call | flops 100000000 | bytes 1000000 | tf_op jit(solution)/shard_map/conv/pallas_call | solution.py:281
  42.2 0.0 copy-start.1
  42.2 1.3 %copy-done.1 = f32[128,4096]{1,0:T(8,128)} copy-done((f32[128,4096]{1,0:T(8,128)}, f32[128,4096]{1,0:T(8,128)S(1)}, u32[]{:S(2)}) %copy-start.1) | copy-done | bytes 2097176
  43.6 7.7 %all-to-all-start.1 = ((bf16[8,32,128]{2,1,0:T(8,128)(2,1)}), bf16[8,32,128]{2,1,0:T(8,128)(2,1)S(1)}, u32[]{:S(2)}, u32[]{:S(2)}) async-start(bf16[8,32,128]{2,1,0:T(8,128)(2,1)} %get-tuple-element.25), calls=%async_computation.1 | async-start | bytes 131072 | tf_op jit(solution)/shard_map/all_to_all | solution.py:288
  51.3 5.6 %all-to-all-done.1.pieces = bf16[8,32,128]{2,1,0:T(8,128)(2,1)S(1)} async-done(((bf16[8,32,128]{2,1,0:T(8,128)(2,1)}), bf16[8,32,128]{2,1,0:T(8,128)(2,1)S(1)}, u32[]{:S(2)}, u32[]{:S(2)}) %all-to-all-start.1) | async-done | bytes 65568 | tf_op jit(solution)/shard_map/all_to_all | solution.py:288
  56.9 0.7 near.1
  57.6 7.7 %all-to-all-start.2 = ((bf16[16,32,128]{2,1,0:T(8,128)(2,1)}), bf16[16,32,128]{2,1,0:T(8,128)(2,1)S(1)}, u32[]{:S(2)}, u32[]{:S(2)}) async-start(bf16[16,32,128]{2,1,0:T(8,128)(2,1)} %get-tuple-element.26), calls=%async_computation.2 | async-start | bytes 262144 | tf_op jit(solution)/shard_map/all_to_all | solution.py:296
  65.3 0.0 collective-permute-done.2.query
  65.3 0.0 copy-done
  65.3 3.9 %ahead.1 = (bf16[32,128,128]{2,1,0:T(8,128)(2,1)S(1)}, f32[128,128]{1,0:T(8,128)S(1)}) custom-call(bf16[128,4096]{1,0:T(8,128)(2,1)} %collective-permute-done.2.query, bf16[128,4096]{1,0:T(8,128)(2,1)S(1)} %copy-done), custom_call_target="tpu_custom_call" | custom-call | flops 100000000 | bytes 1000000 | tf_op jit(solution)/shard_map/ahead/pallas_call | solution.py:300
  69.2 0.0 copy-start.12
  69.2 1.0 copy-done.12
  70.1 1.9 %collective-permute-start.3 = (f32[128,128]{1,0:T(8,128)S(1)}, f32[128,128]{1,0:T(8,128)S(1)}, u32[]{:S(2)}, u32[]{:S(2)}) collective-permute-start(f32[128,128]{1,0:T(8,128)S(1)} %get-tuple-element.31), channel_id=1, source_target_pairs={{0,2},{2,4},{4,6},{6,8},{8,10},{10,12},{12,14},{14,16},{16,18},{18... | collective-permute-start | bytes 196616 | tf_op jit(solution)/shard_map/ppermute | solution.py:46
  72.0 0.1 pad_add_fusion.place
  72.1 9.3 %collective-permute-done.3.before = f32[128,128]{1,0:T(8,128)S(1)} collective-permute-done((f32[128,128]{1,0:T(8,128)S(1)}, f32[128,128]{1,0:T(8,128)S(1)}, u32[]{:S(2)}, u32[]{:S(2)}) %collective-permute-start.3) | collective-permute-done | bytes 65568 | tf_op jit(solution)/shard_map/ppermute | solution.py:46
  81.4 0.0 all-to-all-done.2.others
  81.4 0.0 copy-start.2
  81.4 1.6 %copy-done.2 = f32[128,4096]{1,0:T(8,128)S(1)} copy-done((f32[128,4096]{1,0:T(8,128)S(1)}, f32[128,4096]{1,0:T(8,128)}, u32[]{:S(2)}) %copy-start.2) | copy-done | bytes 2097176
  83.0 0.0 copy-start.13
  83.0 1.2 %copy-done.13 = bf16[32,128,128]{2,1,0:T(8,128)(2,1)S(1)} copy-done((bf16[32,128,128]{2,1,0:T(8,128)(2,1)S(1)}, bf16[32,128,128]{2,1,0:T(8,128)(2,1)}, u32[]{:S(2)}) %copy-start.13) | copy-done | bytes 1048600
  84.2 0.0 copy-start.10
  84.3 2.1 %finish.1 = (bf16[128,4096]{1,0:T(8,128)(2,1)}, bf16[128,4096]{1,0:T(8,128)(2,1)S(1)}) custom-call(s32[2]{0:T(128)S(1)} %pad_add_fusion.place, bf16[16,32,128]{2,1,0:T(8,128)(2,1)S(1)} %all-to-all-done.2.others, f32[32,128]{1,0:T(8,128)S(1)} %get-tuple-element.27.inside, f32[32,128]{1,0:T(8,128)S(1)} %get-tuple-element.40.rate, f32[128,4096]{1,0:T(8,128)S(1)} %copy-done.2, ...), custom_call_target="tpu_custom_call" | custom-call | flops 100000000 | bytes 1000000 | tf_op jit(solution)/shard_map/finish/pallas_call | solution.py:311
  86.4 0.0 copy-start.11
  86.4 2.2 %collective-permute-start.4 = (bf16[128,4096]{1,0:T(8,128)(2,1)S(1)}, bf16[128,4096]{1,0:T(8,128)(2,1)S(1)}, u32[]{:S(2)}, u32[]{:S(2)}) collective-permute-start(bf16[128,4096]{1,0:T(8,128)(2,1)S(1)} %get-tuple-element.39), channel_id=1, source_target_pairs={{0,2},{2,4},{4,6},{6,8},{8,10},{10,12},{12,14},{14,16},{16,18},{18... | collective-permute-start | bytes 3145736 | tf_op jit(solution)/shard_map/ppermute | solution.py:46
  88.6 0.0 copy-done.10
  88.6 2.7 %own.1 = (bf16[32,128,128]{2,1,0:T(8,128)(2,1)S(1)}, f32[128,128]{1,0:T(8,128)S(1)}) custom-call(bf16[128,4096]{1,0:T(8,128)(2,1)S(1)} %copy-done.10, bf16[128,4096]{1,0:T(8,128)(2,1)S(1)} %copy-done), custom_call_target="tpu_custom_call" | custom-call | flops 100000000 | bytes 1000000 | tf_op jit(solution)/shard_map/own/pallas_call | solution.py:297
  91.3 0.0 copy-done.11
  91.3 10.4 %here.1 = (f32[128,4096]{1,0:T(8,128)S(1)}, f32[128,128]{1,0:T(8,128)S(1)}) custom-call(bf16[32,128,128]{2,1,0:T(8,128)(2,1)S(1)} %get-tuple-element.34.weights, bf16[128,4096]{1,0:T(8,128)(2,1)S(1)} %copy-done.11, f32[128,128]{1,0:T(8,128)S(1)} %get-tuple-element.35.here, f32[128,128]{1,0:T(8,128)S(1)} %collective-permute-done.3.before), custom_call_target="tpu_custom_call" | custom-call | flops 100000000 | bytes 1000000 | tf_op jit(solution)/shard_map/here/pallas_call | solution.py:315
  101.7 6.6 %collective-permute-done.4.before = bf16[128,4096]{1,0:T(8,128)(2,1)S(1)} collective-permute-done((bf16[128,4096]{1,0:T(8,128)(2,1)S(1)}, bf16[128,4096]{1,0:T(8,128)(2,1)S(1)}, u32[]{:S(2)}, u32[]{:S(2)}) %collective-permute-start.4) | collective-permute-done | bytes 1048608 | tf_op jit(solution)/shard_map/ppermute | solution.py:46
  108.3 1.6 %join.1 = bf16[128,4096]{1,0:T(8,128)(2,1)} custom-call(f32[128,4096]{1,0:T(8,128)S(1)} %get-tuple-element.37.partial, f32[128,128]{1,0:T(8,128)S(1)} %get-tuple-element.38.share, bf16[128,4096]{1,0:T(8,128)(2,1)S(1)} %collective-permute-done.4.before), custom_call_target="tpu_custom_call" | custom-call | flops 100000000 | bytes 1000000 | tf_op jit(solution)/shard_map/join/pallas_call | solution.py:318
  (3 shorter events, 0.1 us)
Async XLA Ops:
  0.6 27.2 %copy-start.7 = (f32[256,256]{1,0:T(8,128)S(1)}, f32[256,256]{1,0:T(8,128)}, u32[]{:S(2)}) copy-start(f32[256,256]{1,0:T(8,128)} %constant.39.clone.forward) | copy-start | bytes 786436
  0.6 27.2 %copy-start.3 = (bf16[128,4096]{1,0:T(8,128)(2,1)S(1)}, bf16[128,4096]{1,0:T(8,128)(2,1)}, u32[]{:S(2)}) copy-start(bf16[128,4096]{1,0:T(8,128)(2,1)} %taps.1) | copy-start | bytes 3145732
  0.7 1.3 %copy-start.8 = (bf16[128,4096]{1,0:T(8,128)(2,1)S(1)}, bf16[128,4096]{1,0:T(8,128)(2,1)}, u32[]{:S(2)}) copy-start(bf16[128,4096]{1,0:T(8,128)(2,1)} %stream.1) | copy-start | bytes 3145732
  2.0 1.2 %copy-start.9 = (bf16[128,4096]{1,0:T(8,128)(2,1)S(1)}, bf16[128,4096]{1,0:T(8,128)(2,1)}, u32[]{:S(2)}) copy-start(bf16[128,4096]{1,0:T(8,128)(2,1)} %inner.2) | copy-start | bytes 3145732
  3.2 0.7 copy-start.17
  3.9 18.3 %copy-start.14 = (f32[4096]{0:T(1024)S(1)}, f32[4096]{0:T(1024)}, u32[]{:S(2)}) copy-start(f32[4096]{0:T(1024)} %param.20) | copy-start | bytes 49156
  7.1 29.4 %collective-permute-start = (bf16[128,4096]{1,0:T(8,128)(2,1)}, bf16[128,4096]{1,0:T(8,128)(2,1)}, u32[]{:S(2)}, u32[]{:S(2)}) collective-permute-start(bf16[128,4096]{1,0:T(8,128)(2,1)} %get-tuple-element.21.here), channel_id=1, source_target_pairs={{0,2},{2,4},{4,6},{6,8},{8,10},{10,12},{12,14},{14,16},{16,18},{18... | collective-permute-start | bytes 3145736 | tf_op jit(solution)/shard_map/ppermute | solution.py:46
  9.0 56.2 %collective-permute-start.2 = (bf16[128,4096]{1,0:T(8,128)(2,1)}, bf16[128,4096]{1,0:T(8,128)(2,1)}, u32[]{:S(2)}, u32[]{:S(2)}) collective-permute-start(bf16[128,4096]{1,0:T(8,128)(2,1)} %query.1), channel_id=1, source_target_pairs={{2,0},{4,2},{6,4},{8,6},{10,8},{12,10},{14,12},{16,14},{18,16},{20... | collective-permute-start | bytes 3145736 | tf_op jit(solution)/shard_map/ppermute | solution.py:46
  19.0 6.9 %all-to-all-start = ((f32[2,1,128]{2,1,0:T(1,128)}), f32[2,1,128]{2,1,0:T(1,128)S(1)}, u32[]{:S(2)}, u32[]{:S(2)}) async-start(f32[2,1,128]{2,1,0:T(1,128)} %broadcast_in_dim.11), calls=%async_computation | async-start | bytes 2048 | tf_op jit(solution)/shard_map/all_to_all | solution.py:51
  25.9 10.6 %collective-permute-start.1 = (f32[1,128]{1,0:T(1,128)S(1)}, f32[1,128]{1,0:T(1,128)S(1)}, u32[]{:S(2)}, u32[]{:S(2)}) collective-permute-start(f32[1,128]{1,0:T(1,128)S(1)} %bitcast.17), channel_id=1, source_target_pairs={{0,2},{2,4},{4,6},{6,8},{8,10},{10,12},{12,14},{14,16},{16,18},{18... | collective-permute-start | bytes 1544 | tf_op jit(solution)/shard_map/ppermute | solution.py:46
  27.9 1.2 %copy-start.4 = (bf16[128,4096]{1,0:T(8,128)(2,1)S(1)}, bf16[128,4096]{1,0:T(8,128)(2,1)}, u32[]{:S(2)}) copy-start(bf16[128,4096]{1,0:T(8,128)(2,1)} %inner.3) | copy-start | bytes 3145732
  29.1 1.2 %copy-start.5 = (bf16[128,4096]{1,0:T(8,128)(2,1)S(1)}, bf16[128,4096]{1,0:T(8,128)(2,1)}, u32[]{:S(2)}) copy-start(bf16[128,4096]{1,0:T(8,128)(2,1)} %short_outer.1) | copy-start | bytes 3145732
  30.3 1.2 %copy-start.6 = (bf16[128,4096]{1,0:T(8,128)(2,1)S(1)}, bf16[128,4096]{1,0:T(8,128)(2,1)}, u32[]{:S(2)}) copy-start(bf16[128,4096]{1,0:T(8,128)(2,1)} %long_outer.1) | copy-start | bytes 3145732
  31.6 5.0 %copy-start.15 = (f32[128,256]{1,0:T(8,128)S(1)}, f32[128,256]{1,0:T(8,128)}, u32[]{:S(2)}) copy-start(f32[128,256]{1,0:T(8,128)} %constant.40.clone.back) | copy-start | bytes 393220
  31.6 5.0 %copy-start.16 = (bf16[128,128]{1,0:T(8,128)(2,1)S(1)}, bf16[128,128]{1,0:T(8,128)(2,1)}, u32[]{:S(2)}) copy-start(bf16[128,128]{1,0:T(8,128)(2,1)} %constant.41.clone.lower) | copy-start | bytes 98308
  36.6 28.7 %copy-start = (bf16[128,4096]{1,0:T(8,128)(2,1)S(1)}, bf16[128,4096]{1,0:T(8,128)(2,1)}, u32[]{:S(2)}) copy-start(bf16[128,4096]{1,0:T(8,128)(2,1)} %key.3) | copy-start | bytes 3145732
  42.2 1.3 %copy-start.1 = (f32[128,4096]{1,0:T(8,128)}, f32[128,4096]{1,0:T(8,128)S(1)}, u32[]{:S(2)}) copy-start(f32[128,4096]{1,0:T(8,128)S(1)} %get-tuple-element.28.total) | copy-start | bytes 6291460
  43.6 13.4 %all-to-all-start.1 = ((bf16[8,32,128]{2,1,0:T(8,128)(2,1)}), bf16[8,32,128]{2,1,0:T(8,128)(2,1)S(1)}, u32[]{:S(2)}, u32[]{:S(2)}) async-start(bf16[8,32,128]{2,1,0:T(8,128)(2,1)} %get-tuple-element.25), calls=%async_computation.1 | async-start | bytes 131072 | tf_op jit(solution)/shard_map/all_to_all | solution.py:288
  57.6 23.8 %all-to-all-start.2 = ((bf16[16,32,128]{2,1,0:T(8,128)(2,1)}), bf16[16,32,128]{2,1,0:T(8,128)(2,1)S(1)}, u32[]{:S(2)}, u32[]{:S(2)}) async-start(bf16[16,32,128]{2,1,0:T(8,128)(2,1)} %get-tuple-element.26), calls=%async_computation.2 | async-start | bytes 262144 | tf_op jit(solution)/shard_map/all_to_all | solution.py:296
  69.2 1.0 copy-start.12
  70.1 11.3 %collective-permute-start.3 = (f32[128,128]{1,0:T(8,128)S(1)}, f32[128,128]{1,0:T(8,128)S(1)}, u32[]{:S(2)}, u32[]{:S(2)}) collective-permute-start(f32[128,128]{1,0:T(8,128)S(1)} %get-tuple-element.31), channel_id=1, source_target_pairs={{0,2},{2,4},{4,6},{6,8},{8,10},{10,12},{12,14},{14,16},{16,18},{18... | collective-permute-start | bytes 196616 | tf_op jit(solution)/shard_map/ppermute | solution.py:46
  81.4 1.6 %copy-start.2 = (f32[128,4096]{1,0:T(8,128)S(1)}, f32[128,4096]{1,0:T(8,128)}, u32[]{:S(2)}) copy-start(f32[128,4096]{1,0:T(8,128)} %copy-done.1) | copy-start | bytes 6291460
  83.0 1.2 %copy-start.13 = (bf16[32,128,128]{2,1,0:T(8,128)(2,1)S(1)}, bf16[32,128,128]{2,1,0:T(8,128)(2,1)}, u32[]{:S(2)}) copy-start(bf16[32,128,128]{2,1,0:T(8,128)(2,1)} %copy-done.12) | copy-start | bytes 3145732
  84.2 4.4 %copy-start.10 = (bf16[128,4096]{1,0:T(8,128)(2,1)S(1)}, bf16[128,4096]{1,0:T(8,128)(2,1)}, u32[]{:S(2)}) copy-start(bf16[128,4096]{1,0:T(8,128)(2,1)} %query.1) | copy-start | bytes 3145732
  86.4 4.9 %copy-start.11 = (bf16[128,4096]{1,0:T(8,128)(2,1)S(1)}, bf16[128,4096]{1,0:T(8,128)(2,1)}, u32[]{:S(2)}) copy-start(bf16[128,4096]{1,0:T(8,128)(2,1)} %get-tuple-element.19.mixed) | copy-start | bytes 3145732
  86.4 22.0 %collective-permute-start.4 = (bf16[128,4096]{1,0:T(8,128)(2,1)S(1)}, bf16[128,4096]{1,0:T(8,128)(2,1)S(1)}, u32[]{:S(2)}, u32[]{:S(2)}) collective-permute-start(bf16[128,4096]{1,0:T(8,128)(2,1)S(1)} %get-tuple-element.39), channel_id=1, source_target_pairs={{0,2},{2,4},{4,6},{6,8},{8,10},{10,12},{12,14},{14,16},{16,18},{18... | collective-permute-start | bytes 3145736 | tf_op jit(solution)/shard_map/ppermute | solution.py:46

commit v3 on v2

v3 whole, which is shorter than its diff:
```python
import functools

import jax
import jax.numpy as jnp
import numpy as np
from jax import lax
from jax.experimental import pallas as pl
from jax.experimental.pallas import tpu as pltpu
from jax.sharding import Mesh
from jax.sharding import PartitionSpec as P

D = 8192
HEAD_DIM = 128
BLOCK = 128
SEQ = ("seq_0", "seq_1", "seq_2", "seq_3")
NEAR = ("seq_2", "seq_3")
FAR = ("seq_0", "seq_1")
F32 = jnp.float32
BF16 = jnp.bfloat16
SUB = 256
VMEM = 8 * 2**20


def dft_matrices():
    n = 2 * BLOCK
    k = np.arange(BLOCK, dtype=np.float64)[:, None]
    t = np.arange(n, dtype=np.float64)[None, :]
    angle = np.pi * (2 * k + 1) * t / n
    forward = np.concatenate([np.cos(angle), -np.sin(angle)], axis=0)
    back = np.concatenate([np.cos(angle), -np.sin(angle)], axis=0).T[BLOCK:] * (2.0 / n)
    return forward.astype(np.float32), back.astype(np.float32)


FORWARD, BACK = dft_matrices()


def split(value):
    high = value.astype(BF16)
    return high, (value - high.astype(F32)).astype(BF16)


def dot(a, b):
    return jnp.dot(a, b, preferred_element_type=F32)


def shifted(block, axis, distance):
    size = lax.axis_size(axis)
    return lax.ppermute(block, axis, [(i, i + distance) for i in range(size) if 0 <= i + distance < size])


def swapped(block):
    sides = lax.axis_size("mp")
    return lax.ppermute(block, "mp", [(m, sides - 1 - m) for m in range(sides)])


def call(body, outs, name, scratch=(), scalars=0, operands=0, flops=10**8):
    specs = [pl.BlockSpec(memory_space=pltpu.SMEM)] * scalars
    specs += [pl.BlockSpec(memory_space=pltpu.VMEM)] * operands
    return pl.pallas_call(
        body,
        in_specs=specs,
        out_specs=[pl.BlockSpec(memory_space=pltpu.VMEM)] * len(outs),
        out_shape=[jax.ShapeDtypeStruct(shape, kind) for shape, kind in outs],
        scratch_shapes=list(scratch),
        compiler_params=pltpu.CompilerParams(vmem_limit_bytes=VMEM),
        cost_estimate=pl.CostEstimate(flops=flops, transcendentals=0, bytes_accessed=10**6),
        name=name,
    )


def pieces_of(width, sub=SUB):
    return [slice(j * sub, (j + 1) * sub) for j in range(width // sub)]


def times(width):
    return lax.broadcasted_iota(jnp.int32, (BLOCK, width), 0).astype(F32)


def squares_body(stream, squares):
    acc = jnp.zeros((stream.shape[0], 128), F32)
    for at in pieces_of(stream.shape[1], 128):
        x = stream[:, at].astype(F32)
        acc = acc + x * x
    squares[...] = jnp.sum(acc.T, axis=0, keepdims=True)


def gate_body(stream, inner, gain, v, sent):
    for at in pieces_of(stream.shape[1], 128):
        value = inner[:, at].astype(F32) * stream[:, at].astype(F32) * gain[:, at]
        v[:, at] = value.astype(BF16)
        sent[:, at] = value.astype(BF16)


def label_body(squares, beside, sent, total, out):
    value = squares[...] + beside[...]
    total[...] = value
    first = lax.broadcasted_iota(jnp.int32, (16, 128), 0) == 0
    for k in range(3):
        col = slice(k * 128, (k + 1) * 128)
        term = value.astype(BF16).astype(F32)
        value = value - term
        out[:, col] = jnp.where(first, term, sent[:, col].astype(F32)).astype(BF16)


def label(squares, beside, sent):
    rows, width = sent.shape
    part = pl.BlockSpec((16, 3 * 128), lambda i: (0, 0))
    row = pl.BlockSpec((1, rows), lambda i: (0, 0))
    return pl.pallas_call(
        label_body,
        grid=(1,),
        in_specs=[row, row, part],
        out_specs=[row, part],
        out_shape=[jax.ShapeDtypeStruct((1, rows), F32), jax.ShapeDtypeStruct((rows, width), BF16)],
        input_output_aliases={2: 1},
        compiler_params=pltpu.CompilerParams(vmem_limit_bytes=VMEM),
        name="label",
    )(squares, beside, sent)


def tables_body(forward, taps, inner, short_outer, decay, spectrum, gate):
    f_hi, f_lo = split(forward[:, :BLOCK])
    for at in pieces_of(taps.shape[1]):
        d = decay[:, at]
        spectrum[:, at] = dot(f_hi, taps[:, at]) + dot(f_lo, taps[:, at])
        time = times(SUB)
        gate[:, at] = inner[:, at].astype(F32) * short_outer[:, at].astype(F32) * jnp.exp(d * time)


def conv_body(
    before,
    here,
    squares,
    forward,
    back,
    lower,
    spectrum,
    gate,
    decay,
    summed,
    copied,
    rows32,
):
    carried = before[:16, : 3 * 128].astype(F32)
    earlier = (carried[:1, :128] + carried[:1, 128:256]) + carried[:1, 256:]
    sums = jnp.concatenate([earlier, squares[...]], axis=1)
    column = lax.broadcasted_iota(jnp.int32, (1, 2 * BLOCK), 1)
    factor = jnp.where(column == 0, 0.0, 1.0 / jnp.sqrt(sums / D + 0.5))
    fr = (forward[...] * factor).astype(BF16)
    b = back[...].astype(BF16)
    for j, at in enumerate(pieces_of(here.shape[1])):
        x = dot(fr, jnp.concatenate([before[:, at], here[:, at]], axis=0))
        h = spectrum[:, at]
        x_re, x_im = x[:BLOCK], x[BLOCK:]
        h_re, h_im = h[:BLOCK], h[BLOCK:]
        y_re = (x_re * h_re - x_im * h_im).astype(BF16)
        y_im = (x_re * h_im + x_im * h_re).astype(BF16)
        conv = dot(b, jnp.concatenate([y_re, y_im], axis=0))
        z = (gate[:, at] * conv).astype(BF16)
        summed[:, at] = z
        result = dot(lower[...], z)
        last = result[BLOCK - 1 :] * jnp.exp(decay[:, at] * (1.0 - BLOCK))
        for k in range(SUB // 128):
            row = j * (SUB // 128) + k
            rows32[row : row + 1, :] = last[:, k * 128 : (k + 1) * 128]
    state = rows32[...].astype(BF16)
    for k in range(copied.shape[0]):
        copied[k] = state


def weighted(pieces, place, rate):
    out = jnp.zeros(rate.shape, F32)
    for k in range(pieces.shape[0]):
        gap = place - 1 - k
        weight = jnp.exp(-rate * jnp.maximum(gap, 0).astype(F32))
        out = out + jnp.where(gap >= 0, weight * pieces[k].astype(F32), 0.0)
    return out


def near_body(place, pieces, rate, inside, copied):
    size = pieces.shape[0]
    inside[...] = weighted(pieces, place[0], rate[...])
    group = weighted(pieces, jnp.int32(size), rate[...]).astype(BF16)
    for k in range(copied.shape[0]):
        copied[k] = group


def finish_body(near_size, place, others, inside, rate, summed, lower, long_outer, decay, scale, weights, mixed, ahead):
    near, far = place[0], place[1]
    r = rate[...]
    carry = inside[...] + jnp.exp(-r * near.astype(F32)) * weighted(others, far, r * near_size)
    time = times(HEAD_DIM)
    for j in range(summed.shape[1] // HEAD_DIM):
        at = slice(j * HEAD_DIM, (j + 1) * HEAD_DIM)
        d = decay[:, at]
        entering = carry[j : j + 1] * jnp.exp(-d)
        outer = long_outer[:, at].astype(F32) * (jnp.exp(-d * time) * scale[:, at])
        value = (outer * (dot(lower[...], summed[:, at]) + entering)).astype(BF16)
        mixed[:, at] = value
        ahead[:, at] = dot(weights[j], value).astype(BF16)


def score(query, key):
    return lax.dot_general(
        query, key, (((1,), (1,)), ((), ())), preferred_element_type=F32
    ) * HEAD_DIM ** (-0.5)


def soft(scores):
    top = jnp.max(scores, axis=1, keepdims=True)
    e = jnp.exp(scores - top)
    return e, top, jnp.sum(e, axis=1, keepdims=True)


def own_body(query, key, weights, stats):
    row = lax.broadcasted_iota(jnp.int32, (BLOCK, BLOCK), 0)
    lane = lax.broadcasted_iota(jnp.int32, (BLOCK, BLOCK), 1)
    tops = jnp.zeros((BLOCK, BLOCK), F32)
    sizes = jnp.zeros((BLOCK, BLOCK), F32)
    for j in range(weights.shape[0]):
        at = slice(j * HEAD_DIM, (j + 1) * HEAD_DIM)
        e, top, size = soft(jnp.where(lane <= row, score(query[:, at], key[:, at]), -1e30))
        weights[j] = e.astype(BF16)
        tops = jnp.where(lane == j, top, tops)
        sizes = jnp.where(lane == j + BLOCK // 2, size, sizes)
    stats[...] = jnp.where(lane < BLOCK // 2, tops, sizes)


def ahead_body(query, key, weights, stats):
    lane = lax.broadcasted_iota(jnp.int32, (BLOCK, BLOCK), 1)
    tops = jnp.zeros((BLOCK, BLOCK), F32)
    sizes = jnp.zeros((BLOCK, BLOCK), F32)
    for j in range(weights.shape[0]):
        at = slice(j * HEAD_DIM, (j + 1) * HEAD_DIM)
        e, top, size = soft(score(query[:, at], key[:, at]))
        weights[j] = (e * (1.0 / size)).astype(BF16)
        tops = jnp.where(lane == j, top, tops)
        sizes = jnp.where(lane == j + BLOCK // 2, size, sizes)
    stats[...] = jnp.where(lane < BLOCK // 2, tops, sizes)


def here_body(weights, mixed, here, before, partial, share):
    top, size = here[...], pltpu.roll(here[...], BLOCK // 2, 1)
    size_b = pltpu.roll(before[...], BLOCK // 2, 1)
    top_b = jnp.where(size_b > 0.0, before[...], -1e30)
    highest = jnp.maximum(top, top_b)
    scale = jnp.exp(top - highest)
    scale_b = size_b * jnp.exp(top_b - highest)
    whole = 1.0 / (size * scale + scale_b)
    own = scale * whole
    share[...] = scale_b * whole
    for j in range(weights.shape[0]):
        at = slice(j * HEAD_DIM, (j + 1) * HEAD_DIM)
        partial[:, at] = dot(weights[j], mixed[:, at]) * own[:, j : j + 1]


def join_body(partial, share, before, attended):
    for j in range(partial.shape[1] // HEAD_DIM):
        at = slice(j * HEAD_DIM, (j + 1) * HEAD_DIM)
        attended[:, at] = (
            partial[:, at] + share[:, j : j + 1] * before[:, at].astype(F32)
        ).astype(BF16)


def on_device(
    stream,
    norm_gain,
    short_outer,
    short_inner,
    short_filter,
    long_outer,
    long_inner,
    long_decay,
    query_heads,
    key_heads,
):
    rows, width = stream.shape
    heads, lanes = width // HEAD_DIM, width // 128
    decay = long_decay[None]
    scale = jnp.sqrt(-jnp.expm1(-2.0 * decay))
    rate = long_decay.reshape(lanes, 128) * rows
    near, far = lax.axis_index(NEAR), lax.axis_index(FAR)
    near_size, far_size = lax.axis_size(NEAR), lax.axis_size(FAR)
    forward, back = jnp.asarray(FORWARD), jnp.asarray(BACK)
    lower = jnp.asarray(np.tril(np.ones((rows, rows), np.float32)), BF16)
    square = ((rows, rows), F32)
    wide, wide_float = ((rows, width), BF16), ((rows, width), F32)

    (squares,) = call(squares_body, [((1, rows), F32)], "squares", operands=1)(stream)
    beside = swapped(squares)
    v, sent = call(gate_body, [wide, wide], "gate", operands=3)(stream, short_inner, norm_gain[None])
    total, sent = label(squares, beside, sent)
    v_before = shifted(sent, SEQ, 1)
    queries, total = lax.optimization_barrier((query_heads, total))
    query_next = shifted(queries, SEQ, -1)
    spectrum, gate = call(
        tables_body, [((2 * rows, width), F32), wide_float], "tables", operands=5
    )(forward, short_filter, long_inner, short_outer, decay)
    weights_here, stats_here = call(
        own_body, [((heads, rows, rows), BF16), square], "own", operands=2
    )(query_heads, key_heads)
    v_before, stats_here = lax.optimization_barrier((v_before, stats_here))
    summed, state = call(
        conv_body,
        [wide, ((near_size, lanes, 128), BF16)],
        "conv",
        scratch=[pltpu.VMEM((lanes, 128), F32)],
        operands=9,
    )(v_before, v, total, forward, back, lower, spectrum, gate, decay)
    pieces = lax.all_to_all(state, NEAR, 0, 0, tiled=True)
    weights_next, stats_next = call(
        ahead_body, [((heads, rows, rows), BF16), square], "ahead", operands=2
    )(query_next, key_heads)
    pieces, stats_next = lax.optimization_barrier((pieces, stats_next))
    stats_before = shifted(stats_next, SEQ, 1)
    inside, group = call(
        near_body,
        [((lanes, 128), F32), ((far_size, lanes, 128), BF16)],
        "near",
        scalars=1,
        operands=2,
    )(near[None], pieces, rate)
    others = lax.all_to_all(group, FAR, 0, 0, tiled=True)
    others, stats_before = lax.optimization_barrier((others, stats_before))
    mixed, sent = call(
        functools.partial(finish_body, float(near_size)), [wide, wide], "finish", scalars=1, operands=9
    )(
        jnp.stack([near, far]),
        others,
        inside,
        rate,
        summed,
        lower,
        long_outer,
        decay,
        scale,
        weights_next,
    )
    arrived = shifted(sent, SEQ, 1)
    partial, share = call(here_body, [wide_float, square], "here", operands=4)(
        weights_here, mixed, stats_here, stats_before
    )
    (attended,) = call(join_body, [wide], "join", operands=3)(partial, share, arrived)
    return (mixed, attended)


def solution(mesh):
    finer = Mesh(
        mesh.devices.reshape(8, 2, 4, 2, mesh.shape["mp"]),
        ("seq_0", "seq_1", "seq_2", "seq_3", "mp"),
    )
    placed = (
        P(SEQ, "mp"),
        P("mp"),
        P(SEQ, "mp"),
        P(SEQ, "mp"),
        P(None, "mp"),
        P(SEQ, "mp"),
        P(SEQ, "mp"),
        P("mp"),
        P(SEQ, "mp"),
        P(SEQ, "mp"),
    )
    return jax.shard_map(
        on_device,
        mesh=finer,
        in_specs=placed,
        out_specs=(P(SEQ, "mp"), P(SEQ, "mp")),
        check_vma=False,
    )
```

time: 111 us -> 89.6 us (0.81)
  Pallas kernels: 31.6 us -> 18.1 us
  starting transfers between devices: 35.9 us -> 27.7 us
  waiting for transfers between devices: 28.8 us -> 33 us
  local copies, waits for them, and re-layouts: 12.7 us -> 9.18 us
    ppermute x5 -> x4, waiting for transfers between devices: 19.5 us -> 33 us  [shifted(): lax.ppermute(block, axis, [(i, i + distance) for i in range(size) if 0 <=...]
    pallas_call x1, Pallas kernels: 10.4 us -> 0.8 us  [on_device(): call(here_body, [wide_float, square], 'here', operands=4)]
    all_to_all x1, waiting for transfers between devices: 5.62 us -> 0.01 us  [on_device(): pieces = lax.all_to_all(state, NEAR, 0, 0, tiled=True)]
    all_to_all x1, starting transfers between devices: 7.75 us -> 3.48 us  [on_device(): pieces = lax.all_to_all(state, NEAR, 0, 0, tiled=True)]
    pallas_call x4 -> x6, Pallas kernels: 12.4 us -> 8.6 us  [the longest x1 4 us: on_device(): call(conv_body, [wide, ((near_size, lanes, 128), BF16)], 'conv', scratch=...]
    all_to_all x1 -> x0, waiting for transfers between devices: 3.7 us -> none  [copies(): return lax.all_to_all(sent, axis, split_axis=0, concat_axis=0, tiled=True)]
    all_to_all x1 -> x0, starting transfers between devices: 3.19 us -> none  [copies(): return lax.all_to_all(sent, axis, split_axis=0, concat_axis=0, tiled=True)]
    unnamed x36 -> x42, local copies, waits for them, and re-layouts: 12.1 us -> 9.18 us
  transfers between devices with their start and end apart: 8 -> 7, of which waited for: 5 -> 3; matrix products, arithmetic and copies ran while one was open for 1% -> 0% of each run, Pallas kernels for 22% -> 15%
where the time goes in v3:
time: 89.6 us; the launch traced here: 89 us
  waiting for transfers between devices  33 us (37%)
  starting transfers between devices  27.7 us (31%)
  Pallas kernels  18.1 us (20%)
  local copies, waits for them, and re-layouts  9.18 us (10%)
    ppermute x4, waiting for transfers between devices, shifted(): lax.ppermute(block, axis, [(i, i + distance) for i in range(size) if 0 <=...  33 us
    ppermute x4, starting transfers between devices, shifted(): lax.ppermute(block, axis, [(i, i + distance) for i in range(size) if 0 <=...  15.4 us
    unnamed x42, local copies, waits for them, and re-layouts  9.18 us
    all_to_all x1, starting transfers between devices, on_device(): others = lax.all_to_all(group, FAR, 0, 0, tiled=True)  7.3 us
    pallas_call x1, Pallas kernels, on_device(): call(conv_body, [wide, ((near_size, lanes, 128), BF16)], 'conv', scratch=...  4 us
    pallas_call x1, Pallas kernels, on_device(): call(ahead_body, [((heads, rows, rows), BF16), square], 'ahead', operands=2)  3.87 us
    all_to_all x1, starting transfers between devices, on_device(): pieces = lax.all_to_all(state, NEAR, 0, 0, tiled=True)  3.48 us
    pallas_call x1, Pallas kernels, on_device(): call(functools.partial(finish_body, float(near_size)), [wide, wide], 'fin...  2.58 us
  transfers between devices with their start and end apart: 7, of which 3 were waited for; matrix products, arithmetic and copies ran while one was open for 0% of the time, Pallas kernels for 15%

profile of v3, /device:TPU:128, one launch (start us, length us, event | category | flops | bytes accessed | tf_op | source)
XLA Modules:
  0.0 89.0 jit_solution(12119083404436183704)
XLA Ops:
  0.6 0.0 copy-start
  0.6 1.2 %copy-done = bf16[128,4096]{1,0:T(8,128)(2,1)S(1)} copy-done((bf16[128,4096]{1,0:T(8,128)(2,1)S(1)}, bf16[128,4096]{1,0:T(8,128)(2,1)}, u32[]{:S(2)}) %copy-start) | copy-done | bytes 1048600
  1.9 0.0 copy-start.1
  1.9 0.3 squares.1
  2.2 1.6 %collective-permute-start = (f32[1,128]{1,0:T(1,128)S(1)}, f32[1,128]{1,0:T(1,128)S(1)}, u32[]{:S(2)}, u32[]{:S(2)}) collective-permute-start(f32[1,128]{1,0:T(1,128)S(1)} %squares.1), channel_id=1, source_target_pairs={{0,1},{1,0},{2,3},{3,2},{4,5},{5,4},{6,7},{7,6},{8,9},{9,8},{10,11... | collective-permute-start | bytes 1544 | tf_op jit(solution)/shard_map/ppermute | solution.py:53
  3.7 0.0 copy-start.2
  3.7 1.2 %copy-done.2 = bf16[128,4096]{1,0:T(8,128)(2,1)S(1)} copy-done((bf16[128,4096]{1,0:T(8,128)(2,1)S(1)}, bf16[128,4096]{1,0:T(8,128)(2,1)}, u32[]{:S(2)}) %copy-start.2) | copy-done | bytes 1048600
  5.0 0.0 copy-start.19
  5.0 0.7 copy-done.19
  5.7 0.0 copy-start.6
  5.7 0.0 copy-start.15
  5.7 0.0 copy-start.16
  5.7 0.4 gate.1
  6.0 0.0 copy-start.3
  6.0 0.0 copy-start.4
  6.1 0.0 copy-start.5
  6.1 0.0 collective-permute-done.beside
  6.1 2.2 %collective-permute-start.1 = (bf16[128,4096]{1,0:T(8,128)(2,1)S(1)}, bf16[128,4096]{1,0:T(8,128)(2,1)S(1)}, u32[]{:S(2)}, u32[]{:S(2)}) collective-permute-start(bf16[128,4096]{1,0:T(8,128)(2,1)S(1)} %get-tuple-element.29), channel_id=1, source_target_pairs={{0,2},{2,4},{4,6},{6,8},{8,10},{10,12},{12,14},{14,16},{16,18},{18... | collective-permute-start | bytes 3145736 | tf_op jit(solution)/shard_map/ppermute | solution.py:48
  8.3 0.0 copy-done.6
  8.3 9.4 %collective-permute-start.2 = (bf16[128,4096]{1,0:T(8,128)(2,1)S(1)}, bf16[128,4096]{1,0:T(8,128)(2,1)}, u32[]{:S(2)}, u32[]{:S(2)}) collective-permute-start(bf16[128,4096]{1,0:T(8,128)(2,1)S(1)} %copy-done.6), channel_id=1, source_target_pairs={{2,0},{4,2},{6,4},{8,6},{10,8},{12,10},{14,12},{16,14},{18,16},{20... | collective-permute-start | bytes 3145736 | tf_op jit(solution)/shard_map/ppermute | solution.py:48
  17.7 0.0 copy-done.1
  17.7 2.5 %own.1 = (bf16[32,128,128]{2,1,0:T(8,128)(2,1)S(1)}, f32[128,128]{1,0:T(8,128)S(1)}) custom-call(bf16[128,4096]{1,0:T(8,128)(2,1)S(1)} %copy-done.6, bf16[128,4096]{1,0:T(8,128)(2,1)S(1)} %copy-done.1), custom_call_target="tpu_custom_call" | custom-call | flops 100000000 | bytes 1000000 | tf_op jit(solution)/shard_map/own/pallas_call | solution.py:299
  20.3 0.0 copy-start.8
  20.3 1.0 %copy-done.8 = bf16[32,128,128]{2,1,0:T(8,128)(2,1)} copy-done((bf16[32,128,128]{2,1,0:T(8,128)(2,1)}, bf16[32,128,128]{2,1,0:T(8,128)(2,1)S(1)}, u32[]{:S(2)}) %copy-start.8) | copy-done | bytes 1048600
  21.2 0.0 copy-start.17
  21.2 0.0 copy-start.18
  21.2 0.0 copy-done.15
  21.2 0.0 copy-done.16
  21.2 0.0 copy-done.3
  21.3 0.0 copy-done.4
  21.3 0.0 copy-done.5
  21.3 1.3 %tables.1 = (f32[256,4096]{1,0:T(8,128)S(1)}, f32[128,4096]{1,0:T(8,128)S(1)}) custom-call(f32[256,256]{1,0:T(8,128)S(1)} %copy-done.15, bf16[128,4096]{1,0:T(8,128)(2,1)S(1)} %copy-done.3, bf16[128,4096]{1,0:T(8,128)(2,1)S(1)} %copy-done.4, bf16[128,4096]{1,0:T(8,128)(2,1)S(1)} %copy-done.5, f32[1,4096]{1,0:T(1,128)S(1)} %bitcast.7), custom_call_target="tpu_custom_call" | custom-call | flops 100000000 | bytes 1000000 | tf_op jit(solution)/shard_map/tables/pallas_call | solution.py:296
  22.6 5.6 %collective-permute-done.1.before = bf16[128,4096]{1,0:T(8,128)(2,1)S(1)} collective-permute-done((bf16[128,4096]{1,0:T(8,128)(2,1)S(1)}, bf16[128,4096]{1,0:T(8,128)(2,1)S(1)}, u32[]{:S(2)}, u32[]{:S(2)}) %collective-permute-start.1) | collective-permute-done | bytes 1048608 | tf_op jit(solution)/shard_map/ppermute | solution.py:48
  28.2 0.0 copy-done.17
  28.2 0.0 copy-done.18
  28.2 4.0 %conv.1 = (bf16[128,4096]{1,0:T(8,128)(2,1)S(1)}, bf16[8,32,128]{2,1,0:T(8,128)(2,1)}) custom-call(bf16[128,4096]{1,0:T(8,128)(2,1)S(1)} %collective-permute-done.1.before, bf16[128,4096]{1,0:T(8,128)(2,1)S(1)} %get-tuple-element.32.here, f32[1,128]{1,0:T(1,128)S(1)} %get-tuple-element.34.squares, f32[256,256]{1,0:T(8,128)S(1)} %copy-done.15, ...), custom_call_target="tpu_custom_call" | custom-call | flops 100000000 | bytes 1000000 | tf_op jit(solution)/shard_map/conv/pallas_call | solution.py:303
  32.2 0.0 copy-start.10
  32.2 1.0 %copy-done.10 = bf16[128,4096]{1,0:T(8,128)(2,1)} copy-done((bf16[128,4096]{1,0:T(8,128)(2,1)}, bf16[128,4096]{1,0:T(8,128)(2,1)S(1)}, u32[]{:S(2)}) %copy-start.10) | copy-done | bytes 1048600
  33.2 3.5 %all-to-all-start = ((bf16[8,32,128]{2,1,0:T(8,128)(2,1)}), bf16[8,32,128]{2,1,0:T(8,128)(2,1)S(1)}, u32[]{:S(2)}, u32[]{:S(2)}) async-start(bf16[8,32,128]{2,1,0:T(8,128)(2,1)} %get-tuple-element.37), calls=%async_computation | async-start | bytes 131072 | tf_op jit(solution)/shard_map/all_to_all | solution.py:310
  36.7 0.0 collective-permute-done.2.query
  36.7 0.0 copy-start.11
  36.7 3.9 %ahead.1 = (bf16[32,128,128]{2,1,0:T(8,128)(2,1)S(1)}, f32[128,128]{1,0:T(8,128)S(1)}) custom-call(bf16[128,4096]{1,0:T(8,128)(2,1)} %collective-permute-done.2.query, bf16[128,4096]{1,0:T(8,128)(2,1)S(1)} %copy-done.1), custom_call_target="tpu_custom_call" | custom-call | flops 100000000 | bytes 1000000 | tf_op jit(solution)/shard_map/ahead/pallas_call | solution.py:311
  40.6 0.0 copy-start.12
  40.6 1.0 %copy-done.12 = bf16[32,128,128]{2,1,0:T(8,128)(2,1)} copy-done((bf16[32,128,128]{2,1,0:T(8,128)(2,1)}, bf16[32,128,128]{2,1,0:T(8,128)(2,1)S(1)}, u32[]{:S(2)}) %copy-start.12) | copy-done | bytes 1048600
  41.6 0.6 copy-done.20
  42.2 0.0 all-to-all-done.pieces
  42.2 0.7 near.1
  42.9 7.3 %all-to-all-start.1 = ((bf16[16,32,128]{2,1,0:T(8,128)(2,1)}), bf16[16,32,128]{2,1,0:T(8,128)(2,1)S(1)}, u32[]{:S(2)}, u32[]{:S(2)}) async-start(bf16[16,32,128]{2,1,0:T(8,128)(2,1)} %get-tuple-element.41), calls=%async_computation.1 | async-start | bytes 262144 | tf_op jit(solution)/shard_map/all_to_all | solution.py:323
  50.2 1.9 %collective-permute-start.3 = (f32[128,128]{1,0:T(8,128)}, f32[128,128]{1,0:T(8,128)S(1)}, u32[]{:S(2)}, u32[]{:S(2)}) collective-permute-start(f32[128,128]{1,0:T(8,128)} %copy-done.20), channel_id=1, source_target_pairs={{0,2},{2,4},{4,6},{6,8},{8,10},{10,12},{12,14},{14,16},{16,18},{18... | collective-permute-start | bytes 196616 | tf_op jit(solution)/shard_map/ppermute | solution.py:48
  52.1 0.1 pad_add_fusion.place
  52.2 9.5 %collective-permute-done.3.before = f32[128,128]{1,0:T(8,128)S(1)} collective-permute-done((f32[128,128]{1,0:T(8,128)}, f32[128,128]{1,0:T(8,128)S(1)}, u32[]{:S(2)}, u32[]{:S(2)}) %collective-permute-start.3) | collective-permute-done | bytes 65568 | tf_op jit(solution)/shard_map/ppermute | solution.py:48
  61.7 0.0 all-to-all-done.1.others
  61.7 0.0 copy-done.7
  61.7 0.0 copy-done.11
  61.7 0.0 copy-start.13
  61.7 1.2 %copy-done.13 = bf16[32,128,128]{2,1,0:T(8,128)(2,1)S(1)} copy-done((bf16[32,128,128]{2,1,0:T(8,128)(2,1)S(1)}, bf16[32,128,128]{2,1,0:T(8,128)(2,1)}, u32[]{:S(2)}) %copy-start.13) | copy-done | bytes 1048600
  63.0 2.6 %finish.1 = (bf16[128,4096]{1,0:T(8,128)(2,1)}, bf16[128,4096]{1,0:T(8,128)(2,1)S(1)}) custom-call(s32[2]{0:T(128)S(1)} %pad_add_fusion.place, bf16[16,32,128]{2,1,0:T(8,128)(2,1)S(1)} %all-to-all-done.1.others, f32[32,128]{1,0:T(8,128)S(1)} %get-tuple-element.44.inside, f32[32,128]{1,0:T(8,128)S(1)} %get-tuple-element.55.rate, ...), custom_call_target="tpu_custom_call" | custom-call | flops 100000000 | bytes 1000000 | tf_op jit(solution)/shard_map/finish/pallas_call | solution.py:325
  65.5 1.9 %collective-permute-start.4 = (bf16[128,4096]{1,0:T(8,128)(2,1)S(1)}, bf16[128,4096]{1,0:T(8,128)(2,1)S(1)}, u32[]{:S(2)}, u32[]{:S(2)}) collective-permute-start(bf16[128,4096]{1,0:T(8,128)(2,1)S(1)} %get-tuple-element.53), channel_id=1, source_target_pairs={{0,2},{2,4},{4,6},{6,8},{8,10},{10,12},{12,14},{14,16},{16,18},{18... | collective-permute-start | bytes 3145736 | tf_op jit(solution)/shard_map/ppermute | solution.py:48
  67.5 0.0 copy-done.9
  67.5 0.0 copy-start.14
  67.5 1.2 %copy-done.14 = bf16[128,4096]{1,0:T(8,128)(2,1)S(1)} copy-done((bf16[128,4096]{1,0:T(8,128)(2,1)S(1)}, bf16[128,4096]{1,0:T(8,128)(2,1)}, u32[]{:S(2)}) %copy-start.14) | copy-done | bytes 1048600
  68.7 0.8 here.1
  69.5 17.9 %collective-permute-done.4.before = bf16[128,4096]{1,0:T(8,128)(2,1)S(1)} collective-permute-done((bf16[128,4096]{1,0:T(8,128)(2,1)S(1)}, bf16[128,4096]{1,0:T(8,128)(2,1)S(1)}, u32[]{:S(2)}, u32[]{:S(2)}) %collective-permute-start.4) | collective-permute-done | bytes 1048608 | tf_op jit(solution)/shard_map/ppermute | solution.py:48
  87.4 1.6 %join.1 = bf16[128,4096]{1,0:T(8,128)(2,1)} custom-call(f32[128,4096]{1,0:T(8,128)S(1)} %get-tuple-element.51.partial, f32[128,128]{1,0:T(8,128)S(1)} %get-tuple-element.52.share, bf16[128,4096]{1,0:T(8,128)(2,1)S(1)} %collective-permute-done.4.before), custom_call_target="tpu_custom_call" | custom-call | flops 100000000 | bytes 1000000 | tf_op jit(solution)/shard_map/join/pallas_call | solution.py:343
  (5 shorter events, 0.1 us)
Async XLA Ops:
  0.6 1.2 %copy-start = (bf16[128,4096]{1,0:T(8,128)(2,1)S(1)}, bf16[128,4096]{1,0:T(8,128)(2,1)}, u32[]{:S(2)}) copy-start(bf16[128,4096]{1,0:T(8,128)(2,1)} %stream.3) | copy-start | bytes 3145732
  1.9 15.8 %copy-start.1 = (bf16[128,4096]{1,0:T(8,128)(2,1)S(1)}, bf16[128,4096]{1,0:T(8,128)(2,1)}, u32[]{:S(2)}) copy-start(bf16[128,4096]{1,0:T(8,128)(2,1)} %key.3) | copy-start | bytes 3145732
  2.2 3.9 %collective-permute-start = (f32[1,128]{1,0:T(1,128)S(1)}, f32[1,128]{1,0:T(1,128)S(1)}, u32[]{:S(2)}, u32[]{:S(2)}) collective-permute-start(f32[1,128]{1,0:T(1,128)S(1)} %squares.1), channel_id=1, source_target_pairs={{0,1},{1,0},{2,3},{3,2},{4,5},{5,4},{6,7},{7,6},{8,9},{9,8},{10,11... | collective-permute-start | bytes 1544 | tf_op jit(solution)/shard_map/ppermute | solution.py:53
  3.7 1.2 %copy-start.2 = (bf16[128,4096]{1,0:T(8,128)(2,1)S(1)}, bf16[128,4096]{1,0:T(8,128)(2,1)}, u32[]{:S(2)}) copy-start(bf16[128,4096]{1,0:T(8,128)(2,1)} %inner.2) | copy-start | bytes 3145732
  5.0 0.7 copy-start.19
  5.7 2.6 %copy-start.6 = (bf16[128,4096]{1,0:T(8,128)(2,1)S(1)}, bf16[128,4096]{1,0:T(8,128)(2,1)}, u32[]{:S(2)}) copy-start(bf16[128,4096]{1,0:T(8,128)(2,1)} %query.1) | copy-start | bytes 3145732
  5.7 15.6 %copy-start.15 = (f32[256,256]{1,0:T(8,128)S(1)}, f32[256,256]{1,0:T(8,128)}, u32[]{:S(2)}) copy-start(f32[256,256]{1,0:T(8,128)} %constant.31.clone.forward) | copy-start | bytes 786436
  5.7 15.6 %copy-start.16 = (f32[4096]{0:T(1024)S(1)}, f32[4096]{0:T(1024)}, u32[]{:S(2)}) copy-start(f32[4096]{0:T(1024)} %param.20) | copy-start | bytes 49156
  6.0 15.2 %copy-start.3 = (bf16[128,4096]{1,0:T(8,128)(2,1)S(1)}, bf16[128,4096]{1,0:T(8,128)(2,1)}, u32[]{:S(2)}) copy-start(bf16[128,4096]{1,0:T(8,128)(2,1)} %taps.1) | copy-start | bytes 3145732
  6.0 15.2 %copy-start.4 = (bf16[128,4096]{1,0:T(8,128)(2,1)S(1)}, bf16[128,4096]{1,0:T(8,128)(2,1)}, u32[]{:S(2)}) copy-start(bf16[128,4096]{1,0:T(8,128)(2,1)} %inner.3) | copy-start | bytes 3145732
  6.1 15.2 %copy-start.5 = (bf16[128,4096]{1,0:T(8,128)(2,1)S(1)}, bf16[128,4096]{1,0:T(8,128)(2,1)}, u32[]{:S(2)}) copy-start(bf16[128,4096]{1,0:T(8,128)(2,1)} %short_outer.1) | copy-start | bytes 3145732
  6.1 22.1 %collective-permute-start.1 = (bf16[128,4096]{1,0:T(8,128)(2,1)S(1)}, bf16[128,4096]{1,0:T(8,128)(2,1)S(1)}, u32[]{:S(2)}, u32[]{:S(2)}) collective-permute-start(bf16[128,4096]{1,0:T(8,128)(2,1)S(1)} %get-tuple-element.29), channel_id=1, source_target_pairs={{0,2},{2,4},{4,6},{6,8},{8,10},{10,12},{12,14},{14,16},{16,18},{18... | collective-permute-start | bytes 3145736 | tf_op jit(solution)/shard_map/ppermute | solution.py:48
  8.3 28.4 %collective-permute-start.2 = (bf16[128,4096]{1,0:T(8,128)(2,1)S(1)}, bf16[128,4096]{1,0:T(8,128)(2,1)}, u32[]{:S(2)}, u32[]{:S(2)}) collective-permute-start(bf16[128,4096]{1,0:T(8,128)(2,1)S(1)} %copy-done.6), channel_id=1, source_target_pairs={{2,0},{4,2},{6,4},{8,6},{10,8},{12,10},{14,12},{16,14},{18,16},{20... | collective-permute-start | bytes 3145736 | tf_op jit(solution)/shard_map/ppermute | solution.py:48
  20.3 1.0 %copy-start.8 = (bf16[32,128,128]{2,1,0:T(8,128)(2,1)}, bf16[32,128,128]{2,1,0:T(8,128)(2,1)S(1)}, u32[]{:S(2)}) copy-start(bf16[32,128,128]{2,1,0:T(8,128)(2,1)S(1)} %get-tuple-element.48.weights) | copy-start | bytes 3145732
  21.2 7.0 %copy-start.17 = (f32[128,256]{1,0:T(8,128)S(1)}, f32[128,256]{1,0:T(8,128)}, u32[]{:S(2)}) copy-start(f32[128,256]{1,0:T(8,128)} %constant.32.clone.back) | copy-start | bytes 393220
  21.2 7.0 %copy-start.18 = (bf16[128,128]{1,0:T(8,128)(2,1)S(1)}, bf16[128,128]{1,0:T(8,128)(2,1)}, u32[]{:S(2)}) copy-start(bf16[128,128]{1,0:T(8,128)(2,1)} %constant.33.clone.lower) | copy-start | bytes 98308
  32.2 1.0 %copy-start.10 = (bf16[128,4096]{1,0:T(8,128)(2,1)}, bf16[128,4096]{1,0:T(8,128)(2,1)S(1)}, u32[]{:S(2)}) copy-start(bf16[128,4096]{1,0:T(8,128)(2,1)S(1)} %get-tuple-element.45.summed) | copy-start | bytes 3145732
  33.2 28.5 %copy-start.7 = (bf16[128,4096]{1,0:T(8,128)(2,1)S(1)}, bf16[128,4096]{1,0:T(8,128)(2,1)}, u32[]{:S(2)}) copy-start(bf16[128,4096]{1,0:T(8,128)(2,1)} %long_outer.1) | copy-start | bytes 3145732
  33.2 9.0 %all-to-all-start = ((bf16[8,32,128]{2,1,0:T(8,128)(2,1)}), bf16[8,32,128]{2,1,0:T(8,128)(2,1)S(1)}, u32[]{:S(2)}, u32[]{:S(2)}) async-start(bf16[8,32,128]{2,1,0:T(8,128)(2,1)} %get-tuple-element.37), calls=%async_computation | async-start | bytes 131072 | tf_op jit(solution)/shard_map/all_to_all | solution.py:310
  36.7 25.0 %copy-start.11 = (bf16[128,4096]{1,0:T(8,128)(2,1)S(1)}, bf16[128,4096]{1,0:T(8,128)(2,1)}, u32[]{:S(2)}) copy-start(bf16[128,4096]{1,0:T(8,128)(2,1)} %copy-done.10) | copy-start | bytes 3145732
  40.6 1.0 %copy-start.12 = (bf16[32,128,128]{2,1,0:T(8,128)(2,1)}, bf16[32,128,128]{2,1,0:T(8,128)(2,1)S(1)}, u32[]{:S(2)}) copy-start(bf16[32,128,128]{2,1,0:T(8,128)(2,1)S(1)} %get-tuple-element.46.weights) | copy-start | bytes 3145732
  41.6 0.6 copy-start.20
  42.2 25.3 %copy-start.9 = (bf16[32,128,128]{2,1,0:T(8,128)(2,1)S(1)}, bf16[32,128,128]{2,1,0:T(8,128)(2,1)}, u32[]{:S(2)}) copy-start(bf16[32,128,128]{2,1,0:T(8,128)(2,1)} %copy-done.8) | copy-start | bytes 3145732
  42.9 18.8 %all-to-all-start.1 = ((bf16[16,32,128]{2,1,0:T(8,128)(2,1)}), bf16[16,32,128]{2,1,0:T(8,128)(2,1)S(1)}, u32[]{:S(2)}, u32[]{:S(2)}) async-start(bf16[16,32,128]{2,1,0:T(8,128)(2,1)} %get-tuple-element.41), calls=%async_computation.1 | async-start | bytes 262144 | tf_op jit(solution)/shard_map/all_to_all | solution.py:323
  50.2 11.5 %collective-permute-start.3 = (f32[128,128]{1,0:T(8,128)}, f32[128,128]{1,0:T(8,128)S(1)}, u32[]{:S(2)}, u32[]{:S(2)}) collective-permute-start(f32[128,128]{1,0:T(8,128)} %copy-done.20), channel_id=1, source_target_pairs={{0,2},{2,4},{4,6},{6,8},{8,10},{10,12},{12,14},{14,16},{16,18},{18... | collective-permute-start | bytes 196616 | tf_op jit(solution)/shard_map/ppermute | solution.py:48
  61.7 1.2 %copy-start.13 = (bf16[32,128,128]{2,1,0:T(8,128)(2,1)S(1)}, bf16[32,128,128]{2,1,0:T(8,128)(2,1)}, u32[]{:S(2)}) copy-start(bf16[32,128,128]{2,1,0:T(8,128)(2,1)} %copy-done.12) | copy-start | bytes 3145732
  65.5 21.8 %collective-permute-start.4 = (bf16[128,4096]{1,0:T(8,128)(2,1)S(1)}, bf16[128,4096]{1,0:T(8,128)(2,1)S(1)}, u32[]{:S(2)}, u32[]{:S(2)}) collective-permute-start(bf16[128,4096]{1,0:T(8,128)(2,1)S(1)} %get-tuple-element.53), channel_id=1, source_target_pairs={{0,2},{2,4},{4,6},{6,8},{8,10},{10,12},{12,14},{14,16},{16,18},{18... | collective-permute-start | bytes 3145736 | tf_op jit(solution)/shard_map/ppermute | solution.py:48
  67.5 1.2 %copy-start.14 = (bf16[128,4096]{1,0:T(8,128)(2,1)S(1)}, bf16[128,4096]{1,0:T(8,128)(2,1)}, u32[]{:S(2)}) copy-start(bf16[128,4096]{1,0:T(8,128)(2,1)} %get-tuple-element.26.mixed) | copy-start | bytes 3145732

commit v4 on v3

v4 whole, which is shorter than its diff:
```python
import functools

import jax
import jax.numpy as jnp
import numpy as np
from jax import lax
from jax.experimental import pallas as pl
from jax.experimental.pallas import tpu as pltpu
from jax.sharding import Mesh
from jax.sharding import PartitionSpec as P

D = 8192
HEAD_DIM = 128
BLOCK = 128
SEQ = ("seq_0", "seq_1", "seq_2", "seq_3")
NEAR = ("seq_2", "seq_3")
FAR = ("seq_0", "seq_1")
F32 = jnp.float32
BF16 = jnp.bfloat16
SUB = 256
PARTS = 2
CHUNKS = 4
VMEM = 8 * 2**20


def dft_matrices():
    n = 2 * BLOCK
    k = np.arange(BLOCK, dtype=np.float64)[:, None]
    t = np.arange(n, dtype=np.float64)[None, :]
    angle = np.pi * (2 * k + 1) * t / n
    forward = np.concatenate([np.cos(angle), -np.sin(angle)], axis=0)
    back = np.concatenate([np.cos(angle), -np.sin(angle)], axis=0).T[BLOCK:] * (2.0 / n)
    return forward.astype(np.float32), back.astype(np.float32)


FORWARD, BACK = dft_matrices()


def split(value):
    high = value.astype(BF16)
    return high, (value - high.astype(F32)).astype(BF16)


def dot(a, b):
    return jnp.dot(a, b, preferred_element_type=F32)


def shifted(block, axis, distance):
    size = lax.axis_size(axis)
    return lax.ppermute(block, axis, [(i, i + distance) for i in range(size) if 0 <= i + distance < size])


def swapped(block):
    sides = lax.axis_size("mp")
    return lax.ppermute(block, "mp", [(m, sides - 1 - m) for m in range(sides)])


def call(body, outs, scratch=(), scalars=0, operands=0, flops=10**8, outside=(), kept=()):
    specs = [pl.BlockSpec(memory_space=pltpu.SMEM)] * scalars
    specs += [pl.BlockSpec(memory_space=pltpu.VMEM)] * operands
    for k in outside:
        specs[k] = pl.BlockSpec(memory_space=pltpu.HBM)
    return pl.pallas_call(
        body,
        in_specs=specs,
        out_specs=[
            pl.BlockSpec(memory_space=pltpu.HBM if k in kept else pltpu.VMEM)
            for k in range(len(outs))
        ],
        out_shape=[
            pltpu.HBM(shape, kind) if k in kept else jax.ShapeDtypeStruct(shape, kind)
            for k, (shape, kind) in enumerate(outs)
        ],
        scratch_shapes=list(scratch),
        compiler_params=pltpu.CompilerParams(vmem_limit_bytes=VMEM),
        cost_estimate=pl.CostEstimate(flops=flops, transcendentals=0, bytes_accessed=10**6),
    )


def in_hbm(array):
    return pltpu.with_memory_space_constraint(array, pltpu.HBM)


def pieces_of(width, sub=SUB):
    return [slice(j * sub, (j + 1) * sub) for j in range(width // sub)]


def times(width):
    return lax.broadcasted_iota(jnp.int32, (BLOCK, width), 0).astype(F32)


def squares_body(stream, squares):
    acc = jnp.zeros((stream.shape[0], 128), F32)
    for at in pieces_of(stream.shape[1], 128):
        x = stream[:, at].astype(F32)
        acc = acc + x * x
    squares[...] = jnp.sum(acc.T, axis=0, keepdims=True)


def gate_body(stream, inner, gain, v, *sent):
    share = stream.shape[1] // len(sent)
    for at in pieces_of(stream.shape[1], 128):
        value = inner[:, at].astype(F32) * stream[:, at].astype(F32) * gain[:, at]
        v[:, at] = value.astype(BF16)
        start = at.start % share
        sent[at.start // share][:, start : start + 128] = value.astype(BF16)


def label_body(squares, beside, sent, total, out):
    value = squares[...] + beside[...]
    total[...] = value
    first = lax.broadcasted_iota(jnp.int32, (16, 128), 0) == 0
    for k in range(3):
        col = slice(k * 128, (k + 1) * 128)
        term = value.astype(BF16).astype(F32)
        value = value - term
        out[:, col] = jnp.where(first, term, sent[:, col].astype(F32)).astype(BF16)


def label(squares, beside, sent):
    rows, width = sent.shape
    part = pl.BlockSpec((16, 3 * 128), lambda i: (0, 0))
    row = pl.BlockSpec((1, rows), lambda i: (0, 0))
    return pl.pallas_call(
        label_body,
        grid=(1,),
        in_specs=[row, row, part],
        out_specs=[row, part],
        out_shape=[jax.ShapeDtypeStruct((1, rows), F32), jax.ShapeDtypeStruct((rows, width), BF16)],
        input_output_aliases={2: 1},
        compiler_params=pltpu.CompilerParams(vmem_limit_bytes=VMEM),
        name="label",
    )(squares, beside, sent)


def tables_body(forward, taps, inner, short_outer, decay, spectrum, gate):
    f_hi, f_lo = split(forward[:, :BLOCK])
    for at in pieces_of(taps.shape[1]):
        d = decay[:, at]
        spectrum[:, at] = dot(f_hi, taps[:, at]) + dot(f_lo, taps[:, at])
        time = times(SUB)
        gate[:, at] = inner[:, at].astype(F32) * short_outer[:, at].astype(F32) * jnp.exp(d * time)


def conv_first(
    before, here, squares, forward, back, lower, spectrum, gate, decay, far, state, matrix, summed, sems
):
    carried = before[:16, : 3 * 128].astype(F32)
    earlier = (carried[:1, :128] + carried[:1, 128:256]) + carried[:1, 256:]
    sums = jnp.concatenate([earlier, squares[...]], axis=1)
    column = lax.broadcasted_iota(jnp.int32, (1, 2 * BLOCK), 1)
    factor = jnp.where(column == 0, 0.0, 1.0 / jnp.sqrt(sums / D + 0.5))
    matrix[...] = (forward[...] * factor).astype(BF16)
    conv_body(0, before, here, matrix, back, lower, spectrum, gate, decay, far, state, summed, sems)


def conv_last(
    start, before, here, matrix, back, lower, spectrum, gate, decay, earlier, far, copied, rows, summed, sems
):
    conv_body(start, before, here, matrix, back, lower, spectrum, gate, decay, far, rows, summed, sems)
    state = jnp.concatenate([earlier[...], rows[...]], axis=0).astype(BF16)
    for k in range(copied.shape[0]):
        copied[k] = state


def conv_body(
    start, before, here, matrix, back, lower, spectrum, gate, decay, far, state, summed, sems
):
    b = back[...].astype(BF16)
    leaving = []
    width = before.shape[1] // CHUNKS
    for j, to in enumerate(pieces_of(before.shape[1])):
        at = slice(start + to.start, start + to.stop)
        x = dot(matrix[...], jnp.concatenate([before[:, to], here[:, at]], axis=0))
        h = spectrum[:, at]
        x_re, x_im = x[:BLOCK], x[BLOCK:]
        h_re, h_im = h[:BLOCK], h[BLOCK:]
        y_re = (x_re * h_re - x_im * h_im).astype(BF16)
        y_im = (x_re * h_im + x_im * h_re).astype(BF16)
        conv = dot(b, jnp.concatenate([y_re, y_im], axis=0))
        z = (gate[:, at] * conv).astype(BF16)
        summed[:, to] = z
        result = dot(lower[...], z)
        last = result[BLOCK - 1 :] * jnp.exp(decay[:, at] * (1.0 - BLOCK))
        for k in range(SUB // 128):
            row = j * (SUB // 128) + k
            state[row : row + 1, :] = last[:, k * 128 : (k + 1) * 128]
        if to.stop % width == 0:
            chunk = to.stop // width - 1
            at = pl.ds(chunk * width, width)
            leaving.append(pltpu.make_async_copy(summed.at[:, at], far.at[:, at], sems.at[chunk]))
            leaving[-1].start()
    for copy in leaving:
        copy.wait()


def weighted(pieces, place, rate, some=slice(None)):
    out = jnp.zeros(rate.shape, F32)
    for k in range(pieces.shape[0]):
        gap = place - 1 - k
        weight = jnp.exp(-rate * jnp.maximum(gap, 0).astype(F32))
        out = out + jnp.where(gap >= 0, weight * pieces[k, some].astype(F32), 0.0)
    return out


def near_body(place, pieces, rate, inside, copied):
    size, r = pieces.shape[0], rate[...]
    inside[...] = weighted(pieces, place[0], r)
    group = weighted(pieces, jnp.int32(size), r).astype(BF16)
    for k in range(copied.shape[0]):
        copied[k] = group


def finish_body(
    part,
    near_size,
    place,
    others,
    inside,
    rate,
    summed_far,
    lower,
    outer_far,
    decay,
    scale,
    weights,
    mixed,
    ahead,
    summed,
    long_outer,
    summed_sems,
    outer_sems,
):
    width = long_outer.shape[1] // CHUNKS
    summed_in = fetches(summed_far, summed, summed_sems, 0, width)
    outer_in = fetches(outer_far, long_outer, outer_sems, part * long_outer.shape[1], width)
    near, far = place[0], place[1]
    lanes = others.shape[1] // PARTS
    some = slice(part * lanes, (part + 1) * lanes)
    r = rate[some]
    carry = inside[some] + jnp.exp(-r * near.astype(F32)) * weighted(
        others, far, r * near_size, some
    )
    time = times(width)
    group = width // HEAD_DIM
    for k in range(CHUNKS):
        to = slice(k * width, (k + 1) * width)
        at = slice(part * lanes * HEAD_DIM + to.start, part * lanes * HEAD_DIM + to.stop)
        d = decay[:, at]
        entering = jnp.concatenate(
            [carry[j : j + 1] for j in range(k * group, (k + 1) * group)], axis=1
        ) * jnp.exp(-d)
        factor = jnp.exp(-d * time) * scale[:, at]
        summed_in[k].wait()
        base = dot(lower[...], summed[:, to]) + entering
        outer_in[k].wait()
        mixed[:, to] = (long_outer[:, to].astype(F32) * factor * base).astype(BF16)
    for j in range(lanes):
        to = slice(j * HEAD_DIM, (j + 1) * HEAD_DIM)
        ahead[:, to] = dot(weights[part * lanes + j], mixed[:, to]).astype(BF16)


def score(query, key):
    return lax.dot_general(
        query, key, (((1,), (1,)), ((), ())), preferred_element_type=F32
    ) * HEAD_DIM ** (-0.5)


def soft(scores):
    top = jnp.max(scores, axis=1, keepdims=True)
    e = jnp.exp(scores - top)
    return e, top, jnp.sum(e, axis=1, keepdims=True)


def fetches(source, target, sems, first, width):
    copies = []
    for k in range(target.shape[1] // width):
        to = pl.ds(k * width, width)
        at = pl.ds(first + k * width, width)
        copies.append(pltpu.make_async_copy(source.at[:, at], target.at[:, to], sems.at[k]))
    for copy in copies:
        copy.start()
    return copies


def own_body(query_far, key_far, weights, stats, query, key, query_sems, key_sems):
    width = key.shape[1] // CHUNKS
    arriving = [
        pair
        for pair in zip(
            fetches(query_far, query, query_sems, 0, width),
            fetches(key_far, key, key_sems, 0, width),
        )
    ]
    row = lax.broadcasted_iota(jnp.int32, (BLOCK, BLOCK), 0)
    lane = lax.broadcasted_iota(jnp.int32, (BLOCK, BLOCK), 1)
    tops = jnp.zeros((BLOCK, BLOCK), F32)
    sizes = jnp.zeros((BLOCK, BLOCK), F32)
    for j in range(weights.shape[0]):
        at = slice(j * HEAD_DIM, (j + 1) * HEAD_DIM)
        if at.start % width == 0:
            for copy in arriving[at.start // width]:
                copy.wait()
        e, top, size = soft(jnp.where(lane <= row, score(query[:, at], key[:, at]), -1e30))
        weights[j] = e.astype(BF16)
        tops = jnp.where(lane == j, top, tops)
        sizes = jnp.where(lane == j + BLOCK // 2, size, sizes)
    stats[...] = jnp.where(lane < BLOCK // 2, tops, sizes)


def ahead_body(query, key_far, weights, stats, key, sems):
    width = key.shape[1] // CHUNKS
    arriving = fetches(key_far, key, sems, 0, width)
    lane = lax.broadcasted_iota(jnp.int32, (BLOCK, BLOCK), 1)
    tops = jnp.zeros((BLOCK, BLOCK), F32)
    sizes = jnp.zeros((BLOCK, BLOCK), F32)
    for j in range(weights.shape[0]):
        at = slice(j * HEAD_DIM, (j + 1) * HEAD_DIM)
        if at.start % width == 0:
            arriving[at.start // width].wait()
        e, top, size = soft(score(query[:, at], key[:, at]))
        weights[j] = (e * (1.0 / size)).astype(BF16)
        tops = jnp.where(lane == j, top, tops)
        sizes = jnp.where(lane == j + BLOCK // 2, size, sizes)
    stats[...] = jnp.where(lane < BLOCK // 2, tops, sizes)


def here_body(part, weights, mixed, partial):
    heads = partial.shape[1] // HEAD_DIM
    for j in range(heads):
        at = slice(j * HEAD_DIM, (j + 1) * HEAD_DIM)
        partial[:, at] = dot(weights[part * heads + j], mixed[:, at])


def join_body(part, partial, before, stats_here, stats_before, *rest):
    attended = rest[-1]
    top, size = stats_here[...], pltpu.roll(stats_here[...], BLOCK // 2, 1)
    size_b = pltpu.roll(stats_before[...], BLOCK // 2, 1)
    top_b = jnp.where(size_b > 0.0, stats_before[...], -1e30)
    highest = jnp.maximum(top, top_b)
    scale = jnp.exp(top - highest)
    scale_b = size_b * jnp.exp(top_b - highest)
    whole = 1.0 / (size * scale + scale_b)
    own, share = scale * whole, scale_b * whole
    heads = partial.shape[1] // HEAD_DIM
    for j in range(heads):
        at = slice(j * HEAD_DIM, (j + 1) * HEAD_DIM)
        head = part * heads + j
        attended[:, at] = (
            partial[:, at] * own[:, head : head + 1]
            + share[:, head : head + 1] * before[:, at].astype(F32)
        ).astype(BF16)


def copy_body(block, *rest):
    rest[-1][...] = block[...]


def into(body, part, operands, whole, width):
    rows = operands[0].shape[0]
    share = width // PARTS
    specs = [pl.BlockSpec(x.shape, lambda i: (0, 0)) for x in operands]
    aliases = {}
    if whole is not None:
        specs.append(pl.BlockSpec(memory_space=pl.ANY))
        aliases = {len(operands): 0}
        operands = (*operands, whole)
    return pl.pallas_call(
        body,
        grid=(1,),
        in_specs=specs,
        out_specs=pl.BlockSpec((rows, share), lambda i: (0, part)),
        out_shape=jax.ShapeDtypeStruct((rows, width), BF16),
        input_output_aliases=aliases,
        compiler_params=pltpu.CompilerParams(vmem_limit_bytes=VMEM),
    )(*operands)


def on_device(
    stream,
    norm_gain,
    short_outer,
    short_inner,
    short_filter,
    long_outer,
    long_inner,
    long_decay,
    query_heads,
    key_heads,
):
    rows, width = stream.shape
    heads, lanes = width // HEAD_DIM, width // 128
    decay = long_decay[None]
    scale = jnp.sqrt(-jnp.expm1(-2.0 * decay))
    rate = long_decay.reshape(lanes, 128) * rows
    near, far = lax.axis_index(NEAR), lax.axis_index(FAR)
    near_size, far_size = lax.axis_size(NEAR), lax.axis_size(FAR)
    forward, back = jnp.asarray(FORWARD), jnp.asarray(BACK)
    lower = jnp.asarray(np.tril(np.ones((rows, rows), np.float32)), BF16)
    square = ((rows, rows), F32)
    wide, wide_float = ((rows, width), BF16), ((rows, width), F32)

    half = ((rows, width // PARTS), BF16)
    some = lanes // PARTS
    (squares,) = call(squares_body, [((1, rows), F32)], operands=1)(stream)
    beside = swapped(squares)
    v, *sent = call(gate_body, [wide] + [half] * PARTS, operands=3)(
        stream, short_inner, norm_gain[None]
    )
    total, sent[0] = label(squares, beside, sent[0])
    v_before = []
    for part in range(PARTS):
        v_before.append(shifted(sent[part], SEQ, 1))
    queries, total = lax.optimization_barrier((query_heads, total))
    query_next = shifted(queries, SEQ, -1)
    spectrum, gate = call(
        tables_body, [((2 * rows, width), F32), wide_float], operands=5
    )(forward, short_filter, long_inner, short_outer, decay)
    some_state = ((some, 128), F32)
    leaving = [pltpu.VMEM((rows, width // PARTS), BF16), pltpu.SemaphoreType.DMA((CHUNKS,))]
    first, early, matrix = call(
        conv_first, [half, some_state, ((2 * rows, 2 * rows), BF16)], leaving, operands=9, kept=(0,)
    )(v_before[0], v, total, forward, back, lower, spectrum, gate, decay)
    last, state = call(
        functools.partial(conv_last, width // PARTS),
        [half, ((near_size, lanes, 128), BF16)],
        [pltpu.VMEM((some, 128), F32), *leaving],
        operands=9,
        kept=(0,),
    )(v_before[1], v, matrix, back, lower, spectrum, gate, decay, early)
    summed = [first, last]
    pieces = lax.all_to_all(state, NEAR, 0, 0, tiled=True)
    weights_here, stats_here = call(
        own_body,
        [((heads, rows, rows), BF16), square],
        [pltpu.VMEM((rows, width), BF16)] * 2 + [pltpu.SemaphoreType.DMA((CHUNKS,))] * 2,
        operands=2,
        outside=(0, 1),
    )(in_hbm(query_heads), in_hbm(key_heads))
    pieces, stats_here = lax.optimization_barrier((pieces, stats_here))
    inside, group = call(
        near_body, [((lanes, 128), F32), ((far_size, lanes, 128), BF16)], scalars=1, operands=2
    )(near[None], pieces, rate)
    others = lax.all_to_all(group, FAR, 0, 0, tiled=True)
    query_next, keys, inside = lax.optimization_barrier((query_next, key_heads, inside))
    weights_next, stats_next = call(
        ahead_body,
        [((heads, rows, rows), BF16), square],
        [pltpu.VMEM((rows, width), BF16), pltpu.SemaphoreType.DMA((CHUNKS,))],
        operands=2,
        outside=(1,),
    )(query_next, in_hbm(keys))
    stats_before = shifted(stats_next, SEQ, 1)
    mixed, arrived = [], []
    for part in range(PARTS):
        block, ready = call(
            functools.partial(finish_body, part, float(near_size)),
            [half, half],
            [pltpu.VMEM((rows, width // PARTS), BF16)] * 2
            + [pltpu.SemaphoreType.DMA((CHUNKS,))] * 2,
            scalars=1,
            operands=9,
            outside=(4, 6),
        )(
            jnp.stack([near, far]),
            others,
            inside,
            rate,
            in_hbm(summed[part]),
            lower,
            in_hbm(long_outer),
            decay,
            scale,
            weights_next,
        )
        mixed.append(block)
        arrived.append(shifted(ready, SEQ, 1))
    attended = values = None
    for part in range(PARTS):
        (partial,) = call(
            functools.partial(here_body, part), [((rows, width // PARTS), F32)], operands=2
        )(weights_here, mixed[part])
        values = into(copy_body, part, (mixed[part],), values, width)
        attended = into(
            functools.partial(join_body, part),
            part,
            (partial, arrived[part], stats_here, stats_before),
            attended,
            width,
        )
    return (values, attended)


def solution(mesh):
    finer = Mesh(
        mesh.devices.reshape(8, 2, 4, 2, mesh.shape["mp"]),
        ("seq_0", "seq_1", "seq_2", "seq_3", "mp"),
    )
    placed = (
        P(SEQ, "mp"),
        P("mp"),
        P(SEQ, "mp"),
        P(SEQ, "mp"),
        P(None, "mp"),
        P(SEQ, "mp"),
        P(SEQ, "mp"),
        P("mp"),
        P(SEQ, "mp"),
        P(SEQ, "mp"),
    )
    return jax.shard_map(
        on_device,
        mesh=finer,
        in_specs=placed,
        out_specs=(P(SEQ, "mp"), P(SEQ, "mp")),
        check_vma=False,
    )
```

time: 89.6 us -> 92.5 us (1.032)
  the two profiles are of different devices: /device:TPU:128 before, /device:TPU:32 now
where the time goes in v4:
time: 92.5 us; the launch traced here: 91.7 us
  starting transfers between devices  30.8 us (33%)
  waiting for transfers between devices  27.3 us (30%)
  Pallas kernels  25.4 us (27%)
  local copies, waits for them, and re-layouts  7.29 us (8%)
    ppermute x6, waiting for transfers between devices, shifted(): lax.ppermute(block, axis, [(i, i + distance) for i in range(size) if 0 <=...  18.7 us
    ppermute x6, starting transfers between devices, shifted(): lax.ppermute(block, axis, [(i, i + distance) for i in range(size) if 0 <=...  16.1 us
    all_to_all x1, starting transfers between devices, on_device(): others = lax.all_to_all(group, FAR, 0, 0, tiled=True)  9.79 us
    unnamed x22, local copies, waits for them, and re-layouts  7.29 us
    all_to_all x1, waiting for transfers between devices, on_device(): others = lax.all_to_all(group, FAR, 0, 0, tiled=True)  6.34 us
    pallas_call x2, Pallas kernels, on_device(): call(functools.partial(finish_body, part, float(near_size)), [half, half]...  5.53 us
    pallas_call x4, Pallas kernels, into(): pl.pallas_call(body, grid=(1,), in_specs=specs, out_specs=pl.BlockSpec((r...  4.75 us
    all_to_all x1, starting transfers between devices, on_device(): pieces = lax.all_to_all(state, NEAR, 0, 0, tiled=True)  3.36 us
  transfers between devices with their start and end apart: 9, of which 5 were waited for; matrix products, arithmetic and copies ran while one was open for 0% of the time, Pallas kernels for 23%

profile of v4, /device:TPU:32, one launch (start us, length us, event | category | flops | bytes accessed | tf_op | source)
XLA Modules:
  0.0 91.7 jit_solution(7610863924798588234)
XLA Ops:
  0.6 0.0 copy-start
  0.6 1.2 %copy-done = bf16[128,4096]{1,0:T(8,128)(2,1)S(1)} copy-done((bf16[128,4096]{1,0:T(8,128)(2,1)S(1)}, bf16[128,4096]{1,0:T(8,128)(2,1)}, u32[]{:S(2)}) %copy-start) | copy-done | bytes 1048600
  1.9 0.0 copy-start.2
  1.9 0.3 shard_map.141.squares
  2.2 1.6 %collective-permute-start.1 = (f32[1,128]{1,0:T(1,128)S(1)}, f32[1,128]{1,0:T(1,128)S(1)}, u32[]{:S(2)}, u32[]{:S(2)}) collective-permute-start(f32[1,128]{1,0:T(1,128)S(1)} %shard_map.141.squares), channel_id=1, source_target_pairs={{0,1},{1,0},{2,3},{3,2},{4,5},{5,4},{6,7},{7,6},{8,9},{9,8},{10,11... | collective-permute-start | bytes 1544 | tf_op jit(solution)/shard_map/ppermute | solution.py:55
  3.7 0.0 copy-start.1
  3.7 1.2 %copy-done.1 = bf16[128,4096]{1,0:T(8,128)(2,1)S(1)} copy-done((bf16[128,4096]{1,0:T(8,128)(2,1)S(1)}, bf16[128,4096]{1,0:T(8,128)(2,1)}, u32[]{:S(2)}) %copy-start.1) | copy-done | bytes 1048600
  5.0 0.0 copy-start.10
  5.0 0.7 copy-done.10
  5.7 0.0 copy-start.8
  5.7 0.0 copy-start.9
  5.7 0.4 shard_map.140
  6.0 0.0 collective-permute-done.1.beside
  6.1 5.8 %collective-permute-start.3 = (bf16[128,4096]{1,0:T(8,128)(2,1)}, bf16[128,4096]{1,0:T(8,128)(2,1)S(1)}, u32[]{:S(2)}, u32[]{:S(2)}) collective-permute-start(bf16[128,4096]{1,0:T(8,128)(2,1)} %query_far.1), channel_id=1, source_target_pairs={{2,0},{4,2},{6,4},{8,6},{10,8},{12,10},{14,12},{16,14},{18,16},{20... | collective-permute-start | bytes 3145736 | tf_op jit(solution)/shard_map/ppermute | solution.py:50
  11.9 1.9 %collective-permute-start.2 = (bf16[128,2048]{1,0:T(8,128)(2,1)S(1)}, bf16[128,2048]{1,0:T(8,128)(2,1)S(1)}, u32[]{:S(2)}, u32[]{:S(2)}) collective-permute-start(bf16[128,2048]{1,0:T(8,128)(2,1)S(1)} %get-tuple-element.34), channel_id=1, source_target_pairs={{0,2},{2,4},{4,6},{6,8},{8,10},{10,12},{12,14},{14,16},{16,18},{18... | collective-permute-start | bytes 1572872 | tf_op jit(solution)/shard_map/ppermute | solution.py:50
  13.8 1.9 %collective-permute-start = (bf16[128,2048]{1,0:T(8,128)(2,1)S(1)}, bf16[128,2048]{1,0:T(8,128)(2,1)S(1)}, u32[]{:S(2)}, u32[]{:S(2)}) collective-permute-start(bf16[128,2048]{1,0:T(8,128)(2,1)S(1)} %get-tuple-element.31), channel_id=1, source_target_pairs={{0,2},{2,4},{4,6},{6,8},{8,10},{10,12},{12,14},{14,16},{16,18},{18... | collective-permute-start | bytes 1572872 | tf_op jit(solution)/shard_map/ppermute | solution.py:50
  15.7 0.0 copy-done.2
  15.7 0.0 copy-start.3
  15.8 1.2 %copy-done.3 = bf16[128,4096]{1,0:T(8,128)(2,1)S(1)} copy-done((bf16[128,4096]{1,0:T(8,128)(2,1)S(1)}, bf16[128,4096]{1,0:T(8,128)(2,1)}, u32[]{:S(2)}) %copy-start.3) | copy-done | bytes 1048600
  17.0 0.0 copy-start.4
  17.0 1.2 %copy-done.4 = bf16[128,4096]{1,0:T(8,128)(2,1)S(1)} copy-done((bf16[128,4096]{1,0:T(8,128)(2,1)S(1)}, bf16[128,4096]{1,0:T(8,128)(2,1)}, u32[]{:S(2)}) %copy-start.4) | copy-done | bytes 1048600
  18.2 0.0 copy-start.5
  18.2 0.9 %copy-done.5 = f32[256,256]{1,0:T(8,128)S(1)} copy-done((f32[256,256]{1,0:T(8,128)S(1)}, f32[256,256]{1,0:T(8,128)}, u32[]{:S(2)}) %copy-start.5) | copy-done | bytes 262168
  19.1 0.0 copy-start.6
  19.1 0.7 copy-done.6
  19.9 1.3 %shard_map.142 = (f32[256,4096]{1,0:T(8,128)S(1)}, f32[128,4096]{1,0:T(8,128)S(1)}) custom-call(f32[256,256]{1,0:T(8,128)S(1)} %copy-done.5, bf16[128,4096]{1,0:T(8,128)(2,1)S(1)} %copy-done.2, bf16[128,4096]{1,0:T(8,128)(2,1)S(1)} %copy-done.3, bf16[128,4096]{1,0:T(8,128)(2,1)S(1)} %copy-done.4, f32[1,4096]{1,0:T(1,128)S(1)} %bitcast.7), custom_call_target="tpu_custom_call" | custom-call | flops 100000000 | bytes 1000000 | tf_op jit(solution)/shard_map/pallas_call | solution.py:416
  21.2 5.7 %collective-permute-done.2.before = bf16[128,2048]{1,0:T(8,128)(2,1)S(1)} collective-permute-done((bf16[128,2048]{1,0:T(8,128)(2,1)S(1)}, bf16[128,2048]{1,0:T(8,128)(2,1)S(1)}, u32[]{:S(2)}, u32[]{:S(2)}) %collective-permute-start.2) | collective-permute-done | bytes 524320 | tf_op jit(solution)/shard_map/ppermute | solution.py:50
  26.9 0.0 copy-done.8
  26.9 0.0 copy-done.9
  26.9 2.4 %shard_map.143 = (bf16[128,2048]{1,0:T(8,128)(2,1)}, f32[16,128]{1,0:T(8,128)S(1)}, bf16[256,256]{1,0:T(8,128)(2,1)S(1)}) custom-call(bf16[128,2048]{1,0:T(8,128)(2,1)S(1)} %collective-permute-done.2.before, bf16[128,4096]{1,0:T(8,128)(2,1)S(1)} %get-tuple-element.32.here, f32[1,128]{1,0:T(1,128)S(1)} %get-tuple-element.36.squares, ...), custom_call_target="tpu_custom_call" | custom-call | flops 100000000 | bytes 1000000 | tf_op jit(solution)/shard_map/pallas_call | solution.py:421
  29.3 0.0 copy-start.7
  29.3 3.2 %collective-permute-done.before = bf16[128,2048]{1,0:T(8,128)(2,1)S(1)} collective-permute-done((bf16[128,2048]{1,0:T(8,128)(2,1)S(1)}, bf16[128,2048]{1,0:T(8,128)(2,1)S(1)}, u32[]{:S(2)}, u32[]{:S(2)}) %collective-permute-start) | collective-permute-done | bytes 524320 | tf_op jit(solution)/shard_map/ppermute | solution.py:50
  32.5 3.0 %shard_map.144 = (bf16[128,2048]{1,0:T(8,128)(2,1)}, bf16[8,32,128]{2,1,0:T(8,128)(2,1)}) custom-call(bf16[128,2048]{1,0:T(8,128)(2,1)S(1)} %collective-permute-done.before, bf16[128,4096]{1,0:T(8,128)(2,1)S(1)} %get-tuple-element.32.here, bf16[256,256]{1,0:T(8,128)(2,1)S(1)} %get-tuple-element.39.matrix, f32[128,256]{1,0:T(8,128)S(1)} %copy-done.8, ...), custom_call_target="tpu_custom_call" | custom-call | flops 100000000 | bytes 1000000 | tf_op jit(solution)/shard_map/pallas_call | solution.py:424
  35.6 3.4 %all-to-all-start = ((bf16[8,32,128]{2,1,0:T(8,128)(2,1)}), bf16[8,32,128]{2,1,0:T(8,128)(2,1)S(1)}, u32[]{:S(2)}, u32[]{:S(2)}) async-start(bf16[8,32,128]{2,1,0:T(8,128)(2,1)} %get-tuple-element.41), calls=%async_computation | async-start | bytes 131072 | tf_op jit(solution)/shard_map/all_to_all | solution.py:432
  38.9 0.0 copy-done.7
  39.0 3.3 %shard_map.145 = (bf16[32,128,128]{2,1,0:T(8,128)(2,1)S(1)}, f32[128,128]{1,0:T(8,128)S(1)}) custom-call(bf16[128,4096]{1,0:T(8,128)(2,1)} %query_far.1, bf16[128,4096]{1,0:T(8,128)(2,1)} %key_far.2), custom_call_target="tpu_custom_call" | custom-call | flops 100000000 | bytes 1000000 | tf_op jit(solution)/shard_map/pallas_call | solution.py:433
  42.3 2.2 %all-to-all-done.pieces = bf16[8,32,128]{2,1,0:T(8,128)(2,1)S(1)} async-done(((bf16[8,32,128]{2,1,0:T(8,128)(2,1)}), bf16[8,32,128]{2,1,0:T(8,128)(2,1)S(1)}, u32[]{:S(2)}, u32[]{:S(2)}) %all-to-all-start) | async-done | bytes 65568 | tf_op jit(solution)/shard_map/all_to_all | solution.py:432
  44.5 0.7 shard_map.146
  45.2 9.8 %all-to-all-start.1 = ((bf16[16,32,128]{2,1,0:T(8,128)(2,1)}), bf16[16,32,128]{2,1,0:T(8,128)(2,1)S(1)}, u32[]{:S(2)}, u32[]{:S(2)}) async-start(bf16[16,32,128]{2,1,0:T(8,128)(2,1)} %get-tuple-element.44), calls=%async_computation.1 | async-start | bytes 262144 | tf_op jit(solution)/shard_map/all_to_all | solution.py:444
  54.9 0.1 pad_add_fusion.place
  55.0 0.0 collective-permute-done.3.query
  55.0 3.2 %shard_map.147 = (bf16[32,128,128]{2,1,0:T(8,128)(2,1)S(1)}, f32[128,128]{1,0:T(8,128)S(1)}) custom-call(bf16[128,4096]{1,0:T(8,128)(2,1)S(1)} %collective-permute-done.3.query, bf16[128,4096]{1,0:T(8,128)(2,1)} %key_far.2), custom_call_target="tpu_custom_call" | custom-call | flops 100000000 | bytes 1000000 | tf_op jit(solution)/shard_map/pallas_call | solution.py:446
  58.2 6.3 %all-to-all-done.1.others = bf16[16,32,128]{2,1,0:T(8,128)(2,1)S(1)} async-done(((bf16[16,32,128]{2,1,0:T(8,128)(2,1)}), bf16[16,32,128]{2,1,0:T(8,128)(2,1)S(1)}, u32[]{:S(2)}, u32[]{:S(2)}) %all-to-all-start.1) | async-done | bytes 131104 | tf_op jit(solution)/shard_map/all_to_all | solution.py:444
  64.5 2.8 %shard_map.149 = (bf16[128,2048]{1,0:T(8,128)(2,1)S(1)}, bf16[128,2048]{1,0:T(8,128)(2,1)S(1)}) custom-call(s32[2]{0:T(128)S(1)} %pad_add_fusion.place, bf16[16,32,128]{2,1,0:T(8,128)(2,1)S(1)} %all-to-all-done.1.others, f32[32,128]{1,0:T(8,128)S(1)} %get-tuple-element.47.inside, f32[32,128]{1,0:T(8,128)S(1)} %get-tuple-element.61.rate, ...), custom_call_target="tpu_custom_call" | custom-call | flops 100000000 | bytes 1000000 | tf_op jit(solution)/shard_map/pallas_call | solution.py:456
  67.3 1.9 %collective-permute-start.6 = (bf16[128,2048]{1,0:T(8,128)(2,1)S(1)}, bf16[128,2048]{1,0:T(8,128)(2,1)S(1)}, u32[]{:S(2)}, u32[]{:S(2)}) collective-permute-start(bf16[128,2048]{1,0:T(8,128)(2,1)S(1)} %get-tuple-element.59), channel_id=1, source_target_pairs={{0,2},{2,4},{4,6},{6,8},{8,10},{10,12},{12,14},{14,16},{16,18},{18... | collective-permute-start | bytes 1572872 | tf_op jit(solution)/shard_map/ppermute | solution.py:50
  69.2 2.8 %shard_map.148 = (bf16[128,2048]{1,0:T(8,128)(2,1)S(1)}, bf16[128,2048]{1,0:T(8,128)(2,1)S(1)}) custom-call(s32[2]{0:T(128)S(1)} %pad_add_fusion.place, bf16[16,32,128]{2,1,0:T(8,128)(2,1)S(1)} %all-to-all-done.1.others, f32[32,128]{1,0:T(8,128)S(1)} %get-tuple-element.47.inside, f32[32,128]{1,0:T(8,128)S(1)} %get-tuple-element.61.rate, ...), custom_call_target="tpu_custom_call" | custom-call | flops 100000000 | bytes 1000000 | tf_op jit(solution)/shard_map/pallas_call | solution.py:456
  72.0 2.6 %collective-permute-start.4 = (bf16[128,2048]{1,0:T(8,128)(2,1)S(1)}, bf16[128,2048]{1,0:T(8,128)(2,1)S(1)}, u32[]{:S(2)}, u32[]{:S(2)}) collective-permute-start(bf16[128,2048]{1,0:T(8,128)(2,1)S(1)} %get-tuple-element.56), channel_id=1, source_target_pairs={{0,2},{2,4},{4,6},{6,8},{8,10},{10,12},{12,14},{14,16},{16,18},{18... | collective-permute-start | bytes 1572872 | tf_op jit(solution)/shard_map/ppermute | solution.py:50
  74.6 1.9 %collective-permute-start.5 = (f32[128,128]{1,0:T(8,128)S(1)}, f32[128,128]{1,0:T(8,128)S(1)}, u32[]{:S(2)}, u32[]{:S(2)}) collective-permute-start(f32[128,128]{1,0:T(8,128)S(1)} %get-tuple-element.58), channel_id=1, source_target_pairs={{0,2},{2,4},{4,6},{6,8},{8,10},{10,12},{12,14},{14,16},{16,18},{18... | collective-permute-start | bytes 196616 | tf_op jit(solution)/shard_map/ppermute | solution.py:50
  76.5 0.8 shard_map.150.rest_0_
  77.4 0.8 shard_map.151
  78.2 0.3 shard_map.153.partial
  78.5 0.3 shard_map.152.partial
  78.8 9.8 %collective-permute-done.5.stats_before = f32[128,128]{1,0:T(8,128)S(1)} collective-permute-done((f32[128,128]{1,0:T(8,128)S(1)}, f32[128,128]{1,0:T(8,128)S(1)}, u32[]{:S(2)}, u32[]{:S(2)}) %collective-permute-start.5) | collective-permute-done | bytes 65568 | tf_op jit(solution)/shard_map/ppermute | solution.py:50
  88.6 0.0 collective-permute-done.6.before
  88.6 1.5 %shard_map.154.rest_0_ = bf16[128,4096]{1,0:T(8,128)(2,1)} custom-call(f32[128,2048]{1,0:T(8,128)S(1)} %shard_map.153.partial, bf16[128,2048]{1,0:T(8,128)(2,1)S(1)} %collective-permute-done.6.before, f32[128,128]{1,0:T(8,128)S(1)} %get-tuple-element.57.stats_here, f32[128,128]{1,0:T(8,128)S(1)} %collective-permute-done.5.stats_before), custom_call_target="tpu_custom_call" | custom-call | tf_op jit(solution)/shard_map/pallas_call | solution.py:368
  90.2 0.0 collective-permute-done.4.before
  90.2 1.6 %shard_map.155 = bf16[128,4096]{1,0:T(8,128)(2,1)} custom-call(f32[128,2048]{1,0:T(8,128)S(1)} %shard_map.152.partial, bf16[128,2048]{1,0:T(8,128)(2,1)S(1)} %collective-permute-done.4.before, f32[128,128]{1,0:T(8,128)S(1)} %get-tuple-element.57.stats_here, f32[128,128]{1,0:T(8,128)S(1)} %collective-permute-done.5.stats_before, ...), custom_call_target="tpu_custom_call", output_to_operand_aliasing={{}: (4, {})} | custom-call | tf_op jit(solution)/shard_map/pallas_call | solution.py:368
  (2 shorter events, 0.0 us)
Async XLA Ops:
  0.6 1.2 %copy-start = (bf16[128,4096]{1,0:T(8,128)(2,1)S(1)}, bf16[128,4096]{1,0:T(8,128)(2,1)}, u32[]{:S(2)}) copy-start(bf16[128,4096]{1,0:T(8,128)(2,1)} %stream.3) | copy-start | bytes 3145732
  1.9 13.9 %copy-start.2 = (bf16[128,4096]{1,0:T(8,128)(2,1)S(1)}, bf16[128,4096]{1,0:T(8,128)(2,1)}, u32[]{:S(2)}) copy-start(bf16[128,4096]{1,0:T(8,128)(2,1)} %taps.1) | copy-start | bytes 3145732
  2.2 3.9 %collective-permute-start.1 = (f32[1,128]{1,0:T(1,128)S(1)}, f32[1,128]{1,0:T(1,128)S(1)}, u32[]{:S(2)}, u32[]{:S(2)}) collective-permute-start(f32[1,128]{1,0:T(1,128)S(1)} %shard_map.141.squares), channel_id=1, source_target_pairs={{0,1},{1,0},{2,3},{3,2},{4,5},{5,4},{6,7},{7,6},{8,9},{9,8},{10,11... | collective-permute-start | bytes 1544 | tf_op jit(solution)/shard_map/ppermute | solution.py:55
  3.7 1.2 %copy-start.1 = (bf16[128,4096]{1,0:T(8,128)(2,1)S(1)}, bf16[128,4096]{1,0:T(8,128)(2,1)}, u32[]{:S(2)}) copy-start(bf16[128,4096]{1,0:T(8,128)(2,1)} %inner.2) | copy-start | bytes 3145732
  5.0 0.7 copy-start.10
  5.7 21.2 %copy-start.8 = (f32[128,256]{1,0:T(8,128)S(1)}, f32[128,256]{1,0:T(8,128)}, u32[]{:S(2)}) copy-start(f32[128,256]{1,0:T(8,128)} %constant.32.clone.back) | copy-start | bytes 393220
  5.7 21.2 %copy-start.9 = (bf16[128,128]{1,0:T(8,128)(2,1)S(1)}, bf16[128,128]{1,0:T(8,128)(2,1)}, u32[]{:S(2)}) copy-start(bf16[128,128]{1,0:T(8,128)(2,1)} %constant.33.clone.lower) | copy-start | bytes 98308
  6.1 49.0 %collective-permute-start.3 = (bf16[128,4096]{1,0:T(8,128)(2,1)}, bf16[128,4096]{1,0:T(8,128)(2,1)S(1)}, u32[]{:S(2)}, u32[]{:S(2)}) collective-permute-start(bf16[128,4096]{1,0:T(8,128)(2,1)} %query_far.1), channel_id=1, source_target_pairs={{2,0},{4,2},{6,4},{8,6},{10,8},{12,10},{14,12},{16,14},{18,16},{20... | collective-permute-start | bytes 3145736 | tf_op jit(solution)/shard_map/ppermute | solution.py:50
  11.9 15.0 %collective-permute-start.2 = (bf16[128,2048]{1,0:T(8,128)(2,1)S(1)}, bf16[128,2048]{1,0:T(8,128)(2,1)S(1)}, u32[]{:S(2)}, u32[]{:S(2)}) collective-permute-start(bf16[128,2048]{1,0:T(8,128)(2,1)S(1)} %get-tuple-element.34), channel_id=1, source_target_pairs={{0,2},{2,4},{4,6},{6,8},{8,10},{10,12},{12,14},{14,16},{16,18},{18... | collective-permute-start | bytes 1572872 | tf_op jit(solution)/shard_map/ppermute | solution.py:50
  13.8 18.7 %collective-permute-start = (bf16[128,2048]{1,0:T(8,128)(2,1)S(1)}, bf16[128,2048]{1,0:T(8,128)(2,1)S(1)}, u32[]{:S(2)}, u32[]{:S(2)}) collective-permute-start(bf16[128,2048]{1,0:T(8,128)(2,1)S(1)} %get-tuple-element.31), channel_id=1, source_target_pairs={{0,2},{2,4},{4,6},{6,8},{8,10},{10,12},{12,14},{14,16},{16,18},{18... | collective-permute-start | bytes 1572872 | tf_op jit(solution)/shard_map/ppermute | solution.py:50
  15.7 1.2 %copy-start.3 = (bf16[128,4096]{1,0:T(8,128)(2,1)S(1)}, bf16[128,4096]{1,0:T(8,128)(2,1)}, u32[]{:S(2)}) copy-start(bf16[128,4096]{1,0:T(8,128)(2,1)} %inner.3) | copy-start | bytes 3145732
  17.0 1.2 %copy-start.4 = (bf16[128,4096]{1,0:T(8,128)(2,1)S(1)}, bf16[128,4096]{1,0:T(8,128)(2,1)}, u32[]{:S(2)}) copy-start(bf16[128,4096]{1,0:T(8,128)(2,1)} %short_outer.1) | copy-start | bytes 3145732
  18.2 0.9 %copy-start.5 = (f32[256,256]{1,0:T(8,128)S(1)}, f32[256,256]{1,0:T(8,128)}, u32[]{:S(2)}) copy-start(f32[256,256]{1,0:T(8,128)} %constant.31.clone.forward) | copy-start | bytes 786436
  19.1 0.7 copy-start.6
  29.3 9.6 %copy-start.7 = (f32[4096]{0:T(1024)S(1)}, f32[4096]{0:T(1024)}, u32[]{:S(2)}) copy-start(f32[4096]{0:T(1024)} %param.20) | copy-start | bytes 49156
  35.6 8.9 %all-to-all-start = ((bf16[8,32,128]{2,1,0:T(8,128)(2,1)}), bf16[8,32,128]{2,1,0:T(8,128)(2,1)S(1)}, u32[]{:S(2)}, u32[]{:S(2)}) async-start(bf16[8,32,128]{2,1,0:T(8,128)(2,1)} %get-tuple-element.41), calls=%async_computation | async-start | bytes 131072 | tf_op jit(solution)/shard_map/all_to_all | solution.py:432
  45.2 19.4 %all-to-all-start.1 = ((bf16[16,32,128]{2,1,0:T(8,128)(2,1)}), bf16[16,32,128]{2,1,0:T(8,128)(2,1)S(1)}, u32[]{:S(2)}, u32[]{:S(2)}) async-start(bf16[16,32,128]{2,1,0:T(8,128)(2,1)} %get-tuple-element.44), calls=%async_computation.1 | async-start | bytes 262144 | tf_op jit(solution)/shard_map/all_to_all | solution.py:444
  67.3 21.3 %collective-permute-start.6 = (bf16[128,2048]{1,0:T(8,128)(2,1)S(1)}, bf16[128,2048]{1,0:T(8,128)(2,1)S(1)}, u32[]{:S(2)}, u32[]{:S(2)}) collective-permute-start(bf16[128,2048]{1,0:T(8,128)(2,1)S(1)} %get-tuple-element.59), channel_id=1, source_target_pairs={{0,2},{2,4},{4,6},{6,8},{8,10},{10,12},{12,14},{14,16},{16,18},{18... | collective-permute-start | bytes 1572872 | tf_op jit(solution)/shard_map/ppermute | solution.py:50
  72.0 18.2 %collective-permute-start.4 = (bf16[128,2048]{1,0:T(8,128)(2,1)S(1)}, bf16[128,2048]{1,0:T(8,128)(2,1)S(1)}, u32[]{:S(2)}, u32[]{:S(2)}) collective-permute-start(bf16[128,2048]{1,0:T(8,128)(2,1)S(1)} %get-tuple-element.56), channel_id=1, source_target_pairs={{0,2},{2,4},{4,6},{6,8},{8,10},{10,12},{12,14},{14,16},{16,18},{18... | collective-permute-start | bytes 1572872 | tf_op jit(solution)/shard_map/ppermute | solution.py:50
  74.6 14.0 %collective-permute-start.5 = (f32[128,128]{1,0:T(8,128)S(1)}, f32[128,128]{1,0:T(8,128)S(1)}, u32[]{:S(2)}, u32[]{:S(2)}) collective-permute-start(f32[128,128]{1,0:T(8,128)S(1)} %get-tuple-element.58), channel_id=1, source_target_pairs={{0,2},{2,4},{4,6},{6,8},{8,10},{10,12},{12,14},{14,16},{16,18},{18... | collective-permute-start | bytes 196616 | tf_op jit(solution)/shard_map/ppermute | solution.py:50

commit v5 on v4

--- a/solution.py
+++ b/solution.py
@@ -18,8 +18,10 @@
 F32 = jnp.float32
 BF16 = jnp.bfloat16
 SUB = 256
-PARTS = 2
-CHUNKS = 4
+PIECE = 512
+TAIL = (3072, 1024)
+EARLY = 1024
+MIDDLE = 2048
 VMEM = 8 * 2**20
 
 
@@ -55,7 +57,7 @@
     return lax.ppermute(block, "mp", [(m, sides - 1 - m) for m in range(sides)])
 
 
-def call(body, outs, scratch=(), scalars=0, operands=0, flops=10**8, outside=(), kept=()):
+def call(body, outs, scratch=(), scalars=0, operands=0, flops=10**8, outside=(), kept=(), aliases={}):
     specs = [pl.BlockSpec(memory_space=pltpu.SMEM)] * scalars
     specs += [pl.BlockSpec(memory_space=pltpu.VMEM)] * operands
     for k in outside:
@@ -72,6 +74,7 @@
             for k, (shape, kind) in enumerate(outs)
         ],
         scratch_shapes=list(scratch),
+        input_output_aliases=aliases,
         compiler_params=pltpu.CompilerParams(vmem_limit_bytes=VMEM),
         cost_estimate=pl.CostEstimate(flops=flops, transcendentals=0, bytes_accessed=10**6),
     )
@@ -98,12 +101,14 @@
 
 
 def gate_body(stream, inner, gain, v, *sent):
-    share = stream.shape[1] // len(sent)
-    for at in pieces_of(stream.shape[1], 128):
-        value = inner[:, at].astype(F32) * stream[:, at].astype(F32) * gain[:, at]
-        v[:, at] = value.astype(BF16)
-        start = at.start % share
-        sent[at.start // share][:, start : start + 128] = value.astype(BF16)
+    start = 0
+    for block in sent:
+        for to in pieces_of(block.shape[1], 128):
+            at = slice(start + to.start, start + to.stop)
+            value = inner[:, at].astype(F32) * stream[:, at].astype(F32) * gain[:, at]
+            v[:, at] = value.astype(BF16)
+            block[:, to] = value.astype(BF16)
+        start += block.shape[1]
 
 
 def label_body(squares, beside, sent, total, out):
@@ -155,7 +160,7 @@
 
 
 def conv_last(
-    start, before, here, matrix, back, lower, spectrum, gate, decay, earlier, far, copied, rows, summed, sems
+    start, before, here, matrix, back, lower, spectrum, gate, decay, earlier, whole, far, copied, rows, summed, sems
 ):
     conv_body(start, before, here, matrix, back, lower, spectrum, gate, decay, far, rows, summed, sems)
     state = jnp.concatenate([earlier[...], rows[...]], axis=0).astype(BF16)
@@ -168,7 +173,6 @@
 ):
     b = back[...].astype(BF16)
     leaving = []
-    width = before.shape[1] // CHUNKS
     for j, to in enumerate(pieces_of(before.shape[1])):
         at = slice(start + to.start, start + to.stop)
         x = dot(matrix[...], jnp.concatenate([before[:, to], here[:, at]], axis=0))
@@ -180,16 +184,17 @@
         conv = dot(b, jnp.concatenate([y_re, y_im], axis=0))
         z = (gate[:, at] * conv).astype(BF16)
         summed[:, to] = z
+        leaving.append(
+            pltpu.make_async_copy(
+                summed.at[:, pl.ds(to.start, SUB)], far.at[:, pl.ds(at.start, SUB)], sems.at[j]
+            )
+        )
+        leaving[-1].start()
         result = dot(lower[...], z)
         last = result[BLOCK - 1 :] * jnp.exp(decay[:, at] * (1.0 - BLOCK))
         for k in range(SUB // 128):
             row = j * (SUB // 128) + k
             state[row : row + 1, :] = last[:, k * 128 : (k + 1) * 128]
-        if to.stop % width == 0:
-            chunk = to.stop // width - 1
-            at = pl.ds(chunk * width, width)
-            leaving.append(pltpu.make_async_copy(summed.at[:, at], far.at[:, at], sems.at[chunk]))
-            leaving[-1].start()
     for copy in leaving:
         copy.wait()
 
@@ -211,8 +216,31 @@
         copied[k] = group
 
 
+def early_body(summed_far, lower, outer_far, decay, scale, weights, sent, summed, long_outer, *sems):
+    share = summed.shape[1]
+    summed_in = fetches(summed_far, summed, sems[0], 0, PIECE)
+    outer_in = fetches(outer_far, long_outer, sems[1], 0, PIECE)
+    time = times(PIECE)
+    for k, at in enumerate(pieces_of(share, PIECE)):
+        d = decay[:, at]
+        factor = jnp.exp(-d * time) * scale[:, at]
+        summed_in[k].wait()
+        base = dot(lower[...], summed[:, at])
+        outer_in[k].wait()
+        outer = long_outer[:, at].astype(F32) * factor
+        value = (outer * base).astype(BF16)
+        slope = (outer * jnp.exp(-d)).astype(BF16)
+        for j, to in enumerate(pieces_of(PIECE, HEAD_DIM)):
+            head = at.start // HEAD_DIM + j
+            both = dot(weights[head], jnp.concatenate([value[:, to], slope[:, to]], axis=1))
+            low = head * HEAD_DIM
+            high = share + low
+            sent[:, low : low + HEAD_DIM] = both[:, :HEAD_DIM].astype(BF16)
+            sent[:, high : high + HEAD_DIM] = both[:, HEAD_DIM:].astype(BF16)
+
+
 def finish_body(
-    part,
+    start,
     near_size,
     place,
     others,
@@ -225,39 +253,41 @@
     scale,
     weights,
     mixed,
-    ahead,
-    summed,
-    long_outer,
-    summed_sems,
-    outer_sems,
+    *rest,
 ):
-    width = long_outer.shape[1] // CHUNKS
-    summed_in = fetches(summed_far, summed, summed_sems, 0, width)
-    outer_in = fetches(outer_far, long_outer, outer_sems, part * long_outer.shape[1], width)
+    summed, long_outer, summed_sems, outer_sems = rest[-4:]
+    summed_in = fetches(summed_far, summed, summed_sems, start, PIECE)
+    outer_in = fetches(outer_far, long_outer, outer_sems, start, PIECE)
     near, far = place[0], place[1]
-    lanes = others.shape[1] // PARTS
-    some = slice(part * lanes, (part + 1) * lanes)
-    r = rate[some]
-    carry = inside[some] + jnp.exp(-r * near.astype(F32)) * weighted(
-        others, far, r * near_size, some
-    )
-    time = times(width)
-    group = width // HEAD_DIM
-    for k in range(CHUNKS):
-        to = slice(k * width, (k + 1) * width)
-        at = slice(part * lanes * HEAD_DIM + to.start, part * lanes * HEAD_DIM + to.stop)
+    r = rate[...]
+    carry = inside[...] + jnp.exp(-r * near.astype(F32)) * weighted(others, far, r * near_size)
+    time = times(PIECE)
+    for k, to in enumerate(pieces_of(mixed.shape[1], PIECE)):
+        at = slice(start + to.start, start + to.stop)
         d = decay[:, at]
-        entering = jnp.concatenate(
-            [carry[j : j + 1] for j in range(k * group, (k + 1) * group)], axis=1
-        ) * jnp.exp(-d)
+        heads = range(at.start // HEAD_DIM, at.stop // HEAD_DIM)
+        entering = jnp.concatenate([carry[j : j + 1] for j in heads], axis=1) * jnp.exp(-d)
         factor = jnp.exp(-d * time) * scale[:, at]
         summed_in[k].wait()
         base = dot(lower[...], summed[:, to]) + entering
         outer_in[k].wait()
         mixed[:, to] = (long_outer[:, to].astype(F32) * factor * base).astype(BF16)
-    for j in range(lanes):
-        to = slice(j * HEAD_DIM, (j + 1) * HEAD_DIM)
-        ahead[:, to] = dot(weights[part * lanes + j], mixed[:, to]).astype(BF16)
+    if start == 0:
+        return
+    ahead = rest[0]
+    for j, to in enumerate(pieces_of(mixed.shape[1], HEAD_DIM)):
+        head = start // HEAD_DIM + j
+        ahead[:BLOCK, to] = dot(weights[head], mixed[:, to]).astype(BF16)
+    if ahead.shape[0] > BLOCK:
+        row = lax.broadcasted_iota(jnp.int32, (16, HEAD_DIM), 0)
+        for j, to in enumerate(pieces_of(EARLY, HEAD_DIM)):
+            left = carry[j : j + 1]
+            kept = jnp.zeros((16, HEAD_DIM), F32)
+            for k in range(3):
+                term = left.astype(BF16).astype(F32)
+                left = left - term
+                kept = jnp.where(row == k, term, kept)
+            ahead[BLOCK:, to] = kept.astype(BF16)
 
 
 def score(query, key):
@@ -284,7 +314,7 @@
 
 
 def own_body(query_far, key_far, weights, stats, query, key, query_sems, key_sems):
-    width = key.shape[1] // CHUNKS
+    width = 2 * PIECE
     arriving = [
         pair
         for pair in zip(
@@ -309,7 +339,7 @@
 
 
 def ahead_body(query, key_far, weights, stats, key, sems):
-    width = key.shape[1] // CHUNKS
+    width = 2 * PIECE
     arriving = fetches(key_far, key, sems, 0, width)
     lane = lax.broadcasted_iota(jnp.int32, (BLOCK, BLOCK), 1)
     tops = jnp.zeros((BLOCK, BLOCK), F32)
@@ -325,15 +355,7 @@
     stats[...] = jnp.where(lane < BLOCK // 2, tops, sizes)
 
 
-def here_body(part, weights, mixed, partial):
-    heads = partial.shape[1] // HEAD_DIM
-    for j in range(heads):
-        at = slice(j * HEAD_DIM, (j + 1) * HEAD_DIM)
-        partial[:, at] = dot(weights[part * heads + j], mixed[:, at])
-
-
-def join_body(part, partial, before, stats_here, stats_before, *rest):
-    attended = rest[-1]
+def here_body(weights, first, middle, last, stats_here, stats_before, early, base, slope, share):
     top, size = stats_here[...], pltpu.roll(stats_here[...], BLOCK // 2, 1)
     size_b = pltpu.roll(stats_before[...], BLOCK // 2, 1)
     top_b = jnp.where(size_b > 0.0, stats_before[...], -1e30)
@@ -341,35 +363,63 @@
     scale = jnp.exp(top - highest)
     scale_b = size_b * jnp.exp(top_b - highest)
     whole = 1.0 / (size * scale + scale_b)
-    own, share = scale * whole, scale_b * whole
-    heads = partial.shape[1] // HEAD_DIM
-    for j in range(heads):
-        at = slice(j * HEAD_DIM, (j + 1) * HEAD_DIM)
-        head = part * heads + j
-        attended[:, at] = (
-            partial[:, at] * own[:, head : head + 1]
-            + share[:, head : head + 1] * before[:, at].astype(F32)
-        ).astype(BF16)
+    own, other = scale * whole, scale_b * whole
+    share[...] = other
+    start = 0
+    for block in (first, middle, last):
+        for to in pieces_of(block.shape[1], HEAD_DIM):
+            at = slice(start + to.start, start + to.stop)
+            j = at.start // HEAD_DIM
+            part = dot(weights[j], block[:, to]) * own[:, j : j + 1]
+            if start == 0:
+                column = other[:, j : j + 1]
+                part = part + column * early[:, to].astype(F32)
+                up = slice(EARLY + to.start, EARLY + to.stop)
+                slope[:, to] = column * early[:, up].astype(F32)
+            base[:, at] = part
+        start += block.shape[1]
+
+
+def join_body(base, slope, share, before, last, attended, out, sems):
+    leaving = []
+    for k, at in enumerate(pieces_of(base.shape[1], PIECE)):
+        for to in pieces_of(PIECE, HEAD_DIM):
+            to = slice(at.start + to.start, at.start + to.stop)
+            j = to.start // HEAD_DIM
+            if to.start < EARLY:
+                terms = before[BLOCK:, to].astype(F32)
+                state = (terms[:1] + terms[1:2]) + terms[2:3]
+                more = slope[:, to] * state
+            elif to.start < MIDDLE:
+                of = slice(to.start - EARLY, to.stop - EARLY)
+                more = share[:, j : j + 1] * before[:BLOCK, of].astype(F32)
+            else:
+                of = slice(to.start - MIDDLE, to.stop - MIDDLE)
+                more = share[:, j : j + 1] * last[:, of].astype(F32)
+            out[:, to] = (base[:, to] + more).astype(BF16)
+        at = pl.ds(at.start, PIECE)
+        leaving.append(pltpu.make_async_copy(out.at[:, at], attended.at[:, at], sems.at[k]))
+        leaving[-1].start()
+    for copy in leaving:
+        copy.wait()
 
 
 def copy_body(block, *rest):
     rest[-1][...] = block[...]
 
 
-def into(body, part, operands, whole, width):
-    rows = operands[0].shape[0]
-    share = width // PARTS
-    specs = [pl.BlockSpec(x.shape, lambda i: (0, 0)) for x in operands]
-    aliases = {}
+def into(body, index, block, whole, width):
+    rows, share = block.shape
+    specs = [pl.BlockSpec((rows, share), lambda i: (0, 0))]
+    operands, aliases = (block,), {}
     if whole is not None:
         specs.append(pl.BlockSpec(memory_space=pl.ANY))
-        aliases = {len(operands): 0}
-        operands = (*operands, whole)
+        operands, aliases = (block, whole), {1: 0}
     return pl.pallas_call(
         body,
         grid=(1,),
         in_specs=specs,
-        out_specs=pl.BlockSpec((rows, share), lambda i: (0, part)),
+        out_specs=pl.BlockSpec((rows, share), lambda i: (0, index)),
         out_shape=jax.ShapeDtypeStruct((rows, width), BF16),
         input_output_aliases=aliases,
         compiler_params=pltpu.CompilerParams(vmem_limit_bytes=VMEM),
@@ -400,64 +450,70 @@
     square = ((rows, rows), F32)
     wide, wide_float = ((rows, width), BF16), ((rows, width), F32)
 
-    half = ((rows, width // PARTS), BF16)
-    some = lanes // PARTS
     (squares,) = call(squares_body, [((1, rows), F32)], operands=1)(stream)
     beside = swapped(squares)
-    v, *sent = call(gate_body, [wide] + [half] * PARTS, operands=3)(
+    v, *sent = call(gate_body, [wide] + [((rows, share), BF16) for share in TAIL], operands=3)(
         stream, short_inner, norm_gain[None]
     )
     total, sent[0] = label(squares, beside, sent[0])
     v_before = []
-    for part in range(PARTS):
+    for part in range(len(TAIL)):
         v_before.append(shifted(sent[part], SEQ, 1))
     queries, total = lax.optimization_barrier((query_heads, total))
     query_next = shifted(queries, SEQ, -1)
     spectrum, gate = call(
         tables_body, [((2 * rows, width), F32), wide_float], operands=5
     )(forward, short_filter, long_inner, short_outer, decay)
-    some_state = ((some, 128), F32)
-    leaving = [pltpu.VMEM((rows, width // PARTS), BF16), pltpu.SemaphoreType.DMA((CHUNKS,))]
-    first, early, matrix = call(
-        conv_first, [half, some_state, ((2 * rows, 2 * rows), BF16)], leaving, operands=9, kept=(0,)
-    )(v_before[0], v, total, forward, back, lower, spectrum, gate, decay)
-    last, state = call(
-        functools.partial(conv_last, width // PARTS),
-        [half, ((near_size, lanes, 128), BF16)],
-        [pltpu.VMEM((some, 128), F32), *leaving],
+
+    def leaving(share):
+        return [pltpu.VMEM((rows, share), BF16), pltpu.SemaphoreType.DMA((share // SUB,))]
+
+    summed, state, matrix = call(
+        conv_first,
+        [wide, ((TAIL[0] // 128, 128), F32), ((2 * rows, 2 * rows), BF16)],
+        leaving(TAIL[0]),
         operands=9,
         kept=(0,),
-    )(v_before[1], v, matrix, back, lower, spectrum, gate, decay, early)
-    summed = [first, last]
+    )(v_before[0], v, total, forward, back, lower, spectrum, gate, decay)
+    summed, state = call(
+        functools.partial(conv_last, TAIL[0]),
+        [wide, ((near_size, lanes, 128), BF16)],
+        [pltpu.VMEM((TAIL[1] // 128, 128), F32), *leaving(TAIL[1])],
+        operands=10,
+        outside=(9,),
+        kept=(0,),
+        aliases={9: 0},
+    )(v_before[1], v, matrix, back, lower, spectrum, gate, decay, state, summed)
     pieces = lax.all_to_all(state, NEAR, 0, 0, tiled=True)
-    weights_here, stats_here = call(
-        own_body,
+    weights_next, stats_next = call(
+        ahead_body,
         [((heads, rows, rows), BF16), square],
-        [pltpu.VMEM((rows, width), BF16)] * 2 + [pltpu.SemaphoreType.DMA((CHUNKS,))] * 2,
+        [pltpu.VMEM((rows, width), BF16), pltpu.SemaphoreType.DMA((width // PIECE // 2,))],
         operands=2,
-        outside=(0, 1),
-    )(in_hbm(query_heads), in_hbm(key_heads))
-    pieces, stats_here = lax.optimization_barrier((pieces, stats_here))
+        outside=(1,),
+    )(query_next, in_hbm(key_heads))
+    pieces, stats_next = lax.optimization_barrier((pieces, stats_next))
     inside, group = call(
         near_body, [((lanes, 128), F32), ((far_size, lanes, 128), BF16)], scalars=1, operands=2
     )(near[None], pieces, rate)
     others = lax.all_to_all(group, FAR, 0, 0, tiled=True)
-    query_next, keys, inside = lax.optimization_barrier((query_next, key_heads, inside))
-    weights_next, stats_next = call(
-        ahead_body,
-        [((heads, rows, rows), BF16), square],
-        [pltpu.VMEM((rows, width), BF16), pltpu.SemaphoreType.DMA((CHUNKS,))],
-        operands=2,
-        outside=(1,),
-    )(query_next, in_hbm(keys))
+
+    def fetching(share):
+        space = [pltpu.VMEM((rows, share), BF16)] * 2
+        return space + [pltpu.SemaphoreType.DMA((share // PIECE,))] * 2
+
+    summed, inside = lax.optimization_barrier((summed, inside))
+    (early,) = call(
+        early_body, [((rows, 2 * EARLY), BF16)], fetching(EARLY), operands=6, outside=(0, 2)
+    )(in_hbm(summed), lower, in_hbm(long_outer), decay, scale, weights_next)
+    early = shifted(early, SEQ, 1)
     stats_before = shifted(stats_next, SEQ, 1)
-    mixed, arrived = [], []
-    for part in range(PARTS):
-        block, ready = call(
-            functools.partial(finish_body, part, float(near_size)),
-            [half, half],
-            [pltpu.VMEM((rows, width // PARTS), BF16)] * 2
-            + [pltpu.SemaphoreType.DMA((CHUNKS,))] * 2,
+
+    def finish(start, stop, extra):
+        return call(
+            functools.partial(finish_body, start, float(near_size)),
+            [((rows, stop - start), BF16), *extra],
+            fetching(stop - start),
             scalars=1,
             operands=9,
             outside=(4, 6),
@@ -466,28 +522,43 @@
             others,
             inside,
             rate,
-            in_hbm(summed[part]),
+            in_hbm(summed),
             lower,
             in_hbm(long_outer),
             decay,
             scale,
             weights_next,
         )
-        mixed.append(block)
-        arrived.append(shifted(ready, SEQ, 1))
-    attended = values = None
-    for part in range(PARTS):
-        (partial,) = call(
-            functools.partial(here_body, part), [((rows, width // PARTS), F32)], operands=2
-        )(weights_here, mixed[part])
-        values = into(copy_body, part, (mixed[part],), values, width)
-        attended = into(
-            functools.partial(join_body, part),
-            part,
-            (partial, arrived[part], stats_here, stats_before),
-            attended,
-            width,
-        )
+
+    middle, ready = finish(EARLY, MIDDLE, [((rows + 16, MIDDLE - EARLY), BF16)])
+    arrived = shifted(ready, SEQ, 1)
+    others, middle = lax.optimization_barrier((others, middle))
+    last, ready = finish(MIDDLE, width, [((rows, width - MIDDLE), BF16)])
+    arrived_last = shifted(ready, SEQ, 1)
+    others, last = lax.optimization_barrier((others, last))
+    (first,) = finish(0, EARLY, [])
+    values = into(copy_body, 0, first, None, width)
+    values = into(copy_body, EARLY // (MIDDLE - EARLY), middle, values, width)
+    values = into(copy_body, MIDDLE // (width - MIDDLE), last, values, width)
+    query_own, key_own, last = lax.optimization_barrier((query_heads, key_heads, last))
+    weights_here, stats_here = call(
+        own_body,
+        [((heads, rows, rows), BF16), square],
+        [pltpu.VMEM((rows, width), BF16)] * 2
+        + [pltpu.SemaphoreType.DMA((width // PIECE // 2,))] * 2,
+        operands=2,
+        outside=(0, 1),
+    )(in_hbm(query_own), in_hbm(key_own))
+    base, slope, share = call(
+        here_body, [wide_float, ((rows, EARLY), F32), square], operands=7
+    )(weights_here, first, middle, last, stats_here, stats_before, early)
+    (attended,) = call(
+        join_body,
+        [wide],
+        [pltpu.VMEM((rows, width), BF16), pltpu.SemaphoreType.DMA((width // PIECE,))],
+        operands=5,
+        kept=(0,),
+    )(base, slope, share, arrived, arrived_last)
     return (values, attended)
 
 

time: 92.5 us -> 91.4 us (0.988)
  waiting for transfers between devices: 27.3 us -> 24.2 us
  local copies, waits for them, and re-layouts: 7.29 us -> 4.41 us
  Pallas kernels: 25.4 us -> 27.8 us
  starting transfers between devices: 30.8 us -> 33 us
    pallas_call x7 -> x9, Pallas kernels: 11.9 us -> 16.8 us  [the longest x3 6.85 us: finish(): call(functools.partial(finish_body, start, float(near_size)), [((rows, st...]
    unnamed x22 -> x20, local copies, waits for them, and re-layouts: 7.29 us -> 4.41 us
    ppermute x6 -> x7, waiting for transfers between devices: 18.7 us -> 16.1 us  [shifted(): lax.ppermute(block, axis, [(i, i + distance) for i in range(size) if 0 <=...]
    pallas_call x4 -> x3, Pallas kernels: 4.75 us -> 2.27 us  [into(): pl.pallas_call(body, grid=(1,), in_specs=specs, out_specs=pl.BlockSpec((r...]
    ppermute x6 -> x7, starting transfers between devices: 16.1 us -> 18.3 us  [shifted(): lax.ppermute(block, axis, [(i, i + distance) for i in range(size) if 0 <=...]
  transfers between devices with their start and end apart: 9 -> 10, of which waited for: 5 -> 4; matrix products, arithmetic and copies ran while one was open for 0% -> 0% of each run, Pallas kernels for 23% -> 28%
where the time goes in v5:
time: 91.4 us; the launch traced here: 90.6 us
  starting transfers between devices  33 us (36%)
  Pallas kernels  27.8 us (30%)
  waiting for transfers between devices  24.2 us (26%)
  local copies, waits for them, and re-layouts  4.41 us (5%)
  between operations  1.07 us (1%)
    ppermute x7, starting transfers between devices, shifted(): lax.ppermute(block, axis, [(i, i + distance) for i in range(size) if 0 <=...  18.3 us
    ppermute x7, waiting for transfers between devices, shifted(): lax.ppermute(block, axis, [(i, i + distance) for i in range(size) if 0 <=...  16.1 us
    all_to_all x1, starting transfers between devices, on_device(): others = lax.all_to_all(group, FAR, 0, 0, tiled=True)  9.8 us
    pallas_call x3, Pallas kernels, finish(): call(functools.partial(finish_body, start, float(near_size)), [((rows, st...  6.85 us
    all_to_all x1, waiting for transfers between devices, on_device(): others = lax.all_to_all(group, FAR, 0, 0, tiled=True)  5.8 us
    unnamed x20, local copies, waits for them, and re-layouts  4.41 us
    all_to_all x1, starting transfers between devices, on_device(): pieces = lax.all_to_all(state, NEAR, 0, 0, tiled=True)  3.36 us
    pallas_call x1, Pallas kernels, on_device(): call(own_body, [((heads, rows, rows), BF16), square], [pltpu.VMEM((rows,...  3.26 us
  transfers between devices with their start and end apart: 10, of which 4 were waited for; matrix products, arithmetic and copies ran while one was open for 0% of the time, Pallas kernels for 28%

profile of v5, /device:TPU:32, one launch (start us, length us, event | category | flops | bytes accessed | tf_op | source)
XLA Modules:
  0.0 90.6 jit_solution(896451290166973638)
XLA Ops:
  0.6 0.0 copy-start
  0.6 1.2 %copy-done = bf16[128,4096]{1,0:T(8,128)(2,1)S(1)} copy-done((bf16[128,4096]{1,0:T(8,128)(2,1)S(1)}, bf16[128,4096]{1,0:T(8,128)(2,1)}, u32[]{:S(2)}) %copy-start) | copy-done | bytes 1048600
  1.9 0.0 copy-start.2
  1.9 0.0 copy-start.7
  1.9 0.3 shard_map.141.squares
  2.2 1.6 %collective-permute-start.1 = (f32[1,128]{1,0:T(1,128)S(1)}, f32[1,128]{1,0:T(1,128)S(1)}, u32[]{:S(2)}, u32[]{:S(2)}) collective-permute-start(f32[1,128]{1,0:T(1,128)S(1)} %shard_map.141.squares), channel_id=1, source_target_pairs={{0,1},{1,0},{2,3},{3,2},{4,5},{5,4},{6,7},{7,6},{8,9},{9,8},{10,11... | collective-permute-start | bytes 1544 | tf_op jit(solution)/shard_map/ppermute | solution.py:57
  3.7 0.0 copy-start.3
  3.7 1.2 %copy-done.3 = bf16[128,4096]{1,0:T(8,128)(2,1)S(1)} copy-done((bf16[128,4096]{1,0:T(8,128)(2,1)S(1)}, bf16[128,4096]{1,0:T(8,128)(2,1)}, u32[]{:S(2)}) %copy-start.3) | copy-done | bytes 1048600
  5.0 0.0 copy-start.9
  5.0 0.7 copy-done.9
  5.7 0.0 copy-start.4
  5.7 0.0 copy-start.5
  5.7 0.5 shard_map.140
  6.2 0.0 collective-permute-done.1.beside
  6.2 0.0 copy-start.1
  6.2 0.0 copy-start.8
  6.3 5.9 %collective-permute-start.3 = (bf16[128,4096]{1,0:T(8,128)(2,1)}, bf16[128,4096]{1,0:T(8,128)(2,1)S(1)}, u32[]{:S(2)}, u32[]{:S(2)}) collective-permute-start(bf16[128,4096]{1,0:T(8,128)(2,1)} %query_far), channel_id=1, source_target_pairs={{2,0},{4,2},{6,4},{8,6},{10,8},{12,10},{14,12},{16,14},{18,16},{20... | collective-permute-start | bytes 3145736 | tf_op jit(solution)/shard_map/ppermute | solution.py:52
  12.2 1.9 %collective-permute-start.2 = (bf16[128,3072]{1,0:T(8,128)(2,1)S(1)}, bf16[128,3072]{1,0:T(8,128)(2,1)S(1)}, u32[]{:S(2)}, u32[]{:S(2)}) collective-permute-start(bf16[128,3072]{1,0:T(8,128)(2,1)S(1)} %get-tuple-element.43), channel_id=1, source_target_pairs={{0,2},{2,4},{4,6},{6,8},{8,10},{10,12},{12,14},{14,16},{16,18},{18... | collective-permute-start | bytes 2359304 | tf_op jit(solution)/shard_map/ppermute | solution.py:52
  14.1 1.9 %collective-permute-start = (bf16[128,1024]{1,0:T(8,128)(2,1)S(1)}, bf16[128,1024]{1,0:T(8,128)(2,1)S(1)}, u32[]{:S(2)}, u32[]{:S(2)}) collective-permute-start(bf16[128,1024]{1,0:T(8,128)(2,1)S(1)} %get-tuple-element.40), channel_id=1, source_target_pairs={{0,2},{2,4},{4,6},{6,8},{8,10},{10,12},{12,14},{14,16},{16,18},{18... | collective-permute-start | bytes 786440 | tf_op jit(solution)/shard_map/ppermute | solution.py:52
  16.0 0.0 copy-done.2
  16.1 0.0 copy-done.7
  16.1 0.0 copy-done.4
  16.1 0.0 copy-done.5
  16.1 0.0 copy-start.6
  16.1 1.2 %copy-done.6 = bf16[128,4096]{1,0:T(8,128)(2,1)S(1)} copy-done((bf16[128,4096]{1,0:T(8,128)(2,1)S(1)}, bf16[128,4096]{1,0:T(8,128)(2,1)}, u32[]{:S(2)}) %copy-start.6) | copy-done | bytes 1048600
  17.3 1.3 %shard_map.142 = (f32[256,4096]{1,0:T(8,128)S(1)}, f32[128,4096]{1,0:T(8,128)S(1)}) custom-call(f32[256,256]{1,0:T(8,128)S(1)} %copy-done.7, bf16[128,4096]{1,0:T(8,128)(2,1)S(1)} %copy-done.4, bf16[128,4096]{1,0:T(8,128)(2,1)S(1)} %copy-done.5, bf16[128,4096]{1,0:T(8,128)(2,1)S(1)} %copy-done.6, f32[1,4096]{1,0:T(1,128)S(1)} %bitcast.7), custom_call_target="tpu_custom_call" | custom-call | flops 100000000 | bytes 1000000 | tf_op jit(solution)/shard_map/pallas_call | solution.py:464
  18.6 11.4 %collective-permute-done.2.before = bf16[128,3072]{1,0:T(8,128)(2,1)S(1)} collective-permute-done((bf16[128,3072]{1,0:T(8,128)(2,1)S(1)}, bf16[128,3072]{1,0:T(8,128)(2,1)S(1)}, u32[]{:S(2)}, u32[]{:S(2)}) %collective-permute-start.2) | collective-permute-done | bytes 786464 | tf_op jit(solution)/shard_map/ppermute | solution.py:52
  30.0 0.0 copy-done.1
  30.0 0.0 copy-done.8
  30.0 3.2 %shard_map.143 = (bf16[128,4096]{1,0:T(8,128)(2,1)}, f32[24,128]{1,0:T(8,128)S(1)}, bf16[256,256]{1,0:T(8,128)(2,1)S(1)}) custom-call(bf16[128,3072]{1,0:T(8,128)(2,1)S(1)} %collective-permute-done.2.before, bf16[128,4096]{1,0:T(8,128)(2,1)S(1)} %get-tuple-element.41.here, f32[1,128]{1,0:T(1,128)S(1)} %get-tuple-element.45.squares, ...), custom_call_target="tpu_custom_call" | custom-call | flops 100000000 | bytes 1000000 | tf_op jit(solution)/shard_map/pallas_call | solution.py:471
  33.2 0.0 collective-permute-done.before
  33.2 2.2 %shard_map.144 = (bf16[128,4096]{1,0:T(8,128)(2,1)}, bf16[8,32,128]{2,1,0:T(8,128)(2,1)}) custom-call(bf16[128,1024]{1,0:T(8,128)(2,1)S(1)} %collective-permute-done.before, bf16[128,4096]{1,0:T(8,128)(2,1)S(1)} %get-tuple-element.41.here, bf16[256,256]{1,0:T(8,128)(2,1)S(1)} %get-tuple-element.48.matrix, ...), custom_call_target="tpu_custom_call", output_to_operand_aliasing={{0}: (9, {})} | custom-call | flops 100000000 | bytes 1000000 | tf_op jit(solution)/shard_map/pallas_call | solution.py:478
  35.5 3.4 %all-to-all-start = ((bf16[8,32,128]{2,1,0:T(8,128)(2,1)}), bf16[8,32,128]{2,1,0:T(8,128)(2,1)S(1)}, u32[]{:S(2)}, u32[]{:S(2)}) async-start(bf16[8,32,128]{2,1,0:T(8,128)(2,1)} %get-tuple-element.51), calls=%async_computation | async-start | bytes 131072 | tf_op jit(solution)/shard_map/all_to_all | solution.py:487
  38.9 0.0 collective-permute-done.3.query
  38.9 3.2 %shard_map.145 = (bf16[32,128,128]{2,1,0:T(8,128)(2,1)S(1)}, f32[128,128]{1,0:T(8,128)S(1)}) custom-call(bf16[128,4096]{1,0:T(8,128)(2,1)S(1)} %collective-permute-done.3.query, bf16[128,4096]{1,0:T(8,128)(2,1)} %key_far.2), custom_call_target="tpu_custom_call" | custom-call | flops 100000000 | bytes 1000000 | tf_op jit(solution)/shard_map/pallas_call | solution.py:488
  42.1 2.3 %all-to-all-done.pieces = bf16[8,32,128]{2,1,0:T(8,128)(2,1)S(1)} async-done(((bf16[8,32,128]{2,1,0:T(8,128)(2,1)}), bf16[8,32,128]{2,1,0:T(8,128)(2,1)S(1)}, u32[]{:S(2)}, u32[]{:S(2)}) %all-to-all-start) | async-done | bytes 65568 | tf_op jit(solution)/shard_map/all_to_all | solution.py:487
  44.4 0.7 shard_map.146
  45.1 9.8 %all-to-all-start.1 = ((bf16[16,32,128]{2,1,0:T(8,128)(2,1)}), bf16[16,32,128]{2,1,0:T(8,128)(2,1)S(1)}, u32[]{:S(2)}, u32[]{:S(2)}) async-start(bf16[16,32,128]{2,1,0:T(8,128)(2,1)} %get-tuple-element.55), calls=%async_computation.1 | async-start | bytes 262144 | tf_op jit(solution)/shard_map/all_to_all | solution.py:499
  54.9 0.1 pad_add_fusion.place
  54.9 1.8 %shard_map.154 = bf16[128,2048]{1,0:T(8,128)(2,1)S(1)} custom-call(bf16[128,4096]{1,0:T(8,128)(2,1)} %get-tuple-element.59.summed_far, bf16[128,128]{1,0:T(8,128)(2,1)S(1)} %copy-done.1, bf16[128,4096]{1,0:T(8,128)(2,1)} %outer_far.7, f32[1,4096]{1,0:T(1,128)S(1)} %bitcast.10, f32[1,4096]{1,0:T(1,128)S(1)} %bitcast.14, ...), custom_call_target="tpu_custom_call" | custom-call | flops 100000000 | bytes 1000000 | tf_op jit(solution)/shard_map/pallas_call | solution.py:506
  56.7 1.9 %collective-permute-start.5 = (bf16[128,2048]{1,0:T(8,128)(2,1)S(1)}, bf16[128,2048]{1,0:T(8,128)(2,1)S(1)}, u32[]{:S(2)}, u32[]{:S(2)}) collective-permute-start(bf16[128,2048]{1,0:T(8,128)(2,1)S(1)} %shard_map.154), channel_id=1, source_target_pairs={{0,2},{2,4},{4,6},{6,8},{8,10},{10,12},{12,14},{14,16},{16,18},{18... | collective-permute-start | bytes 1572872 | tf_op jit(solution)/shard_map/ppermute | solution.py:52
  58.7 5.8 %all-to-all-done.1.others = bf16[16,32,128]{2,1,0:T(8,128)(2,1)S(1)} async-done(((bf16[16,32,128]{2,1,0:T(8,128)(2,1)}), bf16[16,32,128]{2,1,0:T(8,128)(2,1)S(1)}, u32[]{:S(2)}, u32[]{:S(2)}) %all-to-all-start.1) | async-done | bytes 131104 | tf_op jit(solution)/shard_map/all_to_all | solution.py:499
  64.5 2.1 %shard_map.147 = (bf16[128,1024]{1,0:T(8,128)(2,1)S(1)}, bf16[144,1024]{1,0:T(8,128)(2,1)S(1)}) custom-call(s32[2]{0:T(128)S(1)} %pad_add_fusion.place, bf16[16,32,128]{2,1,0:T(8,128)(2,1)S(1)} %all-to-all-done.1.others, f32[32,128]{1,0:T(8,128)S(1)} %get-tuple-element.58.inside, f32[32,128]{1,0:T(8,128)S(1)} %get-tuple-element.79.rate, ...), custom_call_target="tpu_custom_call" | custom-call | flops 100000000 | bytes 1000000 | tf_op jit(solution)/shard_map/pallas_call | solution.py:513
  66.6 2.8 %shard_map.148 = (bf16[128,2048]{1,0:T(8,128)(2,1)S(1)}, bf16[128,2048]{1,0:T(8,128)(2,1)S(1)}) custom-call(s32[2]{0:T(128)S(1)} %pad_add_fusion.place, bf16[16,32,128]{2,1,0:T(8,128)(2,1)S(1)} %all-to-all-done.1.others, f32[32,128]{1,0:T(8,128)S(1)} %get-tuple-element.58.inside, f32[32,128]{1,0:T(8,128)S(1)} %get-tuple-element.79.rate, ...), custom_call_target="tpu_custom_call" | custom-call | flops 100000000 | bytes 1000000 | tf_op jit(solution)/shard_map/pallas_call | solution.py:513
  69.4 1.9 %collective-permute-start.7 = (bf16[128,2048]{1,0:T(8,128)(2,1)S(1)}, bf16[128,2048]{1,0:T(8,128)(2,1)S(1)}, u32[]{:S(2)}, u32[]{:S(2)}) collective-permute-start(bf16[128,2048]{1,0:T(8,128)(2,1)S(1)} %get-tuple-element.77), channel_id=1, source_target_pairs={{0,2},{2,4},{4,6},{6,8},{8,10},{10,12},{12,14},{14,16},{16,18},{18... | collective-permute-start | bytes 1572872 | tf_op jit(solution)/shard_map/ppermute | solution.py:52
  71.3 2.6 %collective-permute-start.6 = (bf16[144,1024]{1,0:T(8,128)(2,1)S(1)}, bf16[144,1024]{1,0:T(8,128)(2,1)S(1)}, u32[]{:S(2)}, u32[]{:S(2)}) collective-permute-start(bf16[144,1024]{1,0:T(8,128)(2,1)S(1)} %get-tuple-element.76), channel_id=1, source_target_pairs={{0,2},{2,4},{4,6},{6,8},{8,10},{10,12},{12,14},{14,16},{16,18},{18... | collective-permute-start | bytes 884744 | tf_op jit(solution)/shard_map/ppermute | solution.py:52
  73.9 2.1 %collective-permute-start.4 = (f32[128,128]{1,0:T(8,128)S(1)}, f32[128,128]{1,0:T(8,128)S(1)}, u32[]{:S(2)}, u32[]{:S(2)}) collective-permute-start(f32[128,128]{1,0:T(8,128)S(1)} %get-tuple-element.72), channel_id=1, source_target_pairs={{0,2},{2,4},{4,6},{6,8},{8,10},{10,12},{12,14},{14,16},{16,18},{18... | collective-permute-start | bytes 196616 | tf_op jit(solution)/shard_map/ppermute | solution.py:52
  76.0 1.9 %shard_map.149.block.first = bf16[128,1024]{1,0:T(8,128)(2,1)S(1)} custom-call(s32[2]{0:T(128)S(1)} %pad_add_fusion.place, bf16[16,32,128]{2,1,0:T(8,128)(2,1)S(1)} %all-to-all-done.1.others, f32[32,128]{1,0:T(8,128)S(1)} %get-tuple-element.58.inside, f32[32,128]{1,0:T(8,128)S(1)} %get-tuple-element.79.rate, bf16[128,4096]{1,0:T(8,128)(2,1)} %get-tuple-element.59.summed_far, ...), custom_call_target="tpu_custom_call" | custom-call | flops 100000000 | bytes 1000000 | tf_op jit(solution)/shard_map/pallas_call | solution.py:513
  78.0 0.7 shard_map.150.rest_0_
  78.7 0.7 shard_map.151.rest_0_
  79.4 0.8 shard_map.152
  80.2 3.3 %shard_map.153 = (bf16[32,128,128]{2,1,0:T(8,128)(2,1)S(1)}, f32[128,128]{1,0:T(8,128)S(1)}) custom-call(bf16[128,4096]{1,0:T(8,128)(2,1)} %query_far, bf16[128,4096]{1,0:T(8,128)(2,1)} %key_far.2), custom_call_target="tpu_custom_call" | custom-call | flops 100000000 | bytes 1000000 | tf_op jit(solution)/shard_map/pallas_call | solution.py:544
  83.5 4.8 %collective-permute-done.4.stats_before = f32[128,128]{1,0:T(8,128)S(1)} collective-permute-done((f32[128,128]{1,0:T(8,128)S(1)}, f32[128,128]{1,0:T(8,128)S(1)}, u32[]{:S(2)}, u32[]{:S(2)}) %collective-permute-start.4) | collective-permute-done | bytes 65568 | tf_op jit(solution)/shard_map/ppermute | solution.py:52
  88.3 0.0 collective-permute-done.5.early
  88.3 0.9 %shard_map.155 = (f32[128,4096]{1,0:T(8,128)S(1)}, f32[128,1024]{1,0:T(8,128)S(1)}, f32[128,128]{1,0:T(8,128)S(1)}) custom-call(bf16[32,128,128]{2,1,0:T(8,128)(2,1)S(1)} %get-tuple-element.69.weights, bf16[128,1024]{1,0:T(8,128)(2,1)S(1)} %shard_map.149.block.first, bf16[128,1024]{1,0:T(8,128)(2,1)S(1)} %get-tuple-element.65.block.middle, ...), custom_call_target="tpu_custom_call" | custom-call | flops 100000000 | bytes 1000000 | tf_op jit(solution)/shard_map/pallas_call | solution.py:552
  89.2 0.0 collective-permute-done.6.before
  89.2 0.0 collective-permute-done.7.last
  89.2 1.3 %shard_map.156 = bf16[128,4096]{1,0:T(8,128)(2,1)} custom-call(f32[128,4096]{1,0:T(8,128)S(1)} %get-tuple-element.73.base, f32[128,1024]{1,0:T(8,128)S(1)} %get-tuple-element.74.slope, f32[128,128]{1,0:T(8,128)S(1)} %get-tuple-element.75.share, bf16[144,1024]{1,0:T(8,128)(2,1)S(1)} %collective-permute-done.6.before, ...), custom_call_target="tpu_custom_call" | custom-call | flops 100000000 | bytes 1000000 | tf_op jit(solution)/shard_map/pallas_call | solution.py:555
  (2 shorter events, 0.0 us)
Async XLA Ops:
  0.6 1.2 %copy-start = (bf16[128,4096]{1,0:T(8,128)(2,1)S(1)}, bf16[128,4096]{1,0:T(8,128)(2,1)}, u32[]{:S(2)}) copy-start(bf16[128,4096]{1,0:T(8,128)(2,1)} %stream.3) | copy-start | bytes 3145732
  1.9 14.2 %copy-start.2 = (f32[4096]{0:T(1024)S(1)}, f32[4096]{0:T(1024)}, u32[]{:S(2)}) copy-start(f32[4096]{0:T(1024)} %param.20) | copy-start | bytes 49156
  1.9 14.2 %copy-start.7 = (f32[256,256]{1,0:T(8,128)S(1)}, f32[256,256]{1,0:T(8,128)}, u32[]{:S(2)}) copy-start(f32[256,256]{1,0:T(8,128)} %constant.31.clone.forward) | copy-start | bytes 786436
  2.2 4.0 %collective-permute-start.1 = (f32[1,128]{1,0:T(1,128)S(1)}, f32[1,128]{1,0:T(1,128)S(1)}, u32[]{:S(2)}, u32[]{:S(2)}) collective-permute-start(f32[1,128]{1,0:T(1,128)S(1)} %shard_map.141.squares), channel_id=1, source_target_pairs={{0,1},{1,0},{2,3},{3,2},{4,5},{5,4},{6,7},{7,6},{8,9},{9,8},{10,11... | collective-permute-start | bytes 1544 | tf_op jit(solution)/shard_map/ppermute | solution.py:57
  3.7 1.2 %copy-start.3 = (bf16[128,4096]{1,0:T(8,128)(2,1)S(1)}, bf16[128,4096]{1,0:T(8,128)(2,1)}, u32[]{:S(2)}) copy-start(bf16[128,4096]{1,0:T(8,128)(2,1)} %inner.2) | copy-start | bytes 3145732
  5.0 0.7 copy-start.9
  5.7 10.4 %copy-start.4 = (bf16[128,4096]{1,0:T(8,128)(2,1)S(1)}, bf16[128,4096]{1,0:T(8,128)(2,1)}, u32[]{:S(2)}) copy-start(bf16[128,4096]{1,0:T(8,128)(2,1)} %taps.1) | copy-start | bytes 3145732
  5.7 10.4 %copy-start.5 = (bf16[128,4096]{1,0:T(8,128)(2,1)S(1)}, bf16[128,4096]{1,0:T(8,128)(2,1)}, u32[]{:S(2)}) copy-start(bf16[128,4096]{1,0:T(8,128)(2,1)} %inner.3) | copy-start | bytes 3145732
  6.2 23.8 %copy-start.1 = (bf16[128,128]{1,0:T(8,128)(2,1)S(1)}, bf16[128,128]{1,0:T(8,128)(2,1)}, u32[]{:S(2)}) copy-start(bf16[128,128]{1,0:T(8,128)(2,1)} %constant.33.clone.lower) | copy-start | bytes 98308
  6.2 23.8 %copy-start.8 = (f32[128,256]{1,0:T(8,128)S(1)}, f32[128,256]{1,0:T(8,128)}, u32[]{:S(2)}) copy-start(f32[128,256]{1,0:T(8,128)} %constant.32.clone.back) | copy-start | bytes 393220
  6.3 32.6 %collective-permute-start.3 = (bf16[128,4096]{1,0:T(8,128)(2,1)}, bf16[128,4096]{1,0:T(8,128)(2,1)S(1)}, u32[]{:S(2)}, u32[]{:S(2)}) collective-permute-start(bf16[128,4096]{1,0:T(8,128)(2,1)} %query_far), channel_id=1, source_target_pairs={{2,0},{4,2},{6,4},{8,6},{10,8},{12,10},{14,12},{16,14},{18,16},{20... | collective-permute-start | bytes 3145736 | tf_op jit(solution)/shard_map/ppermute | solution.py:52
  12.2 17.8 %collective-permute-start.2 = (bf16[128,3072]{1,0:T(8,128)(2,1)S(1)}, bf16[128,3072]{1,0:T(8,128)(2,1)S(1)}, u32[]{:S(2)}, u32[]{:S(2)}) collective-permute-start(bf16[128,3072]{1,0:T(8,128)(2,1)S(1)} %get-tuple-element.43), channel_id=1, source_target_pairs={{0,2},{2,4},{4,6},{6,8},{8,10},{10,12},{12,14},{14,16},{16,18},{18... | collective-permute-start | bytes 2359304 | tf_op jit(solution)/shard_map/ppermute | solution.py:52
  14.1 19.1 %collective-permute-start = (bf16[128,1024]{1,0:T(8,128)(2,1)S(1)}, bf16[128,1024]{1,0:T(8,128)(2,1)S(1)}, u32[]{:S(2)}, u32[]{:S(2)}) collective-permute-start(bf16[128,1024]{1,0:T(8,128)(2,1)S(1)} %get-tuple-element.40), channel_id=1, source_target_pairs={{0,2},{2,4},{4,6},{6,8},{8,10},{10,12},{12,14},{14,16},{16,18},{18... | collective-permute-start | bytes 786440 | tf_op jit(solution)/shard_map/ppermute | solution.py:52
  16.1 1.2 %copy-start.6 = (bf16[128,4096]{1,0:T(8,128)(2,1)S(1)}, bf16[128,4096]{1,0:T(8,128)(2,1)}, u32[]{:S(2)}) copy-start(bf16[128,4096]{1,0:T(8,128)(2,1)} %short_outer.1) | copy-start | bytes 3145732
  35.5 8.9 %all-to-all-start = ((bf16[8,32,128]{2,1,0:T(8,128)(2,1)}), bf16[8,32,128]{2,1,0:T(8,128)(2,1)S(1)}, u32[]{:S(2)}, u32[]{:S(2)}) async-start(bf16[8,32,128]{2,1,0:T(8,128)(2,1)} %get-tuple-element.51), calls=%async_computation | async-start | bytes 131072 | tf_op jit(solution)/shard_map/all_to_all | solution.py:487
  45.1 19.4 %all-to-all-start.1 = ((bf16[16,32,128]{2,1,0:T(8,128)(2,1)}), bf16[16,32,128]{2,1,0:T(8,128)(2,1)S(1)}, u32[]{:S(2)}, u32[]{:S(2)}) async-start(bf16[16,32,128]{2,1,0:T(8,128)(2,1)} %get-tuple-element.55), calls=%async_computation.1 | async-start | bytes 262144 | tf_op jit(solution)/shard_map/all_to_all | solution.py:499
  56.7 31.5 %collective-permute-start.5 = (bf16[128,2048]{1,0:T(8,128)(2,1)S(1)}, bf16[128,2048]{1,0:T(8,128)(2,1)S(1)}, u32[]{:S(2)}, u32[]{:S(2)}) collective-permute-start(bf16[128,2048]{1,0:T(8,128)(2,1)S(1)} %shard_map.154), channel_id=1, source_target_pairs={{0,2},{2,4},{4,6},{6,8},{8,10},{10,12},{12,14},{14,16},{16,18},{18... | collective-permute-start | bytes 1572872 | tf_op jit(solution)/shard_map/ppermute | solution.py:52
  69.4 19.8 %collective-permute-start.7 = (bf16[128,2048]{1,0:T(8,128)(2,1)S(1)}, bf16[128,2048]{1,0:T(8,128)(2,1)S(1)}, u32[]{:S(2)}, u32[]{:S(2)}) collective-permute-start(bf16[128,2048]{1,0:T(8,128)(2,1)S(1)} %get-tuple-element.77), channel_id=1, source_target_pairs={{0,2},{2,4},{4,6},{6,8},{8,10},{10,12},{12,14},{14,16},{16,18},{18... | collective-permute-start | bytes 1572872 | tf_op jit(solution)/shard_map/ppermute | solution.py:52
  71.3 17.9 %collective-permute-start.6 = (bf16[144,1024]{1,0:T(8,128)(2,1)S(1)}, bf16[144,1024]{1,0:T(8,128)(2,1)S(1)}, u32[]{:S(2)}, u32[]{:S(2)}) collective-permute-start(bf16[144,1024]{1,0:T(8,128)(2,1)S(1)} %get-tuple-element.76), channel_id=1, source_target_pairs={{0,2},{2,4},{4,6},{6,8},{8,10},{10,12},{12,14},{14,16},{16,18},{18... | collective-permute-start | bytes 884744 | tf_op jit(solution)/shard_map/ppermute | solution.py:52
  73.9 14.3 %collective-permute-start.4 = (f32[128,128]{1,0:T(8,128)S(1)}, f32[128,128]{1,0:T(8,128)S(1)}, u32[]{:S(2)}, u32[]{:S(2)}) collective-permute-start(f32[128,128]{1,0:T(8,128)S(1)} %get-tuple-element.72), channel_id=1, source_target_pairs={{0,2},{2,4},{4,6},{6,8},{8,10},{10,12},{12,14},{14,16},{16,18},{18... | collective-permute-start | bytes 196616 | tf_op jit(solution)/shard_map/ppermute | solution.py:52

commit v6 on v5

--- a/solution.py
+++ b/solution.py
@@ -19,9 +19,10 @@
 BF16 = jnp.bfloat16
 SUB = 256
 PIECE = 512
-TAIL = (3072, 1024)
+ROWS = 16
+TAIL = (2560, 1536)
 EARLY = 1024
-MIDDLE = 2048
+MIDDLE = 2560
 VMEM = 8 * 2**20
 
 
@@ -57,7 +58,7 @@
     return lax.ppermute(block, "mp", [(m, sides - 1 - m) for m in range(sides)])
 
 
-def call(body, outs, scratch=(), scalars=0, operands=0, flops=10**8, outside=(), kept=(), aliases={}):
+def call(body, outs, scratch=(), scalars=0, operands=0, flops=10**8, outside=(), kept=()):
     specs = [pl.BlockSpec(memory_space=pltpu.SMEM)] * scalars
     specs += [pl.BlockSpec(memory_space=pltpu.VMEM)] * operands
     for k in outside:
@@ -74,7 +75,6 @@
             for k, (shape, kind) in enumerate(outs)
         ],
         scratch_shapes=list(scratch),
-        input_output_aliases=aliases,
         compiler_params=pltpu.CompilerParams(vmem_limit_bytes=VMEM),
         cost_estimate=pl.CostEstimate(flops=flops, transcendentals=0, bytes_accessed=10**6),
     )
@@ -92,23 +92,45 @@
     return lax.broadcasted_iota(jnp.int32, (BLOCK, width), 0).astype(F32)
 
 
-def squares_body(stream, squares):
-    acc = jnp.zeros((stream.shape[0], 128), F32)
-    for at in pieces_of(stream.shape[1], 128):
-        x = stream[:, at].astype(F32)
-        acc = acc + x * x
-    squares[...] = jnp.sum(acc.T, axis=0, keepdims=True)
-
-
-def gate_body(stream, inner, gain, v, *sent):
-    start = 0
-    for block in sent:
-        for to in pieces_of(block.shape[1], 128):
-            at = slice(start + to.start, start + to.stop)
-            value = inner[:, at].astype(F32) * stream[:, at].astype(F32) * gain[:, at]
-            v[:, at] = value.astype(BF16)
-            block[:, to] = value.astype(BF16)
-        start += block.shape[1]
+def squares_body(stream_far, squares, stream, sems):
+    arriving = rows_in(stream_far, stream, sems)
+    parts = []
+    for k, copy in enumerate(arriving):
+        copy.wait()
+        part = jnp.zeros((ROWS, 128), F32)
+        for at in pieces_of(stream.shape[1], 128):
+            x = stream[k * ROWS : (k + 1) * ROWS, at].astype(F32)
+            part = part + x * x
+        parts.append(part)
+    squares[...] = jnp.sum(jnp.concatenate(parts, axis=0).T, axis=0, keepdims=True)
+
+
+def rows_in(source, target, sems):
+    copies = []
+    for k in range(target.shape[0] // ROWS):
+        at = pl.ds(k * ROWS, ROWS)
+        copies.append(pltpu.make_async_copy(source.at[at], target.at[at], sems.at[k]))
+        copies[-1].start()
+    return copies
+
+
+def gate_body(stream, inner_far, gain_far, v, *rest):
+    sent, (inner, gain, sems, sem) = rest[:-4], rest[-4:]
+    copy = pltpu.make_async_copy(gain_far, gain, sem)
+    copy.start()
+    arriving = rows_in(inner_far, inner, sems)
+    copy.wait()
+    for k in range(len(arriving)):
+        arriving[k].wait()
+        row = slice(k * ROWS, (k + 1) * ROWS)
+        start = 0
+        for block in sent:
+            for to in pieces_of(block.shape[1], 128):
+                at = slice(start + to.start, start + to.stop)
+                value = inner[row, at].astype(F32) * stream[row, at].astype(F32) * gain[:, at]
+                v[row, at] = value.astype(BF16)
+                block[row, to] = value.astype(BF16)
+            start += block.shape[1]
 
 
 def label_body(squares, beside, sent, total, out):
@@ -156,23 +178,32 @@
     column = lax.broadcasted_iota(jnp.int32, (1, 2 * BLOCK), 1)
     factor = jnp.where(column == 0, 0.0, 1.0 / jnp.sqrt(sums / D + 0.5))
     matrix[...] = (forward[...] * factor).astype(BF16)
-    conv_body(0, before, here, matrix, back, lower, spectrum, gate, decay, far, state, summed, sems)
+    leaving = []
+
+    def done(j, to):
+        at = pl.ds(to.start, SUB)
+        leaving.append(pltpu.make_async_copy(summed.at[:, at], far.at[:, at], sems.at[j]))
+        leaving[-1].start()
+
+    conv_body(0, before, here, matrix, back, lower, spectrum, gate, decay, summed, state, done)
+    for copy in leaving:
+        copy.wait()
 
 
 def conv_last(
-    start, before, here, matrix, back, lower, spectrum, gate, decay, earlier, whole, far, copied, rows, summed, sems
-):
-    conv_body(start, before, here, matrix, back, lower, spectrum, gate, decay, far, rows, summed, sems)
-    state = jnp.concatenate([earlier[...], rows[...]], axis=0).astype(BF16)
+    start, before, here, matrix, back, lower, spectrum, gate, decay, earlier, summed, copied, state
+):
+    state[: start // 128, :] = earlier[...]
+    conv_body(start, before, here, matrix, back, lower, spectrum, gate, decay, summed, state)
+    rows = state[...].astype(BF16)
     for k in range(copied.shape[0]):
-        copied[k] = state
+        copied[k] = rows
 
 
 def conv_body(
-    start, before, here, matrix, back, lower, spectrum, gate, decay, far, state, summed, sems
+    start, before, here, matrix, back, lower, spectrum, gate, decay, summed, state, done=None
 ):
     b = back[...].astype(BF16)
-    leaving = []
     for j, to in enumerate(pieces_of(before.shape[1])):
         at = slice(start + to.start, start + to.stop)
         x = dot(matrix[...], jnp.concatenate([before[:, to], here[:, at]], axis=0))
@@ -184,19 +215,13 @@
         conv = dot(b, jnp.concatenate([y_re, y_im], axis=0))
         z = (gate[:, at] * conv).astype(BF16)
         summed[:, to] = z
-        leaving.append(
-            pltpu.make_async_copy(
-                summed.at[:, pl.ds(to.start, SUB)], far.at[:, pl.ds(at.start, SUB)], sems.at[j]
-            )
-        )
-        leaving[-1].start()
+        if done is not None:
+            done(j, to)
         result = dot(lower[...], z)
         last = result[BLOCK - 1 :] * jnp.exp(decay[:, at] * (1.0 - BLOCK))
         for k in range(SUB // 128):
-            row = j * (SUB // 128) + k
+            row = at.start // 128 + k
             state[row : row + 1, :] = last[:, k * 128 : (k + 1) * 128]
-    for copy in leaving:
-        copy.wait()
 
 
 def weighted(pieces, place, rate, some=slice(None)):
@@ -216,10 +241,32 @@
         copied[k] = group
 
 
-def early_body(summed_far, lower, outer_far, decay, scale, weights, sent, summed, long_outer, *sems):
+def early_body(
+    summed_far,
+    lower,
+    outer_far,
+    decay,
+    scale,
+    weights,
+    stats,
+    sent,
+    summed_middle,
+    outer_middle,
+    summed,
+    long_outer,
+    *sems,
+):
     share = summed.shape[1]
     summed_in = fetches(summed_far, summed, sems[0], 0, PIECE)
     outer_in = fetches(outer_far, long_outer, sems[1], 0, PIECE)
+    left = stats[...]
+    for k in range(3):
+        term = left.astype(BF16)
+        left = left - term.astype(F32)
+        low = 2 * share + k * BLOCK
+        sent[:, low : low + BLOCK] = term
+    later = fetches(summed_far, summed_middle, sems[2], EARLY, PIECE)
+    later += fetches(outer_far, outer_middle, sems[3], EARLY, PIECE)
     time = times(PIECE)
     for k, at in enumerate(pieces_of(share, PIECE)):
         d = decay[:, at]
@@ -237,27 +284,11 @@
             high = share + low
             sent[:, low : low + HEAD_DIM] = both[:, :HEAD_DIM].astype(BF16)
             sent[:, high : high + HEAD_DIM] = both[:, HEAD_DIM:].astype(BF16)
-
-
-def finish_body(
-    start,
-    near_size,
-    place,
-    others,
-    inside,
-    rate,
-    summed_far,
-    lower,
-    outer_far,
-    decay,
-    scale,
-    weights,
-    mixed,
-    *rest,
-):
-    summed, long_outer, summed_sems, outer_sems = rest[-4:]
-    summed_in = fetches(summed_far, summed, summed_sems, start, PIECE)
-    outer_in = fetches(outer_far, long_outer, outer_sems, start, PIECE)
+    for copy in later:
+        copy.wait()
+
+
+def finish(start, near_size, place, others, inside, rate, lower, decay, scale, mixed, read):
     near, far = place[0], place[1]
     r = rate[...]
     carry = inside[...] + jnp.exp(-r * near.astype(F32)) * weighted(others, far, r * near_size)
@@ -268,26 +299,110 @@
         heads = range(at.start // HEAD_DIM, at.stop // HEAD_DIM)
         entering = jnp.concatenate([carry[j : j + 1] for j in heads], axis=1) * jnp.exp(-d)
         factor = jnp.exp(-d * time) * scale[:, at]
+        summed, outer = read(k, to)
+        base = dot(lower[...], summed) + entering
+        mixed[:, to] = (outer.astype(F32) * factor * base).astype(BF16)
+    return carry
+
+
+def finish_first(
+    near_size, place, others, inside, rate, summed_far, lower, outer_far, decay, scale, mixed, *rest
+):
+    summed, outer, summed_sems, outer_sems = rest
+    summed_in = fetches(summed_far, summed, summed_sems, 0, PIECE)
+    outer_in = fetches(outer_far, outer, outer_sems, 0, PIECE)
+
+    def read(k, to):
         summed_in[k].wait()
-        base = dot(lower[...], summed[:, to]) + entering
         outer_in[k].wait()
-        mixed[:, to] = (long_outer[:, to].astype(F32) * factor * base).astype(BF16)
-    if start == 0:
-        return
-    ahead = rest[0]
+        return summed[:, to], outer[:, to]
+
+    finish(0, near_size, place, others, inside, rate, lower, decay, scale, mixed, read)
+
+
+def partial_attention(start, weights, mixed, ahead):
     for j, to in enumerate(pieces_of(mixed.shape[1], HEAD_DIM)):
         head = start // HEAD_DIM + j
         ahead[:BLOCK, to] = dot(weights[head], mixed[:, to]).astype(BF16)
-    if ahead.shape[0] > BLOCK:
-        row = lax.broadcasted_iota(jnp.int32, (16, HEAD_DIM), 0)
-        for j, to in enumerate(pieces_of(EARLY, HEAD_DIM)):
+
+
+def finish_middle(
+    near_size,
+    place,
+    others,
+    inside,
+    rate,
+    summed,
+    lower,
+    outer,
+    decay,
+    scale,
+    weights,
+    mixed,
+    ahead,
+):
+    carry = finish(
+        EARLY,
+        near_size,
+        place,
+        others,
+        inside,
+        rate,
+        lower,
+        decay,
+        scale,
+        mixed,
+        lambda k, to: (summed[:, to], outer[:, to]),
+    )
+    partial_attention(EARLY, weights, mixed, ahead)
+    row = lax.broadcasted_iota(jnp.int32, (16, HEAD_DIM), 0)
+    for j, to in enumerate(pieces_of(ahead.shape[1], HEAD_DIM)):
+        kept = jnp.zeros((16, HEAD_DIM), F32)
+        if to.start < EARLY:
             left = carry[j : j + 1]
-            kept = jnp.zeros((16, HEAD_DIM), F32)
             for k in range(3):
                 term = left.astype(BF16).astype(F32)
                 left = left - term
                 kept = jnp.where(row == k, term, kept)
-            ahead[BLOCK:, to] = kept.astype(BF16)
+        ahead[BLOCK:, to] = kept.astype(BF16)
+
+
+def finish_last(
+    near_size,
+    place,
+    others,
+    inside,
+    rate,
+    summed,
+    lower,
+    outer_far,
+    decay,
+    scale,
+    weights,
+    mixed,
+    ahead,
+    outer,
+    sems,
+):
+    outer_in = fetches(outer_far, outer, sems, MIDDLE, PIECE)
+
+    def read(k, to):
+        outer_in[k].wait()
+        return summed[:, to], outer[:, to]
+
+    finish(MIDDLE, near_size, place, others, inside, rate, lower, decay, scale, mixed, read)
+    partial_attention(MIDDLE, weights, mixed, ahead)
+
+
+def store_body(first, middle, last, whole, sems):
+    leaving, start = [], 0
+    for k, block in enumerate((first, middle, last)):
+        share = block.shape[1]
+        leaving.append(pltpu.make_async_copy(block, whole.at[:, pl.ds(start, share)], sems.at[k]))
+        leaving[-1].start()
+        start += share
+    for copy in leaving:
+        copy.wait()
 
 
 def score(query, key):
@@ -355,10 +470,12 @@
     stats[...] = jnp.where(lane < BLOCK // 2, tops, sizes)
 
 
-def here_body(weights, first, middle, last, stats_here, stats_before, early, base, slope, share):
+def here_body(weights, first, middle, last, stats_here, early, base, slope, share):
     top, size = stats_here[...], pltpu.roll(stats_here[...], BLOCK // 2, 1)
-    size_b = pltpu.roll(stats_before[...], BLOCK // 2, 1)
-    top_b = jnp.where(size_b > 0.0, stats_before[...], -1e30)
+    terms = early[:, 2 * EARLY :].astype(F32)
+    stats_before = (terms[:, :BLOCK] + terms[:, BLOCK : 2 * BLOCK]) + terms[:, 2 * BLOCK :]
+    size_b = pltpu.roll(stats_before, BLOCK // 2, 1)
+    top_b = jnp.where(size_b > 0.0, stats_before, -1e30)
     highest = jnp.maximum(top, top_b)
     scale = jnp.exp(top - highest)
     scale_b = size_b * jnp.exp(top_b - highest)
@@ -404,28 +521,6 @@
         copy.wait()
 
 
-def copy_body(block, *rest):
-    rest[-1][...] = block[...]
-
-
-def into(body, index, block, whole, width):
-    rows, share = block.shape
-    specs = [pl.BlockSpec((rows, share), lambda i: (0, 0))]
-    operands, aliases = (block,), {}
-    if whole is not None:
-        specs.append(pl.BlockSpec(memory_space=pl.ANY))
-        operands, aliases = (block, whole), {1: 0}
-    return pl.pallas_call(
-        body,
-        grid=(1,),
-        in_specs=specs,
-        out_specs=pl.BlockSpec((rows, share), lambda i: (0, index)),
-        out_shape=jax.ShapeDtypeStruct((rows, width), BF16),
-        input_output_aliases=aliases,
-        compiler_params=pltpu.CompilerParams(vmem_limit_bytes=VMEM),
-    )(*operands)
-
-
 def on_device(
     stream,
     norm_gain,
@@ -450,11 +545,23 @@
     square = ((rows, rows), F32)
     wide, wide_float = ((rows, width), BF16), ((rows, width), F32)
 
-    (squares,) = call(squares_body, [((1, rows), F32)], operands=1)(stream)
+    row_sems = pltpu.SemaphoreType.DMA((rows // ROWS,))
+    squares, stream = call(
+        squares_body, [((1, rows), F32), wide], [row_sems], operands=1, outside=(0,)
+    )(in_hbm(stream))
     beside = swapped(squares)
-    v, *sent = call(gate_body, [wide] + [((rows, share), BF16) for share in TAIL], operands=3)(
-        stream, short_inner, norm_gain[None]
-    )
+    v, *sent = call(
+        gate_body,
+        [wide] + [((rows, share), BF16) for share in TAIL],
+        [
+            pltpu.VMEM((rows, width), BF16),
+            pltpu.VMEM((1, width), F32),
+            row_sems,
+            pltpu.SemaphoreType.DMA,
+        ],
+        operands=3,
+        outside=(1, 2),
+    )(stream, in_hbm(short_inner), in_hbm(norm_gain[None]))
     total, sent[0] = label(squares, beside, sent[0])
     v_before = []
     for part in range(len(TAIL)):
@@ -464,26 +571,19 @@
     spectrum, gate = call(
         tables_body, [((2 * rows, width), F32), wide_float], operands=5
     )(forward, short_filter, long_inner, short_outer, decay)
-
-    def leaving(share):
-        return [pltpu.VMEM((rows, share), BF16), pltpu.SemaphoreType.DMA((share // SUB,))]
-
     summed, state, matrix = call(
         conv_first,
-        [wide, ((TAIL[0] // 128, 128), F32), ((2 * rows, 2 * rows), BF16)],
-        leaving(TAIL[0]),
+        [((rows, TAIL[0]), BF16), ((TAIL[0] // 128, 128), F32), ((2 * rows, 2 * rows), BF16)],
+        [pltpu.VMEM((rows, TAIL[0]), BF16), pltpu.SemaphoreType.DMA((TAIL[0] // SUB,))],
         operands=9,
         kept=(0,),
     )(v_before[0], v, total, forward, back, lower, spectrum, gate, decay)
-    summed, state = call(
+    summed_last, state = call(
         functools.partial(conv_last, TAIL[0]),
-        [wide, ((near_size, lanes, 128), BF16)],
-        [pltpu.VMEM((TAIL[1] // 128, 128), F32), *leaving(TAIL[1])],
-        operands=10,
-        outside=(9,),
-        kept=(0,),
-        aliases={9: 0},
-    )(v_before[1], v, matrix, back, lower, spectrum, gate, decay, state, summed)
+        [((rows, TAIL[1]), BF16), ((near_size, lanes, 128), BF16)],
+        [pltpu.VMEM((lanes, 128), F32)],
+        operands=9,
+    )(v_before[1], v, matrix, back, lower, spectrum, gate, decay, state)
     pieces = lax.all_to_all(state, NEAR, 0, 0, tiled=True)
     weights_next, stats_next = call(
         ahead_body,
@@ -502,44 +602,52 @@
         space = [pltpu.VMEM((rows, share), BF16)] * 2
         return space + [pltpu.SemaphoreType.DMA((share // PIECE,))] * 2
 
+    share = MIDDLE - EARLY
+    middle_wide, last_wide = ((rows, share), BF16), ((rows, width - MIDDLE), BF16)
     summed, inside = lax.optimization_barrier((summed, inside))
-    (early,) = call(
-        early_body, [((rows, 2 * EARLY), BF16)], fetching(EARLY), operands=6, outside=(0, 2)
-    )(in_hbm(summed), lower, in_hbm(long_outer), decay, scale, weights_next)
+    summed, outer = in_hbm(summed), in_hbm(long_outer)
+    early, summed_middle, outer_middle = call(
+        early_body,
+        [((rows, 2 * EARLY + 3 * rows), BF16), middle_wide, middle_wide],
+        fetching(EARLY) + [pltpu.SemaphoreType.DMA((share // PIECE,))] * 2,
+        operands=7,
+        outside=(0, 2),
+    )(summed, lower, outer, decay, scale, weights_next, stats_next)
     early = shifted(early, SEQ, 1)
-    stats_before = shifted(stats_next, SEQ, 1)
-
-    def finish(start, stop, extra):
-        return call(
-            functools.partial(finish_body, start, float(near_size)),
-            [((rows, stop - start), BF16), *extra],
-            fetching(stop - start),
-            scalars=1,
-            operands=9,
-            outside=(4, 6),
-        )(
-            jnp.stack([near, far]),
-            others,
-            inside,
-            rate,
-            in_hbm(summed),
-            lower,
-            in_hbm(long_outer),
-            decay,
-            scale,
-            weights_next,
-        )
-
-    middle, ready = finish(EARLY, MIDDLE, [((rows + 16, MIDDLE - EARLY), BF16)])
+    place, steps = jnp.stack([near, far]), float(near_size)
+    middle, ready = call(
+        functools.partial(finish_middle, steps),
+        [middle_wide, ((rows + 16, share), BF16)],
+        scalars=1,
+        operands=9,
+    )(
+        place, others, inside, rate, summed_middle, lower, outer_middle, decay, scale, weights_next
+    )
     arrived = shifted(ready, SEQ, 1)
-    others, middle = lax.optimization_barrier((others, middle))
-    last, ready = finish(MIDDLE, width, [((rows, width - MIDDLE), BF16)])
+    last, ready = call(
+        functools.partial(finish_last, steps),
+        [last_wide, last_wide],
+        [
+            pltpu.VMEM((rows, width - MIDDLE), BF16),
+            pltpu.SemaphoreType.DMA(((width - MIDDLE) // PIECE,)),
+        ],
+        scalars=1,
+        operands=9,
+        outside=(6,),
+    )(place, others, inside, rate, summed_last, lower, outer, decay, scale, weights_next)
     arrived_last = shifted(ready, SEQ, 1)
     others, last = lax.optimization_barrier((others, last))
-    (first,) = finish(0, EARLY, [])
-    values = into(copy_body, 0, first, None, width)
-    values = into(copy_body, EARLY // (MIDDLE - EARLY), middle, values, width)
-    values = into(copy_body, MIDDLE // (width - MIDDLE), last, values, width)
+    (first,) = call(
+        functools.partial(finish_first, steps),
+        [((rows, EARLY), BF16)],
+        fetching(EARLY),
+        scalars=1,
+        operands=8,
+        outside=(4, 6),
+    )(place, others, inside, rate, summed, lower, outer, decay, scale)
+    (values,) = call(
+        store_body, [wide], [pltpu.SemaphoreType.DMA((3,))], operands=3, kept=(0,)
+    )(first, middle, last)
     query_own, key_own, last = lax.optimization_barrier((query_heads, key_heads, last))
     weights_here, stats_here = call(
         own_body,
@@ -550,8 +658,8 @@
         outside=(0, 1),
     )(in_hbm(query_own), in_hbm(key_own))
     base, slope, share = call(
-        here_body, [wide_float, ((rows, EARLY), F32), square], operands=7
-    )(weights_here, first, middle, last, stats_here, stats_before, early)
+        here_body, [wide_float, ((rows, EARLY), F32), square], operands=6
+    )(weights_here, first, middle, last, stats_here, early)
     (attended,) = call(
         join_body,
         [wide],

time: 91.4 us -> 84.6 us (0.926)
  local copies, waits for them, and re-layouts: 4.41 us -> 0.04 us
  starting transfers between devices: 33 us -> 30.6 us
    unnamed x20 -> x14, local copies, waits for them, and re-layouts: 4.41 us -> 0.04 us
    ppermute x7 -> x6, starting transfers between devices: 18.3 us -> 15.9 us  [shifted(): lax.ppermute(block, axis, [(i, i + distance) for i in range(size) if 0 <=...]
    all_to_all x1, waiting for transfers between devices: 5.8 us -> 4.77 us  [on_device(): others = lax.all_to_all(group, FAR, 0, 0, tiled=True)]
    ppermute x7 -> x6, waiting for transfers between devices: 16.1 us -> 16.8 us  [shifted(): lax.ppermute(block, axis, [(i, i + distance) for i in range(size) if 0 <=...]
    pallas_call x12 -> x10, Pallas kernels: 18.1 us -> 18.1 us  [the longest x1 2.8 us: on_device(): call(early_body, [((rows, 2 * EARLY + 3 * rows), BF16), middle_wide, midd...]
  transfers between devices with their start and end apart: 10 -> 9, of which waited for: 4 -> 6; matrix products, arithmetic and copies ran while one was open for 0% -> 0% of each run, Pallas kernels for 28% -> 29%
where the time goes in v6:
time: 84.6 us; the launch traced here: 84.1 us
  starting transfers between devices  30.6 us (36%)
  Pallas kernels  27.8 us (33%)
  waiting for transfers between devices  24.4 us (29%)
  between operations  1.08 us (1%)
    ppermute x6, waiting for transfers between devices, shifted(): lax.ppermute(block, axis, [(i, i + distance) for i in range(size) if 0 <=...  16.8 us
    ppermute x6, starting transfers between devices, shifted(): lax.ppermute(block, axis, [(i, i + distance) for i in range(size) if 0 <=...  15.9 us
    all_to_all x1, starting transfers between devices, on_device(): others = lax.all_to_all(group, FAR, 0, 0, tiled=True)  9.79 us
    all_to_all x1, waiting for transfers between devices, on_device(): others = lax.all_to_all(group, FAR, 0, 0, tiled=True)  4.77 us
    all_to_all x1, starting transfers between devices, on_device(): pieces = lax.all_to_all(state, NEAR, 0, 0, tiled=True)  3.35 us
    pallas_call x1, Pallas kernels, on_device(): call(own_body, [((heads, rows, rows), BF16), square], [pltpu.VMEM((rows,...  3.27 us
    pallas_call x1, Pallas kernels, on_device(): call(ahead_body, [((heads, rows, rows), BF16), square], [pltpu.VMEM((rows...  3.17 us
    pallas_call x1, Pallas kernels, on_device(): call(early_body, [((rows, 2 * EARLY + 3 * rows), BF16), middle_wide, midd...  2.8 us
  transfers between devices with their start and end apart: 9, of which 6 were waited for; matrix products, arithmetic and copies ran while one was open for 0% of the time, Pallas kernels for 29%

profile of v6, /device:TPU:32, one launch (start us, length us, event | category | flops | bytes accessed | tf_op | source)
XLA Modules:
  0.0 84.1 jit_solution(18328041984105014689)
XLA Ops:
  0.6 0.0 copy-start.5
  0.6 0.0 copy-start.1
  0.7 0.0 copy-start.4
  0.7 0.0 copy-start.2
  0.7 0.0 copy-start.3
  0.7 1.6 %shard_map.140 = (f32[1,128]{1,0:T(1,128)S(1)}, bf16[128,4096]{1,0:T(8,128)(2,1)S(1)}) custom-call(bf16[128,4096]{1,0:T(8,128)(2,1)} %stream_far.1), custom_call_target="tpu_custom_call" | custom-call | flops 100000000 | bytes 1000000 | tf_op jit(solution)/shard_map/pallas_call | solution.py:549
  2.3 1.6 %collective-permute-start.1 = (f32[1,128]{1,0:T(1,128)S(1)}, f32[1,128]{1,0:T(1,128)S(1)}, u32[]{:S(2)}, u32[]{:S(2)}) collective-permute-start(f32[1,128]{1,0:T(1,128)S(1)} %get-tuple-element.46.squares), channel_id=1, source_target_pairs={{0,1},{1,0},{2,3},{3,2},{4,5},{5,4},{6,7},{7,6},{8,9},{9,8},{10,11... | collective-permute-start | bytes 1544 | tf_op jit(solution)/shard_map/ppermute | solution.py:58
  3.9 1.5 %shard_map.141 = (bf16[128,4096]{1,0:T(8,128)(2,1)S(1)}, bf16[128,2560]{1,0:T(8,128)(2,1)S(1)}, bf16[128,1536]{1,0:T(8,128)(2,1)S(1)}) custom-call(bf16[128,4096]{1,0:T(8,128)(2,1)S(1)} %get-tuple-element.43.stream, bf16[128,4096]{1,0:T(8,128)(2,1)} %inner_far.1, f32[1,4096]{1,0:T(1,128)} %bitcast.18), custom_call_target="tpu_custom_call" | custom-call | flops 100000000 | bytes 1000000 | tf_op jit(solution)/shard_map/pallas_call | solution.py:553
  5.4 0.0 copy-start
  5.4 0.0 copy-start.6
  5.5 0.5 collective-permute-done.1.beside
  6.0 5.4 %collective-permute-start.3 = (bf16[128,4096]{1,0:T(8,128)(2,1)}, bf16[128,4096]{1,0:T(8,128)(2,1)S(1)}, u32[]{:S(2)}, u32[]{:S(2)}) collective-permute-start(bf16[128,4096]{1,0:T(8,128)(2,1)} %query_far), channel_id=1, source_target_pairs={{2,0},{4,2},{6,4},{8,6},{10,8},{12,10},{14,12},{16,14},{18,16},{20... | collective-permute-start | bytes 3145736 | tf_op jit(solution)/shard_map/ppermute | solution.py:53
  11.4 1.9 %collective-permute-start.2 = (bf16[128,2560]{1,0:T(8,128)(2,1)S(1)}, bf16[128,2560]{1,0:T(8,128)(2,1)S(1)}, u32[]{:S(2)}, u32[]{:S(2)}) collective-permute-start(bf16[128,2560]{1,0:T(8,128)(2,1)S(1)} %get-tuple-element.48), channel_id=1, source_target_pairs={{0,2},{2,4},{4,6},{6,8},{8,10},{10,12},{12,14},{14,16},{16,18},{18... | collective-permute-start | bytes 1966088 | tf_op jit(solution)/shard_map/ppermute | solution.py:53
  13.4 1.9 %collective-permute-start = (bf16[128,1536]{1,0:T(8,128)(2,1)S(1)}, bf16[128,1536]{1,0:T(8,128)(2,1)S(1)}, u32[]{:S(2)}, u32[]{:S(2)}) collective-permute-start(bf16[128,1536]{1,0:T(8,128)(2,1)S(1)} %get-tuple-element.44), channel_id=1, source_target_pairs={{0,2},{2,4},{4,6},{6,8},{8,10},{10,12},{12,14},{14,16},{16,18},{18... | collective-permute-start | bytes 1179656 | tf_op jit(solution)/shard_map/ppermute | solution.py:53
  15.3 0.0 copy-done.5
  15.3 0.0 copy-done.1
  15.3 0.0 copy-done.4
  15.3 0.0 copy-done.2
  15.3 0.0 copy-done.3
  15.3 1.3 %shard_map.142 = (f32[256,4096]{1,0:T(8,128)S(1)}, f32[128,4096]{1,0:T(8,128)S(1)}) custom-call(f32[256,256]{1,0:T(8,128)S(1)} %copy-done.5, bf16[128,4096]{1,0:T(8,128)(2,1)S(1)} %copy-done.2, bf16[128,4096]{1,0:T(8,128)(2,1)S(1)} %copy-done.3, bf16[128,4096]{1,0:T(8,128)(2,1)S(1)} %copy-done.4, f32[1,4096]{1,0:T(1,128)S(1)} %bitcast.7), custom_call_target="tpu_custom_call" | custom-call | flops 100000000 | bytes 1000000 | tf_op jit(solution)/shard_map/pallas_call | solution.py:571
  16.7 11.2 %collective-permute-done.2.before = bf16[128,2560]{1,0:T(8,128)(2,1)S(1)} collective-permute-done((bf16[128,2560]{1,0:T(8,128)(2,1)S(1)}, bf16[128,2560]{1,0:T(8,128)(2,1)S(1)}, u32[]{:S(2)}, u32[]{:S(2)}) %collective-permute-start.2) | collective-permute-done | bytes 655392 | tf_op jit(solution)/shard_map/ppermute | solution.py:53
  27.8 0.0 copy-done
  27.8 0.0 copy-done.6
  27.8 2.8 %shard_map.143 = (bf16[128,2560]{1,0:T(8,128)(2,1)}, f32[20,128]{1,0:T(8,128)S(1)}, bf16[256,256]{1,0:T(8,128)(2,1)S(1)}) custom-call(bf16[128,2560]{1,0:T(8,128)(2,1)S(1)} %collective-permute-done.2.before, bf16[128,4096]{1,0:T(8,128)(2,1)S(1)} %get-tuple-element.45.here, f32[1,128]{1,0:T(1,128)S(1)} %get-tuple-element.50.squares, ...), custom_call_target="tpu_custom_call" | custom-call | flops 100000000 | bytes 1000000 | tf_op jit(solution)/shard_map/pallas_call | solution.py:574
  30.6 1.4 %collective-permute-done.before = bf16[128,1536]{1,0:T(8,128)(2,1)S(1)} collective-permute-done((bf16[128,1536]{1,0:T(8,128)(2,1)S(1)}, bf16[128,1536]{1,0:T(8,128)(2,1)S(1)}, u32[]{:S(2)}, u32[]{:S(2)}) %collective-permute-start) | collective-permute-done | bytes 393248 | tf_op jit(solution)/shard_map/ppermute | solution.py:53
  32.1 2.1 %shard_map.144 = (bf16[128,1536]{1,0:T(8,128)(2,1)S(1)}, bf16[8,32,128]{2,1,0:T(8,128)(2,1)}) custom-call(bf16[128,1536]{1,0:T(8,128)(2,1)S(1)} %collective-permute-done.before, bf16[128,4096]{1,0:T(8,128)(2,1)S(1)} %get-tuple-element.45.here, bf16[256,256]{1,0:T(8,128)(2,1)S(1)} %get-tuple-element.53.matrix, f32[128,256]{1,0:T(8,128)S(1)} %copy-done.6, ...), custom_call_target="tpu_custom_call" | custom-call | flops 100000000 | bytes 1000000 | tf_op jit(solution)/shard_map/pallas_call | solution.py:581
  34.2 3.4 %all-to-all-start = ((bf16[8,32,128]{2,1,0:T(8,128)(2,1)}), bf16[8,32,128]{2,1,0:T(8,128)(2,1)S(1)}, u32[]{:S(2)}, u32[]{:S(2)}) async-start(bf16[8,32,128]{2,1,0:T(8,128)(2,1)} %get-tuple-element.55), calls=%async_computation | async-start | bytes 131072 | tf_op jit(solution)/shard_map/all_to_all | solution.py:587
  37.6 0.0 collective-permute-done.3.query
  37.6 3.2 %shard_map.145 = (bf16[32,128,128]{2,1,0:T(8,128)(2,1)S(1)}, f32[128,128]{1,0:T(8,128)S(1)}) custom-call(bf16[128,4096]{1,0:T(8,128)(2,1)S(1)} %collective-permute-done.3.query, bf16[128,4096]{1,0:T(8,128)(2,1)} %key_far.2), custom_call_target="tpu_custom_call" | custom-call | flops 100000000 | bytes 1000000 | tf_op jit(solution)/shard_map/pallas_call | solution.py:588
  40.7 2.3 %all-to-all-done.pieces = bf16[8,32,128]{2,1,0:T(8,128)(2,1)S(1)} async-done(((bf16[8,32,128]{2,1,0:T(8,128)(2,1)}), bf16[8,32,128]{2,1,0:T(8,128)(2,1)S(1)}, u32[]{:S(2)}, u32[]{:S(2)}) %all-to-all-start) | async-done | bytes 65568 | tf_op jit(solution)/shard_map/all_to_all | solution.py:587
  43.1 0.7 shard_map.146
  43.8 9.8 %all-to-all-start.1 = ((bf16[16,32,128]{2,1,0:T(8,128)(2,1)}), bf16[16,32,128]{2,1,0:T(8,128)(2,1)S(1)}, u32[]{:S(2)}, u32[]{:S(2)}) async-start(bf16[16,32,128]{2,1,0:T(8,128)(2,1)} %get-tuple-element.59), calls=%async_computation.1 | async-start | bytes 262144 | tf_op jit(solution)/shard_map/all_to_all | solution.py:599
  53.6 2.8 %shard_map.149 = (bf16[128,2432]{1,0:T(8,128)(2,1)}, bf16[128,1536]{1,0:T(8,128)(2,1)S(1)}, bf16[128,1536]{1,0:T(8,128)(2,1)S(1)}) custom-call(bf16[128,2560]{1,0:T(8,128)(2,1)} %get-tuple-element.67.summed_far, bf16[128,128]{1,0:T(8,128)(2,1)S(1)} %copy-done, bf16[128,4096]{1,0:T(8,128)(2,1)} %outer_far.5, f32[1,4096]{1,0:T(1,128)S(1)} %bitcast.10, ...), custom_call_target="tpu_custom_call" | custom-call | flops 100000000 | bytes 1000000 | tf_op jit(solution)/shard_map/pallas_call | solution.py:609
  56.4 1.9 %collective-permute-start.4 = (bf16[128,2432]{1,0:T(8,128)(2,1)}, bf16[128,2432]{1,0:T(8,128)(2,1)S(1)}, u32[]{:S(2)}, u32[]{:S(2)}) collective-permute-start(bf16[128,2432]{1,0:T(8,128)(2,1)} %get-tuple-element.78), channel_id=1, source_target_pairs={{0,2},{2,4},{4,6},{6,8},{8,10},{10,12},{12,14},{14,16},{16,18},{18... | collective-permute-start | bytes 1867784 | tf_op jit(solution)/shard_map/ppermute | solution.py:53
  58.3 0.1 pad_add_fusion.place
  58.4 4.8 %all-to-all-done.1.others = bf16[16,32,128]{2,1,0:T(8,128)(2,1)S(1)} async-done(((bf16[16,32,128]{2,1,0:T(8,128)(2,1)}), bf16[16,32,128]{2,1,0:T(8,128)(2,1)S(1)}, u32[]{:S(2)}, u32[]{:S(2)}) %all-to-all-start.1) | async-done | bytes 131104 | tf_op jit(solution)/shard_map/all_to_all | solution.py:599
  63.1 1.1 %shard_map.150 = (bf16[128,1536]{1,0:T(8,128)(2,1)S(1)}, bf16[144,1536]{1,0:T(8,128)(2,1)S(1)}) custom-call(s32[2]{0:T(128)S(1)} %pad_add_fusion.place, bf16[16,32,128]{2,1,0:T(8,128)(2,1)S(1)} %all-to-all-done.1.others, f32[32,128]{1,0:T(8,128)S(1)} %get-tuple-element.62.inside, f32[32,128]{1,0:T(8,128)S(1)} %get-tuple-element.85.rate, ...), custom_call_target="tpu_custom_call" | custom-call | flops 100000000 | bytes 1000000 | tf_op jit(solution)/shard_map/pallas_call | solution.py:618
  64.3 1.9 %collective-permute-start.5 = (bf16[144,1536]{1,0:T(8,128)(2,1)S(1)}, bf16[144,1536]{1,0:T(8,128)(2,1)S(1)}, u32[]{:S(2)}, u32[]{:S(2)}) collective-permute-start(bf16[144,1536]{1,0:T(8,128)(2,1)S(1)} %get-tuple-element.82), channel_id=1, source_target_pairs={{0,2},{2,4},{4,6},{6,8},{8,10},{10,12},{12,14},{14,16},{16,18},{18... | collective-permute-start | bytes 1327112 | tf_op jit(solution)/shard_map/ppermute | solution.py:53
  66.2 2.2 %shard_map.147 = (bf16[128,1536]{1,0:T(8,128)(2,1)S(1)}, bf16[128,1536]{1,0:T(8,128)(2,1)S(1)}) custom-call(s32[2]{0:T(128)S(1)} %pad_add_fusion.place, bf16[16,32,128]{2,1,0:T(8,128)(2,1)S(1)} %all-to-all-done.1.others, f32[32,128]{1,0:T(8,128)S(1)} %get-tuple-element.62.inside, f32[32,128]{1,0:T(8,128)S(1)} %get-tuple-element.85.rate, ...), custom_call_target="tpu_custom_call" | custom-call | flops 100000000 | bytes 1000000 | tf_op jit(solution)/shard_map/pallas_call | solution.py:627
  68.4 2.8 %collective-permute-start.6 = (bf16[128,1536]{1,0:T(8,128)(2,1)S(1)}, bf16[128,1536]{1,0:T(8,128)(2,1)S(1)}, u32[]{:S(2)}, u32[]{:S(2)}) collective-permute-start(bf16[128,1536]{1,0:T(8,128)(2,1)S(1)} %get-tuple-element.83), channel_id=1, source_target_pairs={{0,2},{2,4},{4,6},{6,8},{8,10},{10,12},{12,14},{14,16},{16,18},{18... | collective-permute-start | bytes 1179656 | tf_op jit(solution)/shard_map/ppermute | solution.py:53
  71.2 1.9 %shard_map.148.first = bf16[128,1024]{1,0:T(8,128)(2,1)S(1)} custom-call(s32[2]{0:T(128)S(1)} %pad_add_fusion.place, bf16[16,32,128]{2,1,0:T(8,128)(2,1)S(1)} %all-to-all-done.1.others, f32[32,128]{1,0:T(8,128)S(1)} %get-tuple-element.62.inside, f32[32,128]{1,0:T(8,128)S(1)} %get-tuple-element.85.rate, bf16[128,2560]{1,0:T(8,128)(2,1)} %get-tuple-element.67.summed_far, ...), custom_call_target="tpu_custom_call" | custom-call | flops 100000000 | bytes 1000000 | tf_op jit(solution)/shard_map/pallas_call | solution.py:640
  73.2 3.3 %shard_map.152 = (bf16[32,128,128]{2,1,0:T(8,128)(2,1)S(1)}, f32[128,128]{1,0:T(8,128)S(1)}) custom-call(bf16[128,4096]{1,0:T(8,128)(2,1)} %query_far, bf16[128,4096]{1,0:T(8,128)(2,1)} %key_far.2), custom_call_target="tpu_custom_call" | custom-call | flops 100000000 | bytes 1000000 | tf_op jit(solution)/shard_map/pallas_call | solution.py:652
  76.4 1.0 %shard_map.151 = bf16[128,4096]{1,0:T(8,128)(2,1)} custom-call(bf16[128,1024]{1,0:T(8,128)(2,1)S(1)} %shard_map.148.first, bf16[128,1536]{1,0:T(8,128)(2,1)S(1)} %get-tuple-element.71.middle, bf16[128,1536]{1,0:T(8,128)(2,1)S(1)} %get-tuple-element.76.last), custom_call_target="tpu_custom_call" | custom-call | flops 100000000 | bytes 1000000 | tf_op jit(solution)/shard_map/pallas_call | solution.py:648
  77.4 0.0 collective-permute-done.4.early
  77.4 1.0 %shard_map.153 = (f32[128,4096]{1,0:T(8,128)S(1)}, f32[128,1024]{1,0:T(8,128)S(1)}, f32[128,128]{1,0:T(8,128)S(1)}) custom-call(bf16[32,128,128]{2,1,0:T(8,128)(2,1)S(1)} %get-tuple-element.75.weights, bf16[128,1024]{1,0:T(8,128)(2,1)S(1)} %shard_map.148.first, bf16[128,1536]{1,0:T(8,128)(2,1)S(1)} %get-tuple-element.71.middle, ...), custom_call_target="tpu_custom_call" | custom-call | flops 100000000 | bytes 1000000 | tf_op jit(solution)/shard_map/pallas_call | solution.py:660
  78.4 4.2 %collective-permute-done.6.last = bf16[128,1536]{1,0:T(8,128)(2,1)S(1)} collective-permute-done((bf16[128,1536]{1,0:T(8,128)(2,1)S(1)}, bf16[128,1536]{1,0:T(8,128)(2,1)S(1)}, u32[]{:S(2)}, u32[]{:S(2)}) %collective-permute-start.6) | collective-permute-done | bytes 393248 | tf_op jit(solution)/shard_map/ppermute | solution.py:53
  82.7 0.0 collective-permute-done.5.before
  82.7 1.3 %shard_map.154 = bf16[128,4096]{1,0:T(8,128)(2,1)} custom-call(f32[128,4096]{1,0:T(8,128)S(1)} %get-tuple-element.79.base, f32[128,1024]{1,0:T(8,128)S(1)} %get-tuple-element.80.slope, f32[128,128]{1,0:T(8,128)S(1)} %get-tuple-element.81.share, bf16[144,1536]{1,0:T(8,128)(2,1)S(1)} %collective-permute-done.5.before, ...), custom_call_target="tpu_custom_call" | custom-call | flops 100000000 | bytes 1000000 | tf_op jit(solution)/shard_map/pallas_call | solution.py:663
  (2 shorter events, 0.0 us)
Async XLA Ops:
  0.6 14.7 %copy-start.5 = (f32[256,256]{1,0:T(8,128)S(1)}, f32[256,256]{1,0:T(8,128)}, u32[]{:S(2)}) copy-start(f32[256,256]{1,0:T(8,128)} %constant.31.clone.forward) | copy-start | bytes 786436
  0.6 14.7 %copy-start.1 = (f32[4096]{0:T(1024)S(1)}, f32[4096]{0:T(1024)}, u32[]{:S(2)}) copy-start(f32[4096]{0:T(1024)} %param.20) | copy-start | bytes 49156
  0.7 14.7 %copy-start.4 = (bf16[128,4096]{1,0:T(8,128)(2,1)S(1)}, bf16[128,4096]{1,0:T(8,128)(2,1)}, u32[]{:S(2)}) copy-start(bf16[128,4096]{1,0:T(8,128)(2,1)} %short_outer.1) | copy-start | bytes 3145732
  0.7 14.7 %copy-start.2 = (bf16[128,4096]{1,0:T(8,128)(2,1)S(1)}, bf16[128,4096]{1,0:T(8,128)(2,1)}, u32[]{:S(2)}) copy-start(bf16[128,4096]{1,0:T(8,128)(2,1)} %taps.1) | copy-start | bytes 3145732
  0.7 14.7 %copy-start.3 = (bf16[128,4096]{1,0:T(8,128)(2,1)S(1)}, bf16[128,4096]{1,0:T(8,128)(2,1)}, u32[]{:S(2)}) copy-start(bf16[128,4096]{1,0:T(8,128)(2,1)} %inner.1) | copy-start | bytes 3145732
  2.3 3.7 %collective-permute-start.1 = (f32[1,128]{1,0:T(1,128)S(1)}, f32[1,128]{1,0:T(1,128)S(1)}, u32[]{:S(2)}, u32[]{:S(2)}) collective-permute-start(f32[1,128]{1,0:T(1,128)S(1)} %get-tuple-element.46.squares), channel_id=1, source_target_pairs={{0,1},{1,0},{2,3},{3,2},{4,5},{5,4},{6,7},{7,6},{8,9},{9,8},{10,11... | collective-permute-start | bytes 1544 | tf_op jit(solution)/shard_map/ppermute | solution.py:58
  5.4 22.4 %copy-start = (bf16[128,128]{1,0:T(8,128)(2,1)S(1)}, bf16[128,128]{1,0:T(8,128)(2,1)}, u32[]{:S(2)}) copy-start(bf16[128,128]{1,0:T(8,128)(2,1)} %constant.33.clone.lower) | copy-start | bytes 98308
  5.4 22.4 %copy-start.6 = (f32[128,256]{1,0:T(8,128)S(1)}, f32[128,256]{1,0:T(8,128)}, u32[]{:S(2)}) copy-start(f32[128,256]{1,0:T(8,128)} %constant.32.clone.back) | copy-start | bytes 393220
  6.0 31.6 %collective-permute-start.3 = (bf16[128,4096]{1,0:T(8,128)(2,1)}, bf16[128,4096]{1,0:T(8,128)(2,1)S(1)}, u32[]{:S(2)}, u32[]{:S(2)}) collective-permute-start(bf16[128,4096]{1,0:T(8,128)(2,1)} %query_far), channel_id=1, source_target_pairs={{2,0},{4,2},{6,4},{8,6},{10,8},{12,10},{14,12},{16,14},{18,16},{20... | collective-permute-start | bytes 3145736 | tf_op jit(solution)/shard_map/ppermute | solution.py:53
  11.4 16.4 %collective-permute-start.2 = (bf16[128,2560]{1,0:T(8,128)(2,1)S(1)}, bf16[128,2560]{1,0:T(8,128)(2,1)S(1)}, u32[]{:S(2)}, u32[]{:S(2)}) collective-permute-start(bf16[128,2560]{1,0:T(8,128)(2,1)S(1)} %get-tuple-element.48), channel_id=1, source_target_pairs={{0,2},{2,4},{4,6},{6,8},{8,10},{10,12},{12,14},{14,16},{16,18},{18... | collective-permute-start | bytes 1966088 | tf_op jit(solution)/shard_map/ppermute | solution.py:53
  13.4 18.7 %collective-permute-start = (bf16[128,1536]{1,0:T(8,128)(2,1)S(1)}, bf16[128,1536]{1,0:T(8,128)(2,1)S(1)}, u32[]{:S(2)}, u32[]{:S(2)}) collective-permute-start(bf16[128,1536]{1,0:T(8,128)(2,1)S(1)} %get-tuple-element.44), channel_id=1, source_target_pairs={{0,2},{2,4},{4,6},{6,8},{8,10},{10,12},{12,14},{14,16},{16,18},{18... | collective-permute-start | bytes 1179656 | tf_op jit(solution)/shard_map/ppermute | solution.py:53
  34.2 8.9 %all-to-all-start = ((bf16[8,32,128]{2,1,0:T(8,128)(2,1)}), bf16[8,32,128]{2,1,0:T(8,128)(2,1)S(1)}, u32[]{:S(2)}, u32[]{:S(2)}) async-start(bf16[8,32,128]{2,1,0:T(8,128)(2,1)} %get-tuple-element.55), calls=%async_computation | async-start | bytes 131072 | tf_op jit(solution)/shard_map/all_to_all | solution.py:587
  43.8 19.4 %all-to-all-start.1 = ((bf16[16,32,128]{2,1,0:T(8,128)(2,1)}), bf16[16,32,128]{2,1,0:T(8,128)(2,1)S(1)}, u32[]{:S(2)}, u32[]{:S(2)}) async-start(bf16[16,32,128]{2,1,0:T(8,128)(2,1)} %get-tuple-element.59), calls=%async_computation.1 | async-start | bytes 262144 | tf_op jit(solution)/shard_map/all_to_all | solution.py:599
  56.4 21.1 %collective-permute-start.4 = (bf16[128,2432]{1,0:T(8,128)(2,1)}, bf16[128,2432]{1,0:T(8,128)(2,1)S(1)}, u32[]{:S(2)}, u32[]{:S(2)}) collective-permute-start(bf16[128,2432]{1,0:T(8,128)(2,1)} %get-tuple-element.78), channel_id=1, source_target_pairs={{0,2},{2,4},{4,6},{6,8},{8,10},{10,12},{12,14},{14,16},{16,18},{18... | collective-permute-start | bytes 1867784 | tf_op jit(solution)/shard_map/ppermute | solution.py:53
  64.3 18.4 %collective-permute-start.5 = (bf16[144,1536]{1,0:T(8,128)(2,1)S(1)}, bf16[144,1536]{1,0:T(8,128)(2,1)S(1)}, u32[]{:S(2)}, u32[]{:S(2)}) collective-permute-start(bf16[144,1536]{1,0:T(8,128)(2,1)S(1)} %get-tuple-element.82), channel_id=1, source_target_pairs={{0,2},{2,4},{4,6},{6,8},{8,10},{10,12},{12,14},{14,16},{16,18},{18... | collective-permute-start | bytes 1327112 | tf_op jit(solution)/shard_map/ppermute | solution.py:53
  68.4 14.2 %collective-permute-start.6 = (bf16[128,1536]{1,0:T(8,128)(2,1)S(1)}, bf16[128,1536]{1,0:T(8,128)(2,1)S(1)}, u32[]{:S(2)}, u32[]{:S(2)}) collective-permute-start(bf16[128,1536]{1,0:T(8,128)(2,1)S(1)} %get-tuple-element.83), channel_id=1, source_target_pairs={{0,2},{2,4},{4,6},{6,8},{8,10},{10,12},{12,14},{14,16},{16,18},{18... | collective-permute-start | bytes 1179656 | tf_op jit(solution)/shard_map/ppermute | solution.py:53

commit v7 on v6

--- a/solution.py
+++ b/solution.py
@@ -23,6 +23,7 @@
 TAIL = (2560, 1536)
 EARLY = 1024
 MIDDLE = 2560
+GROUP = 8
 VMEM = 8 * 2**20
 
 
@@ -58,7 +59,7 @@
     return lax.ppermute(block, "mp", [(m, sides - 1 - m) for m in range(sides)])
 
 
-def call(body, outs, scratch=(), scalars=0, operands=0, flops=10**8, outside=(), kept=()):
+def call(body, outs, scratch=(), scalars=0, operands=0, flops=10**8, outside=(), kept=(), aliases={}):
     specs = [pl.BlockSpec(memory_space=pltpu.SMEM)] * scalars
     specs += [pl.BlockSpec(memory_space=pltpu.VMEM)] * operands
     for k in outside:
@@ -75,6 +76,7 @@
             for k, (shape, kind) in enumerate(outs)
         ],
         scratch_shapes=list(scratch),
+        input_output_aliases=aliases,
         compiler_params=pltpu.CompilerParams(vmem_limit_bytes=VMEM),
         cost_estimate=pl.CostEstimate(flops=flops, transcendentals=0, bytes_accessed=10**6),
     )
@@ -249,24 +251,32 @@
     scale,
     weights,
     stats,
-    sent,
-    summed_middle,
-    outer_middle,
+    sent_far,
     summed,
     long_outer,
+    sent,
     *sems,
 ):
     share = summed.shape[1]
     summed_in = fetches(summed_far, summed, sems[0], 0, PIECE)
     outer_in = fetches(outer_far, long_outer, sems[1], 0, PIECE)
+    leaving = []
+
+    def send(low, width):
+        at = pl.ds(low, width)
+        copy = pltpu.make_async_copy(
+            sent.at[:, at], sent_far.at[:, at], sems[2].at[len(leaving)]
+        )
+        copy.start()
+        leaving.append(copy)
+
     left = stats[...]
     for k in range(3):
         term = left.astype(BF16)
         left = left - term.astype(F32)
         low = 2 * share + k * BLOCK
         sent[:, low : low + BLOCK] = term
-    later = fetches(summed_far, summed_middle, sems[2], EARLY, PIECE)
-    later += fetches(outer_far, outer_middle, sems[3], EARLY, PIECE)
+    send(2 * share, 3 * BLOCK)
     time = times(PIECE)
     for k, at in enumerate(pieces_of(share, PIECE)):
         d = decay[:, at]
@@ -284,7 +294,16 @@
             high = share + low
             sent[:, low : low + HEAD_DIM] = both[:, :HEAD_DIM].astype(BF16)
             sent[:, high : high + HEAD_DIM] = both[:, HEAD_DIM:].astype(BF16)
-    for copy in later:
+        send(k * PIECE, PIECE)
+        send(share + k * PIECE, PIECE)
+    for copy in leaving:
+        copy.wait()
+
+
+def fetch_body(summed_far, outer_far, summed, outer, *sems):
+    copies = fetches(summed_far, summed, sems[0], EARLY, PIECE)
+    copies += fetches(outer_far, outer, sems[1], EARLY, PIECE)
+    for copy in copies:
         copy.wait()
 
 
@@ -428,7 +447,10 @@
     return copies
 
 
-def own_body(query_far, key_far, weights, stats, query, key, query_sems, key_sems):
+def own_body(
+    query_far, key_far, weights_far, stats, query, key, weights, query_sems, key_sems, sems
+):
+    leaving = []
     width = 2 * PIECE
     arriving = [
         pair
@@ -448,9 +470,16 @@
                 copy.wait()
         e, top, size = soft(jnp.where(lane <= row, score(query[:, at], key[:, at]), -1e30))
         weights[j] = e.astype(BF16)
+        if (j + 1) % GROUP == 0:
+            at = pl.ds(j + 1 - GROUP, GROUP)
+            copy = pltpu.make_async_copy(weights.at[at], weights_far.at[at], sems.at[j // GROUP])
+            copy.start()
+            leaving.append(copy)
         tops = jnp.where(lane == j, top, tops)
         sizes = jnp.where(lane == j + BLOCK // 2, size, sizes)
     stats[...] = jnp.where(lane < BLOCK // 2, tops, sizes)
+    for copy in leaving:
+        copy.wait()
 
 
 def ahead_body(query, key_far, weights, stats, key, sems):
@@ -470,7 +499,14 @@
     stats[...] = jnp.where(lane < BLOCK // 2, tops, sizes)
 
 
-def here_body(weights, first, middle, last, stats_here, early, base, slope, share):
+def here_body(
+    weights_far, first, middle, last, stats_here, early, base, slope, share, weights, sems
+):
+    arriving = []
+    for k in range(weights.shape[0] // GROUP):
+        at = pl.ds(k * GROUP, GROUP)
+        arriving.append(pltpu.make_async_copy(weights_far.at[at], weights.at[at], sems.at[k]))
+        arriving[-1].start()
     top, size = stats_here[...], pltpu.roll(stats_here[...], BLOCK // 2, 1)
     terms = early[:, 2 * EARLY :].astype(F32)
     stats_before = (terms[:, :BLOCK] + terms[:, BLOCK : 2 * BLOCK]) + terms[:, 2 * BLOCK :]
@@ -487,6 +523,8 @@
         for to in pieces_of(block.shape[1], HEAD_DIM):
             at = slice(start + to.start, start + to.stop)
             j = at.start // HEAD_DIM
+            if j % GROUP == 0:
+                arriving[j // GROUP].wait()
             part = dot(weights[j], block[:, to]) * own[:, j : j + 1]
             if start == 0:
                 column = other[:, j : j + 1]
@@ -497,26 +535,41 @@
         start += block.shape[1]
 
 
-def join_body(base, slope, share, before, last, attended, out, sems):
+def join_first(base, slope, share, before, attended, out, sems):
     leaving = []
-    for k, at in enumerate(pieces_of(base.shape[1], PIECE)):
-        for to in pieces_of(PIECE, HEAD_DIM):
-            to = slice(at.start + to.start, at.start + to.stop)
-            j = to.start // HEAD_DIM
+    for k, at in enumerate(pieces_of(MIDDLE, PIECE)):
+        for j in range(at.start // HEAD_DIM, at.stop // HEAD_DIM):
+            to = slice(j * HEAD_DIM, (j + 1) * HEAD_DIM)
             if to.start < EARLY:
                 terms = before[BLOCK:, to].astype(F32)
-                state = (terms[:1] + terms[1:2]) + terms[2:3]
-                more = slope[:, to] * state
-            elif to.start < MIDDLE:
+                more = slope[:, to] * ((terms[:1] + terms[1:2]) + terms[2:3])
+            else:
                 of = slice(to.start - EARLY, to.stop - EARLY)
                 more = share[:, j : j + 1] * before[:BLOCK, of].astype(F32)
-            else:
-                of = slice(to.start - MIDDLE, to.stop - MIDDLE)
-                more = share[:, j : j + 1] * last[:, of].astype(F32)
             out[:, to] = (base[:, to] + more).astype(BF16)
         at = pl.ds(at.start, PIECE)
         leaving.append(pltpu.make_async_copy(out.at[:, at], attended.at[:, at], sems.at[k]))
         leaving[-1].start()
+    for copy in leaving:
+        copy.wait()
+
+
+def join_last(base, share, last, whole, attended, out, sems):
+    leaving = []
+    for k, to in enumerate(pieces_of(last.shape[1], PIECE)):
+        for j in range(to.start // HEAD_DIM, to.stop // HEAD_DIM):
+            of = slice(j * HEAD_DIM, (j + 1) * HEAD_DIM)
+            at = slice(MIDDLE + of.start, MIDDLE + of.stop)
+            head = MIDDLE // HEAD_DIM + j
+            value = base[:, at] + share[:, head : head + 1] * last[:, of].astype(F32)
+            out[:, of] = value.astype(BF16)
+        copy = pltpu.make_async_copy(
+            out.at[:, pl.ds(to.start, PIECE)],
+            attended.at[:, pl.ds(MIDDLE + to.start, PIECE)],
+            sems.at[k],
+        )
+        copy.start()
+        leaving.append(copy)
     for copy in leaving:
         copy.wait()
 
@@ -571,6 +624,18 @@
     spectrum, gate = call(
         tables_body, [((2 * rows, width), F32), wide_float], operands=5
     )(forward, short_filter, long_inner, short_outer, decay)
+    weights_here, stats_here = call(
+        own_body,
+        [((heads, rows, rows), BF16), square],
+        [pltpu.VMEM((rows, width), BF16)] * 2
+        + [pltpu.VMEM((heads, rows, rows), BF16)]
+        + [pltpu.SemaphoreType.DMA((width // PIECE // 2,))] * 2
+        + [pltpu.SemaphoreType.DMA((heads // GROUP,))],
+        operands=2,
+        outside=(0, 1),
+        kept=(0,),
+    )(in_hbm(query_heads), in_hbm(key_heads))
+    v_before[0], stats_here = lax.optimization_barrier((v_before[0], stats_here))
     summed, state, matrix = call(
         conv_first,
         [((rows, TAIL[0]), BF16), ((TAIL[0] // 128, 128), F32), ((2 * rows, 2 * rows), BF16)],
@@ -606,14 +671,26 @@
     middle_wide, last_wide = ((rows, share), BF16), ((rows, width - MIDDLE), BF16)
     summed, inside = lax.optimization_barrier((summed, inside))
     summed, outer = in_hbm(summed), in_hbm(long_outer)
-    early, summed_middle, outer_middle = call(
+    (early,) = call(
         early_body,
-        [((rows, 2 * EARLY + 3 * rows), BF16), middle_wide, middle_wide],
-        fetching(EARLY) + [pltpu.SemaphoreType.DMA((share // PIECE,))] * 2,
+        [((rows, 2 * EARLY + 3 * rows), BF16)],
+        fetching(EARLY)[:2]
+        + [pltpu.VMEM((rows, 2 * EARLY + 3 * rows), BF16)]
+        + fetching(EARLY)[2:]
+        + [pltpu.SemaphoreType.DMA((1 + 2 * EARLY // PIECE,))],
         operands=7,
         outside=(0, 2),
+        kept=(0,),
     )(summed, lower, outer, decay, scale, weights_next, stats_next)
     early = shifted(early, SEQ, 1)
+    summed_middle, outer_middle = call(
+        fetch_body,
+        [middle_wide, middle_wide],
+        [pltpu.SemaphoreType.DMA((share // PIECE,))] * 2,
+        operands=2,
+        outside=(0, 1),
+    )(summed, outer)
+    others, summed_middle = lax.optimization_barrier((others, summed_middle))
     place, steps = jnp.stack([near, far]), float(near_size)
     middle, ready = call(
         functools.partial(finish_middle, steps),
@@ -648,25 +725,32 @@
     (values,) = call(
         store_body, [wide], [pltpu.SemaphoreType.DMA((3,))], operands=3, kept=(0,)
     )(first, middle, last)
-    query_own, key_own, last = lax.optimization_barrier((query_heads, key_heads, last))
-    weights_here, stats_here = call(
-        own_body,
-        [((heads, rows, rows), BF16), square],
-        [pltpu.VMEM((rows, width), BF16)] * 2
-        + [pltpu.SemaphoreType.DMA((width // PIECE // 2,))] * 2,
-        operands=2,
-        outside=(0, 1),
-    )(in_hbm(query_own), in_hbm(key_own))
     base, slope, share = call(
-        here_body, [wide_float, ((rows, EARLY), F32), square], operands=6
-    )(weights_here, first, middle, last, stats_here, early)
+        here_body,
+        [wide_float, ((rows, EARLY), F32), square],
+        [pltpu.VMEM((heads, rows, rows), BF16), pltpu.SemaphoreType.DMA((heads // GROUP,))],
+        operands=6,
+        outside=(0,),
+    )(in_hbm(weights_here), first, middle, last, stats_here, early)
     (attended,) = call(
-        join_body,
+        join_first,
         [wide],
-        [pltpu.VMEM((rows, width), BF16), pltpu.SemaphoreType.DMA((width // PIECE,))],
-        operands=5,
+        [pltpu.VMEM((rows, MIDDLE), BF16), pltpu.SemaphoreType.DMA((MIDDLE // PIECE,))],
+        operands=4,
         kept=(0,),
-    )(base, slope, share, arrived, arrived_last)
+    )(base, slope, share, arrived)
+    (attended,) = call(
+        join_last,
+        [wide],
+        [
+            pltpu.VMEM((rows, width - MIDDLE), BF16),
+            pltpu.SemaphoreType.DMA(((width - MIDDLE) // PIECE,)),
+        ],
+        operands=4,
+        outside=(3,),
+        kept=(0,),
+        aliases={3: 0},
+    )(base, share, arrived_last, attended)
     return (values, attended)
 
 

time: 84.6 us -> 84.1 us (level)
  waiting for transfers between devices: 24.4 us -> 20.6 us
  Pallas kernels: 27.8 us -> 31.5 us
    pallas_call x3 -> x5, Pallas kernels: 5.03 us -> 7.93 us  [the longest x1 2.61 us: on_device(): call(early_body, [((rows, 2 * EARLY + 3 * rows), BF16)], fetching(EARLY)[...]
    ppermute x6, waiting for transfers between devices: 16.8 us -> 14.2 us  [shifted(): lax.ppermute(block, axis, [(i, i + distance) for i in range(size) if 0 <=...]
    all_to_all x1, waiting for transfers between devices: 4.77 us -> 3.7 us  [on_device(): others = lax.all_to_all(group, FAR, 0, 0, tiled=True)]
  transfers between devices with their start and end apart: 9 -> 9, of which waited for: 6 -> 7; matrix products, arithmetic and copies ran while one was open for 0% -> 0% of each run, Pallas kernels for 29% -> 34%
where the time goes in v7:
time: 84.1 us; the launch traced here: 83.6 us
  Pallas kernels  31.5 us (37%)
  starting transfers between devices  30.5 us (36%)
  waiting for transfers between devices  20.6 us (24%)
  between operations  0.92 us (1%)
    ppermute x6, starting transfers between devices, shifted(): lax.ppermute(block, axis, [(i, i + distance) for i in range(size) if 0 <=...  15.7 us
    ppermute x6, waiting for transfers between devices, shifted(): lax.ppermute(block, axis, [(i, i + distance) for i in range(size) if 0 <=...  14.2 us
    all_to_all x1, starting transfers between devices, on_device(): others = lax.all_to_all(group, FAR, 0, 0, tiled=True)  9.79 us
    pallas_call x1, Pallas kernels, on_device(): call(own_body, [((heads, rows, rows), BF16), square], [pltpu.VMEM((rows,...  3.9 us
    all_to_all x1, waiting for transfers between devices, on_device(): others = lax.all_to_all(group, FAR, 0, 0, tiled=True)  3.7 us
    all_to_all x1, starting transfers between devices, on_device(): pieces = lax.all_to_all(state, NEAR, 0, 0, tiled=True)  3.35 us
    pallas_call x1, Pallas kernels, on_device(): call(ahead_body, [((heads, rows, rows), BF16), square], [pltpu.VMEM((rows...  3.17 us
    pallas_call x1, Pallas kernels, on_device(): call(conv_first, [((rows, TAIL[0]), BF16), ((TAIL[0] // 128, 128), F32),...  2.8 us
  transfers between devices with their start and end apart: 9, of which 7 were waited for; matrix products, arithmetic and copies ran while one was open for 0% of the time, Pallas kernels for 34%

profile of v7, /device:TPU:32, one launch (start us, length us, event | category | flops | bytes accessed | tf_op | source)
XLA Modules:
  0.0 83.6 jit_solution(10455092372104611380)
XLA Ops:
  0.6 0.0 copy-start.7
  0.6 1.6 %shard_map.140 = (f32[1,128]{1,0:T(1,128)S(1)}, bf16[128,4096]{1,0:T(8,128)(2,1)S(1)}) custom-call(bf16[128,4096]{1,0:T(8,128)(2,1)} %stream_far.1), custom_call_target="tpu_custom_call" | custom-call | flops 100000000 | bytes 1000000 | tf_op jit(solution)/shard_map/pallas_call | solution.py:602
  2.2 1.6 %collective-permute-start.1 = (f32[1,128]{1,0:T(1,128)S(1)}, f32[1,128]{1,0:T(1,128)S(1)}, u32[]{:S(2)}, u32[]{:S(2)}) collective-permute-start(f32[1,128]{1,0:T(1,128)S(1)} %get-tuple-element.46.squares), channel_id=1, source_target_pairs={{0,1},{1,0},{2,3},{3,2},{4,5},{5,4},{6,7},{7,6},{8,9},{9,8},{10,11... | collective-permute-start | bytes 1544 | tf_op jit(solution)/shard_map/ppermute | solution.py:59
  3.8 0.0 copy-start.1
  3.8 0.0 copy-start.2
  3.8 0.0 copy-start.3
  3.8 0.0 copy-start.4
  3.8 0.0 copy-start.5
  3.8 1.7 %shard_map.141 = (bf16[128,4096]{1,0:T(8,128)(2,1)S(1)}, bf16[128,2560]{1,0:T(8,128)(2,1)S(1)}, bf16[128,1536]{1,0:T(8,128)(2,1)S(1)}) custom-call(bf16[128,4096]{1,0:T(8,128)(2,1)S(1)} %get-tuple-element.43.stream, bf16[128,4096]{1,0:T(8,128)(2,1)} %inner_far.1, f32[1,4096]{1,0:T(1,128)} %bitcast.18), custom_call_target="tpu_custom_call" | custom-call | flops 100000000 | bytes 1000000 | tf_op jit(solution)/shard_map/pallas_call | solution.py:606
  5.5 0.3 collective-permute-done.1.beside
  5.9 0.0 copy-done.7
  5.9 5.5 %collective-permute-start.3 = (bf16[128,4096]{1,0:T(8,128)(2,1)S(1)}, bf16[128,4096]{1,0:T(8,128)(2,1)S(1)}, u32[]{:S(2)}, u32[]{:S(2)}) collective-permute-start(bf16[128,4096]{1,0:T(8,128)(2,1)S(1)} %copy-done.7), channel_id=1, source_target_pairs={{2,0},{4,2},{6,4},{8,6},{10,8},{12,10},{14,12},{16,14},{18,16},{20... | collective-permute-start | bytes 3145736 | tf_op jit(solution)/shard_map/ppermute | solution.py:54
  11.4 1.9 %collective-permute-start.2 = (bf16[128,2560]{1,0:T(8,128)(2,1)S(1)}, bf16[128,2560]{1,0:T(8,128)(2,1)S(1)}, u32[]{:S(2)}, u32[]{:S(2)}) collective-permute-start(bf16[128,2560]{1,0:T(8,128)(2,1)S(1)} %get-tuple-element.48), channel_id=1, source_target_pairs={{0,2},{2,4},{4,6},{6,8},{8,10},{10,12},{12,14},{14,16},{16,18},{18... | collective-permute-start | bytes 1966088 | tf_op jit(solution)/shard_map/ppermute | solution.py:54
  13.3 1.9 %collective-permute-start = (bf16[128,1536]{1,0:T(8,128)(2,1)S(1)}, bf16[128,1536]{1,0:T(8,128)(2,1)S(1)}, u32[]{:S(2)}, u32[]{:S(2)}) collective-permute-start(bf16[128,1536]{1,0:T(8,128)(2,1)S(1)} %get-tuple-element.44), channel_id=1, source_target_pairs={{0,2},{2,4},{4,6},{6,8},{8,10},{10,12},{12,14},{14,16},{16,18},{18... | collective-permute-start | bytes 1179656 | tf_op jit(solution)/shard_map/ppermute | solution.py:54
  15.2 3.9 %shard_map.142 = (bf16[32,128,128]{2,1,0:T(8,128)(2,1)}, f32[128,128]{1,0:T(8,128)S(1)}) custom-call(bf16[128,4096]{1,0:T(8,128)(2,1)} %query_far.1, bf16[128,4096]{1,0:T(8,128)(2,1)} %key_far.3), custom_call_target="tpu_custom_call" | custom-call | flops 100000000 | bytes 1000000 | tf_op jit(solution)/shard_map/pallas_call | solution.py:627
  19.1 0.0 copy-start
  19.1 0.0 copy-start.6
  19.2 0.0 copy-done.1
  19.2 0.0 copy-done.2
  19.2 0.0 copy-done.3
  19.2 0.0 copy-done.4
  19.2 0.0 copy-done.5
  19.2 1.3 %shard_map.143 = (f32[256,4096]{1,0:T(8,128)S(1)}, f32[128,4096]{1,0:T(8,128)S(1)}) custom-call(f32[256,256]{1,0:T(8,128)S(1)} %copy-done.5, bf16[128,4096]{1,0:T(8,128)(2,1)S(1)} %copy-done.2, bf16[128,4096]{1,0:T(8,128)(2,1)S(1)} %copy-done.3, bf16[128,4096]{1,0:T(8,128)(2,1)S(1)} %copy-done.4, f32[1,4096]{1,0:T(1,128)S(1)} %bitcast.7), custom_call_target="tpu_custom_call" | custom-call | flops 100000000 | bytes 1000000 | tf_op jit(solution)/shard_map/pallas_call | solution.py:624
  20.6 7.2 %collective-permute-done.2.before = bf16[128,2560]{1,0:T(8,128)(2,1)S(1)} collective-permute-done((bf16[128,2560]{1,0:T(8,128)(2,1)S(1)}, bf16[128,2560]{1,0:T(8,128)(2,1)S(1)}, u32[]{:S(2)}, u32[]{:S(2)}) %collective-permute-start.2) | collective-permute-done | bytes 655392 | tf_op jit(solution)/shard_map/ppermute | solution.py:54
  27.8 0.0 copy-done
  27.8 0.0 copy-done.6
  27.8 2.8 %shard_map.144 = (bf16[128,2560]{1,0:T(8,128)(2,1)}, f32[20,128]{1,0:T(8,128)S(1)}, bf16[256,256]{1,0:T(8,128)(2,1)S(1)}) custom-call(bf16[128,2560]{1,0:T(8,128)(2,1)S(1)} %collective-permute-done.2.before, bf16[128,4096]{1,0:T(8,128)(2,1)S(1)} %get-tuple-element.45.here, f32[1,128]{1,0:T(1,128)S(1)} %get-tuple-element.52.squares, ...), custom_call_target="tpu_custom_call" | custom-call | flops 100000000 | bytes 1000000 | tf_op jit(solution)/shard_map/pallas_call | solution.py:639
  30.6 1.4 %collective-permute-done.before = bf16[128,1536]{1,0:T(8,128)(2,1)S(1)} collective-permute-done((bf16[128,1536]{1,0:T(8,128)(2,1)S(1)}, bf16[128,1536]{1,0:T(8,128)(2,1)S(1)}, u32[]{:S(2)}, u32[]{:S(2)}) %collective-permute-start) | collective-permute-done | bytes 393248 | tf_op jit(solution)/shard_map/ppermute | solution.py:54
  32.0 2.1 %shard_map.145 = (bf16[128,1536]{1,0:T(8,128)(2,1)S(1)}, bf16[8,32,128]{2,1,0:T(8,128)(2,1)}) custom-call(bf16[128,1536]{1,0:T(8,128)(2,1)S(1)} %collective-permute-done.before, bf16[128,4096]{1,0:T(8,128)(2,1)S(1)} %get-tuple-element.45.here, bf16[256,256]{1,0:T(8,128)(2,1)S(1)} %get-tuple-element.55.matrix, f32[128,256]{1,0:T(8,128)S(1)} %copy-done.6, ...), custom_call_target="tpu_custom_call" | custom-call | flops 100000000 | bytes 1000000 | tf_op jit(solution)/shard_map/pallas_call | solution.py:646
  34.1 3.3 %all-to-all-start = ((bf16[8,32,128]{2,1,0:T(8,128)(2,1)}), bf16[8,32,128]{2,1,0:T(8,128)(2,1)S(1)}, u32[]{:S(2)}, u32[]{:S(2)}) async-start(bf16[8,32,128]{2,1,0:T(8,128)(2,1)} %get-tuple-element.57), calls=%async_computation | async-start | bytes 131072 | tf_op jit(solution)/shard_map/all_to_all | solution.py:652
  37.5 0.0 collective-permute-done.3.query
  37.5 3.2 %shard_map.146 = (bf16[32,128,128]{2,1,0:T(8,128)(2,1)S(1)}, f32[128,128]{1,0:T(8,128)S(1)}) custom-call(bf16[128,4096]{1,0:T(8,128)(2,1)S(1)} %collective-permute-done.3.query, bf16[128,4096]{1,0:T(8,128)(2,1)} %key_far.3), custom_call_target="tpu_custom_call" | custom-call | flops 100000000 | bytes 1000000 | tf_op jit(solution)/shard_map/pallas_call | solution.py:653
  40.7 2.3 %all-to-all-done.pieces = bf16[8,32,128]{2,1,0:T(8,128)(2,1)S(1)} async-done(((bf16[8,32,128]{2,1,0:T(8,128)(2,1)}), bf16[8,32,128]{2,1,0:T(8,128)(2,1)S(1)}, u32[]{:S(2)}, u32[]{:S(2)}) %all-to-all-start) | async-done | bytes 65568 | tf_op jit(solution)/shard_map/all_to_all | solution.py:652
  43.0 0.7 shard_map.147
  43.7 9.8 %all-to-all-start.1 = ((bf16[16,32,128]{2,1,0:T(8,128)(2,1)}), bf16[16,32,128]{2,1,0:T(8,128)(2,1)S(1)}, u32[]{:S(2)}, u32[]{:S(2)}) async-start(bf16[16,32,128]{2,1,0:T(8,128)(2,1)} %get-tuple-element.61), calls=%async_computation.1 | async-start | bytes 262144 | tf_op jit(solution)/shard_map/all_to_all | solution.py:664
  53.5 2.6 %shard_map.153 = bf16[128,2432]{1,0:T(8,128)(2,1)} custom-call(bf16[128,2560]{1,0:T(8,128)(2,1)} %get-tuple-element.64.summed_far, bf16[128,128]{1,0:T(8,128)(2,1)S(1)} %copy-done, bf16[128,4096]{1,0:T(8,128)(2,1)} %outer_far.7, f32[1,4096]{1,0:T(1,128)S(1)} %bitcast.10, f32[1,4096]{1,0:T(1,128)S(1)} %bitcast.14, ...), custom_call_target="tpu_custom_call" | custom-call | flops 100000000 | bytes 1000000 | tf_op jit(solution)/shard_map/pallas_call | solution.py:674
  56.1 1.9 %collective-permute-start.4 = (bf16[128,2432]{1,0:T(8,128)(2,1)}, bf16[128,2432]{1,0:T(8,128)(2,1)S(1)}, u32[]{:S(2)}, u32[]{:S(2)}) collective-permute-start(bf16[128,2432]{1,0:T(8,128)(2,1)} %shard_map.153), channel_id=1, source_target_pairs={{0,2},{2,4},{4,6},{6,8},{8,10},{10,12},{12,14},{14,16},{16,18},{18... | collective-permute-start | bytes 1867784 | tf_op jit(solution)/shard_map/ppermute | solution.py:54
  58.1 0.1 pad_add_fusion.place
  58.1 1.3 %shard_map.148 = (bf16[128,1536]{1,0:T(8,128)(2,1)S(1)}, bf16[128,1536]{1,0:T(8,128)(2,1)S(1)}) custom-call(bf16[128,2560]{1,0:T(8,128)(2,1)} %get-tuple-element.64.summed_far, bf16[128,4096]{1,0:T(8,128)(2,1)} %outer_far.7), custom_call_target="tpu_custom_call" | custom-call | flops 100000000 | bytes 1000000 | tf_op jit(solution)/shard_map/pallas_call | solution.py:686
  59.4 3.7 %all-to-all-done.1.others = bf16[16,32,128]{2,1,0:T(8,128)(2,1)S(1)} async-done(((bf16[16,32,128]{2,1,0:T(8,128)(2,1)}), bf16[16,32,128]{2,1,0:T(8,128)(2,1)S(1)}, u32[]{:S(2)}, u32[]{:S(2)}) %all-to-all-start.1) | async-done | bytes 131104 | tf_op jit(solution)/shard_map/all_to_all | solution.py:664
  63.1 1.1 %shard_map.151 = (bf16[128,1536]{1,0:T(8,128)(2,1)S(1)}, bf16[144,1536]{1,0:T(8,128)(2,1)S(1)}) custom-call(s32[2]{0:T(128)S(1)} %pad_add_fusion.place, bf16[16,32,128]{2,1,0:T(8,128)(2,1)S(1)} %all-to-all-done.1.others, f32[32,128]{1,0:T(8,128)S(1)} %get-tuple-element.67.inside, f32[32,128]{1,0:T(8,128)S(1)} %get-tuple-element.85.rate, ...), custom_call_target="tpu_custom_call" | custom-call | flops 100000000 | bytes 1000000 | tf_op jit(solution)/shard_map/pallas_call | solution.py:695
  64.2 1.9 %collective-permute-start.6 = (bf16[144,1536]{1,0:T(8,128)(2,1)S(1)}, bf16[144,1536]{1,0:T(8,128)(2,1)S(1)}, u32[]{:S(2)}, u32[]{:S(2)}) collective-permute-start(bf16[144,1536]{1,0:T(8,128)(2,1)S(1)} %get-tuple-element.83), channel_id=1, source_target_pairs={{0,2},{2,4},{4,6},{6,8},{8,10},{10,12},{12,14},{14,16},{16,18},{18... | collective-permute-start | bytes 1327112 | tf_op jit(solution)/shard_map/ppermute | solution.py:54
  66.2 2.2 %shard_map.149 = (bf16[128,1536]{1,0:T(8,128)(2,1)S(1)}, bf16[128,1536]{1,0:T(8,128)(2,1)S(1)}) custom-call(s32[2]{0:T(128)S(1)} %pad_add_fusion.place, bf16[16,32,128]{2,1,0:T(8,128)(2,1)S(1)} %all-to-all-done.1.others, f32[32,128]{1,0:T(8,128)S(1)} %get-tuple-element.67.inside, f32[32,128]{1,0:T(8,128)S(1)} %get-tuple-element.85.rate, ...), custom_call_target="tpu_custom_call" | custom-call | flops 100000000 | bytes 1000000 | tf_op jit(solution)/shard_map/pallas_call | solution.py:704
  68.4 2.6 %collective-permute-start.5 = (bf16[128,1536]{1,0:T(8,128)(2,1)S(1)}, bf16[128,1536]{1,0:T(8,128)(2,1)S(1)}, u32[]{:S(2)}, u32[]{:S(2)}) collective-permute-start(bf16[128,1536]{1,0:T(8,128)(2,1)S(1)} %get-tuple-element.81), channel_id=1, source_target_pairs={{0,2},{2,4},{4,6},{6,8},{8,10},{10,12},{12,14},{14,16},{16,18},{18... | collective-permute-start | bytes 1179656 | tf_op jit(solution)/shard_map/ppermute | solution.py:54
  71.0 1.9 %shard_map.150.first = bf16[128,1024]{1,0:T(8,128)(2,1)S(1)} custom-call(s32[2]{0:T(128)S(1)} %pad_add_fusion.place, bf16[16,32,128]{2,1,0:T(8,128)(2,1)S(1)} %all-to-all-done.1.others, f32[32,128]{1,0:T(8,128)S(1)} %get-tuple-element.67.inside, f32[32,128]{1,0:T(8,128)S(1)} %get-tuple-element.85.rate, bf16[128,2560]{1,0:T(8,128)(2,1)} %get-tuple-element.64.summed_far, ...), custom_call_target="tpu_custom_call" | custom-call | flops 100000000 | bytes 1000000 | tf_op jit(solution)/shard_map/pallas_call | solution.py:717
  72.9 1.0 %shard_map.152 = bf16[128,4096]{1,0:T(8,128)(2,1)} custom-call(bf16[128,1024]{1,0:T(8,128)(2,1)S(1)} %shard_map.150.first, bf16[128,1536]{1,0:T(8,128)(2,1)S(1)} %get-tuple-element.74.middle, bf16[128,1536]{1,0:T(8,128)(2,1)S(1)} %get-tuple-element.75.last), custom_call_target="tpu_custom_call" | custom-call | flops 100000000 | bytes 1000000 | tf_op jit(solution)/shard_map/pallas_call | solution.py:725
  73.9 0.0 collective-permute-done.4.early
  73.9 2.1 %shard_map.154 = (f32[128,4096]{1,0:T(8,128)S(1)}, f32[128,1024]{1,0:T(8,128)S(1)}, f32[128,128]{1,0:T(8,128)S(1)}) custom-call(bf16[32,128,128]{2,1,0:T(8,128)(2,1)} %get-tuple-element.76.weights_far, bf16[128,1024]{1,0:T(8,128)(2,1)S(1)} %shard_map.150.first, bf16[128,1536]{1,0:T(8,128)(2,1)S(1)} %get-tuple-element.74.middle, ...), custom_call_target="tpu_custom_call" | custom-call | flops 100000000 | bytes 1000000 | tf_op jit(solution)/shard_map/pallas_call | solution.py:728
  76.0 2.4 %collective-permute-done.6.before = bf16[144,1536]{1,0:T(8,128)(2,1)S(1)} collective-permute-done((bf16[144,1536]{1,0:T(8,128)(2,1)S(1)}, bf16[144,1536]{1,0:T(8,128)(2,1)S(1)}, u32[]{:S(2)}, u32[]{:S(2)}) %collective-permute-start.6) | collective-permute-done | bytes 442400 | tf_op jit(solution)/shard_map/ppermute | solution.py:54
  78.4 1.0 %shard_map.155.whole = bf16[128,4096]{1,0:T(8,128)(2,1)} custom-call(f32[128,4096]{1,0:T(8,128)S(1)} %get-tuple-element.79.base, f32[128,1024]{1,0:T(8,128)S(1)} %get-tuple-element.82.slope, f32[128,128]{1,0:T(8,128)S(1)} %get-tuple-element.80.share, bf16[144,1536]{1,0:T(8,128)(2,1)S(1)} %collective-permute-done.6.before), custom_call_target="tpu_custom_call" | custom-call | flops 100000000 | bytes 1000000 | tf_op jit(solution)/shard_map/pallas_call | solution.py:735
  79.4 3.2 %collective-permute-done.5.last = bf16[128,1536]{1,0:T(8,128)(2,1)S(1)} collective-permute-done((bf16[128,1536]{1,0:T(8,128)(2,1)S(1)}, bf16[128,1536]{1,0:T(8,128)(2,1)S(1)}, u32[]{:S(2)}, u32[]{:S(2)}) %collective-permute-start.5) | collective-permute-done | bytes 393248 | tf_op jit(solution)/shard_map/ppermute | solution.py:54
  82.6 1.0 %shard_map.156 = bf16[128,4096]{1,0:T(8,128)(2,1)} custom-call(f32[128,4096]{1,0:T(8,128)S(1)} %get-tuple-element.79.base, f32[128,128]{1,0:T(8,128)S(1)} %get-tuple-element.80.share, bf16[128,1536]{1,0:T(8,128)(2,1)S(1)} %collective-permute-done.5.last, bf16[128,4096]{1,0:T(8,128)(2,1)} %shard_map.155.whole), custom_call_target="tpu_custom_call", output_to_operand_aliasing={{}: (3, {})} | custom-call | flops 100000000 | bytes 1000000 | tf_op jit(solution)/shard_map/pallas_call | solution.py:742
  (2 shorter events, 0.0 us)
Async XLA Ops:
  0.6 5.3 %copy-start.7 = (bf16[128,4096]{1,0:T(8,128)(2,1)S(1)}, bf16[128,4096]{1,0:T(8,128)(2,1)}, u32[]{:S(2)}) copy-start(bf16[128,4096]{1,0:T(8,128)(2,1)} %query_far.1) | copy-start | bytes 3145732
  2.2 3.7 %collective-permute-start.1 = (f32[1,128]{1,0:T(1,128)S(1)}, f32[1,128]{1,0:T(1,128)S(1)}, u32[]{:S(2)}, u32[]{:S(2)}) collective-permute-start(f32[1,128]{1,0:T(1,128)S(1)} %get-tuple-element.46.squares), channel_id=1, source_target_pairs={{0,1},{1,0},{2,3},{3,2},{4,5},{5,4},{6,7},{7,6},{8,9},{9,8},{10,11... | collective-permute-start | bytes 1544 | tf_op jit(solution)/shard_map/ppermute | solution.py:59
  3.8 15.4 %copy-start.1 = (f32[4096]{0:T(1024)S(1)}, f32[4096]{0:T(1024)}, u32[]{:S(2)}) copy-start(f32[4096]{0:T(1024)} %param.20) | copy-start | bytes 49156
  3.8 15.4 %copy-start.2 = (bf16[128,4096]{1,0:T(8,128)(2,1)S(1)}, bf16[128,4096]{1,0:T(8,128)(2,1)}, u32[]{:S(2)}) copy-start(bf16[128,4096]{1,0:T(8,128)(2,1)} %taps.1) | copy-start | bytes 3145732
  3.8 15.4 %copy-start.3 = (bf16[128,4096]{1,0:T(8,128)(2,1)S(1)}, bf16[128,4096]{1,0:T(8,128)(2,1)}, u32[]{:S(2)}) copy-start(bf16[128,4096]{1,0:T(8,128)(2,1)} %inner.1) | copy-start | bytes 3145732
  3.8 15.4 %copy-start.4 = (bf16[128,4096]{1,0:T(8,128)(2,1)S(1)}, bf16[128,4096]{1,0:T(8,128)(2,1)}, u32[]{:S(2)}) copy-start(bf16[128,4096]{1,0:T(8,128)(2,1)} %short_outer.1) | copy-start | bytes 3145732
  3.8 15.4 %copy-start.5 = (f32[256,256]{1,0:T(8,128)S(1)}, f32[256,256]{1,0:T(8,128)}, u32[]{:S(2)}) copy-start(f32[256,256]{1,0:T(8,128)} %constant.31.clone.forward) | copy-start | bytes 786436
  5.9 31.6 %collective-permute-start.3 = (bf16[128,4096]{1,0:T(8,128)(2,1)S(1)}, bf16[128,4096]{1,0:T(8,128)(2,1)S(1)}, u32[]{:S(2)}, u32[]{:S(2)}) collective-permute-start(bf16[128,4096]{1,0:T(8,128)(2,1)S(1)} %copy-done.7), channel_id=1, source_target_pairs={{2,0},{4,2},{6,4},{8,6},{10,8},{12,10},{14,12},{16,14},{18,16},{20... | collective-permute-start | bytes 3145736 | tf_op jit(solution)/shard_map/ppermute | solution.py:54
  11.4 16.4 %collective-permute-start.2 = (bf16[128,2560]{1,0:T(8,128)(2,1)S(1)}, bf16[128,2560]{1,0:T(8,128)(2,1)S(1)}, u32[]{:S(2)}, u32[]{:S(2)}) collective-permute-start(bf16[128,2560]{1,0:T(8,128)(2,1)S(1)} %get-tuple-element.48), channel_id=1, source_target_pairs={{0,2},{2,4},{4,6},{6,8},{8,10},{10,12},{12,14},{14,16},{16,18},{18... | collective-permute-start | bytes 1966088 | tf_op jit(solution)/shard_map/ppermute | solution.py:54
  13.3 18.7 %collective-permute-start = (bf16[128,1536]{1,0:T(8,128)(2,1)S(1)}, bf16[128,1536]{1,0:T(8,128)(2,1)S(1)}, u32[]{:S(2)}, u32[]{:S(2)}) collective-permute-start(bf16[128,1536]{1,0:T(8,128)(2,1)S(1)} %get-tuple-element.44), channel_id=1, source_target_pairs={{0,2},{2,4},{4,6},{6,8},{8,10},{10,12},{12,14},{14,16},{16,18},{18... | collective-permute-start | bytes 1179656 | tf_op jit(solution)/shard_map/ppermute | solution.py:54
  19.1 8.7 %copy-start = (bf16[128,128]{1,0:T(8,128)(2,1)S(1)}, bf16[128,128]{1,0:T(8,128)(2,1)}, u32[]{:S(2)}) copy-start(bf16[128,128]{1,0:T(8,128)(2,1)} %constant.33.clone.lower) | copy-start | bytes 98308
  19.1 8.6 %copy-start.6 = (f32[128,256]{1,0:T(8,128)S(1)}, f32[128,256]{1,0:T(8,128)}, u32[]{:S(2)}) copy-start(f32[128,256]{1,0:T(8,128)} %constant.32.clone.back) | copy-start | bytes 393220
  34.1 8.9 %all-to-all-start = ((bf16[8,32,128]{2,1,0:T(8,128)(2,1)}), bf16[8,32,128]{2,1,0:T(8,128)(2,1)S(1)}, u32[]{:S(2)}, u32[]{:S(2)}) async-start(bf16[8,32,128]{2,1,0:T(8,128)(2,1)} %get-tuple-element.57), calls=%async_computation | async-start | bytes 131072 | tf_op jit(solution)/shard_map/all_to_all | solution.py:652
  43.7 19.4 %all-to-all-start.1 = ((bf16[16,32,128]{2,1,0:T(8,128)(2,1)}), bf16[16,32,128]{2,1,0:T(8,128)(2,1)S(1)}, u32[]{:S(2)}, u32[]{:S(2)}) async-start(bf16[16,32,128]{2,1,0:T(8,128)(2,1)} %get-tuple-element.61), calls=%async_computation.1 | async-start | bytes 262144 | tf_op jit(solution)/shard_map/all_to_all | solution.py:664
  56.1 17.8 %collective-permute-start.4 = (bf16[128,2432]{1,0:T(8,128)(2,1)}, bf16[128,2432]{1,0:T(8,128)(2,1)S(1)}, u32[]{:S(2)}, u32[]{:S(2)}) collective-permute-start(bf16[128,2432]{1,0:T(8,128)(2,1)} %shard_map.153), channel_id=1, source_target_pairs={{0,2},{2,4},{4,6},{6,8},{8,10},{10,12},{12,14},{14,16},{16,18},{18... | collective-permute-start | bytes 1867784 | tf_op jit(solution)/shard_map/ppermute | solution.py:54
  64.2 14.1 %collective-permute-start.6 = (bf16[144,1536]{1,0:T(8,128)(2,1)S(1)}, bf16[144,1536]{1,0:T(8,128)(2,1)S(1)}, u32[]{:S(2)}, u32[]{:S(2)}) collective-permute-start(bf16[144,1536]{1,0:T(8,128)(2,1)S(1)} %get-tuple-element.83), channel_id=1, source_target_pairs={{0,2},{2,4},{4,6},{6,8},{8,10},{10,12},{12,14},{14,16},{16,18},{18... | collective-permute-start | bytes 1327112 | tf_op jit(solution)/shard_map/ppermute | solution.py:54
  68.4 14.2 %collective-permute-start.5 = (bf16[128,1536]{1,0:T(8,128)(2,1)S(1)}, bf16[128,1536]{1,0:T(8,128)(2,1)S(1)}, u32[]{:S(2)}, u32[]{:S(2)}) collective-permute-start(bf16[128,1536]{1,0:T(8,128)(2,1)S(1)} %get-tuple-element.81), channel_id=1, source_target_pairs={{0,2},{2,4},{4,6},{6,8},{8,10},{10,12},{12,14},{14,16},{16,18},{18... | collective-permute-start | bytes 1179656 | tf_op jit(solution)/shard_map/ppermute | solution.py:54
